TPU v7x, 256 devices: a whole 4x4x8 slice. The times are simulated.
256 devices in a mesh: ang: 32 (over y, z_hi, x), slab: 8 (over z_lo, core).
Axes of the slice: x: 4, y: 4, z: 8 (z_hi: 2, z_lo: 4; z = z_hi * 4 + z_lo), core: 2. Of those that a mesh axis runs over, the one named last changes fastest.
Arguments:
- updates: float32 [128, 2, 1024, 512], P('ang', None, 'slab'), may hold values from -6 to 6
- interp_tiles: bfloat16 [128, 32, 256, 128], P('ang'), may hold values from -0.25 to 0.25
- band_start: int32 [128, 32], P('ang'), may hold values from 0 to 2
- angle_id: int32 [128], P('ang'), may hold values from 0 to 127, each once
- angle_weight: float32 [128], replicated, may hold values from 0.05 to 0.5
- volume: float32 [4096, 2, 1024], P('ang', None, 'slab'), may hold values from -6 to 6
Outputs:
- volume_next: float32 [4096, 2, 1024], P('ang', None, 'slab')
- projection: float32 [128, 2, 1024, 512], P('ang', None, 'slab')
Inputs may be any that keep to these rules, and one draw needn't show every extreme that they name: Tile j of angle slot a reads detector columns 128 * band_start[a, j] up to 256 further. `angle_id`: each measured angle stands in exactly one slot.
All inputs are finite; a program needn't handle non-finite values.
Results may differ from a plain program's by a relative error of at most 0.0062.
Values may be sent and summed in bfloat16 or wider, within the bound.
No kernel may reach another device: no remote copies, remote signals or barrier semaphores. Data moves between devices by JAX's collectives and lax.ppermute only.
A program may use at most 128 MiB of HBM per device.

v0:
```python
import functools

import jax
import jax.numpy as jnp
from jax import lax
from jax.experimental import pallas as pl
from jax.experimental.pallas import tpu as pltpu
from jax.sharding import PartitionSpec as P


SMOOTHING = 0.25
YS, ZS, XS, SLABS = 4, 2, 4, 8
LINE = 4
FAR = (2, 1, 3)
ORDER = (*FAR, 0)


def position():
    me, core = lax.axis_index("ang"), lax.axis_index("slab") & 1
    y, zh, x = lax.shift_right_logical(me, 3), lax.shift_right_logical(me, 2) & 1, me & 3
    return y, zh, x, 1 - core


def moved(value, first, delta):
    pairs = []
    for y in range(YS):
        for zh in range(ZS):
            for x in range(XS):
                for slab in range(SLABS):
                    along_x = (slab % 2 == 1) == first
                    ty, tx = (y, (x + delta) % XS) if along_x else ((y + delta) % YS, x)
                    source, target = (y * ZS + zh) * XS + x, (ty * ZS + zh) * XS + tx
                    pairs.append((source * SLABS + slab, target * SLABS + slab))
    return lax.ppermute(value, ("ang", "slab"), pairs)


def across(value):
    return lax.ppermute(value, "ang", [(a, a ^ XS) for a in range(YS * ZS * XS)])


def swapped(value):
    return lax.ppermute(value, "slab", [(i, i ^ 1) for i in range(SLABS)])


def place(d):
    return ORDER.index(d) * LINE


def params(mib, **more):
    return pltpu.CompilerParams(vmem_limit_bytes=mib << 20, **more)


VMEM = pl.BlockSpec(memory_space=pltpu.VMEM)
SMEM = pl.BlockSpec(memory_space=pltpu.SMEM)
ANY = pl.BlockSpec(memory_space=pl.ANY)
AHEAD = pl.CostEstimate(flops=1 << 33, bytes_accessed=1 << 20, transcendentals=0)


def call(kernel, in_specs, outs, flops, mib=16):
    return pl.pallas_call(
        kernel,
        in_specs=in_specs,
        out_specs=[VMEM] * len(outs),
        out_shape=[jax.ShapeDtypeStruct(shape, dtype) for shape, dtype in outs],
        compiler_params=params(mib),
        cost_estimate=pl.CostEstimate(flops=flops, bytes_accessed=1 << 20, transcendentals=0),
    )


def plan_kernel(table):
    y, _, x, owner = position()
    for i, (d, k) in enumerate((d, k) for d in ORDER for k in range(LINE)):
        dy = k + owner * (d - k)
        dx = d + owner * (k - d)
        table[i] = ((y + dy) & 3) * 8 + owner * 4 + ((x + dx) & 3)


def plan():
    return pl.pallas_call(
        plan_kernel,
        out_specs=SMEM,
        out_shape=jax.ShapeDtypeStruct((len(ORDER) * LINE,), jnp.int32),
        compiler_params=params(4),
        cost_estimate=AHEAD,
        name="plan",
    )()


def edges_kernel(volume, after, cells, head, tail):
    depth = volume.shape[2]
    for c in range(2):
        turned = volume[:, c, :].T
        cells[c * depth : (c + 1) * depth, :] = turned
        head[c : c + 1, :] = turned[:1, :]
        tail[c : c + 1, :] = turned[depth - 1 :, :]


def edges(volume, after):
    share, _, depth = volume.shape
    outs = [((2 * depth, share), jnp.float32)] + [((2, share), jnp.float32)] * 2
    return call(edges_kernel, [VMEM, ANY], outs, 1 << 20, 4)(volume, after)


def scale_kernel(table, ids, weights, updates, scaled):
    depth = updates.shape[2]
    for a in range(updates.shape[0]):
        weight = weights[ids[a]]
        for c in range(2):
            at = slice(c * depth, (c + 1) * depth)
            scaled[a, at, :] = (weight * updates[a, c]).astype(jnp.bfloat16)


def scale(updates, table, ids, weights):
    angles, _, depth, detector = updates.shape
    outs = [((angles, 2 * depth, detector), jnp.bfloat16)]
    return call(scale_kernel, [SMEM, SMEM, SMEM, VMEM], outs, 1 << 33, 8)(
        table, ids, weights, updates
    )[0]


def product(sources, tiles, starts, j):
    angles, _, _, block = tiles.shape
    rows = []
    for source in sources:
        windows = []
        for a in range(angles):
            start = pl.multiple_of(starts[a, j] * block, block)
            windows.append(source[a, :, pl.ds(start, 2 * block)])
        rows.append(jnp.concatenate(windows, axis=1))
    weights = jnp.concatenate([tiles[a, j] for a in range(angles)], axis=0)
    return jnp.dot(
        jnp.concatenate(rows, axis=0), weights, preferred_element_type=jnp.float32
    )


def own_kernel(ds, table, starts, scaled, tiles, *outs):
    for d, out in zip(ds, outs):
        for k in range(LINE):
            j = table[place(d) + k]
            out[k] = product((scaled,), tiles, starts, j).astype(out.dtype)


def own_rows(scaled, tiles, table, starts, ds):
    angles, _, band, block = tiles.shape
    rows = scaled.shape[1]
    outs = [((LINE, rows, block), jnp.bfloat16)] * len(ds)
    flops = 2 * len(ds) * LINE * angles * rows * band * block
    kernel = functools.partial(own_kernel, ds)
    return call(kernel, [SMEM, SMEM, VMEM, VMEM], outs, flops)(
        table, starts, scaled, tiles
    )


def join_kernel(d, table, starts, other, tiles, own, after, out):
    rows = other.shape[1]
    for k in range(LINE):
        j = table[place(d) + k]
        out[k, :rows, :] = own[k]
        out[k, rows:, :] = product((other,), tiles, starts, j).astype(out.dtype)


def joined(other, tiles, table, starts, d, own, after):
    angles, _, band, block = tiles.shape
    rows = other.shape[1]
    outs = [((LINE, 2 * rows, block), jnp.bfloat16)]
    flops = 2 * LINE * angles * rows * band * block
    kernel = functools.partial(join_kernel, d)
    specs = [SMEM, SMEM, VMEM, VMEM, VMEM, ANY]
    return call(kernel, specs, outs, flops)(table, starts, other, tiles, own, after)[0]


def both_kernel(d, table, starts, scaled, other, tiles, after, out):
    for k in range(LINE):
        j = table[place(d) + k]
        out[k] = product((scaled, other), tiles, starts, j).astype(out.dtype)


def both_rows(scaled, other, tiles, table, starts, d, dtype, after):
    angles, _, band, block = tiles.shape
    rows = 2 * scaled.shape[1]
    flops = 2 * LINE * angles * rows * band * block
    kernel = functools.partial(both_kernel, d)
    specs = [SMEM, SMEM, VMEM, VMEM, VMEM, ANY]
    return call(kernel, specs, [((LINE, rows, block), dtype)], flops)(
        table, starts, scaled, other, tiles, after
    )[0]


def line_kernel(own, s1, s2, s3, after, kept, *sent):
    for k in range(LINE):
        total = own[k]
        for ref in (s1, s2, s3):
            total = total + ref[k].astype(jnp.float32)
        if k == 0:
            kept[...] = total
        else:
            sent[k - 1][...] = total.astype(jnp.bfloat16)


def line_sum(own, arrived, after):
    tile = own.shape[1:]
    outs = [(tile, jnp.float32)] + [(tile, jnp.bfloat16)] * (LINE - 1)
    kept, *sent = call(line_kernel, [VMEM] * 4 + [ANY], outs, 1 << 20)(
        own, *arrived, after
    )
    return kept, sent


def smooth_kernel(cells, before, after, smooth):
    rows, share = cells.shape
    depth = rows // 2
    z = lax.broadcasted_iota(jnp.int32, (depth, share), 0)
    for c in range(2):
        at = slice(c * depth, (c + 1) * depth)
        value = cells[at, :]
        down = jnp.where(z == 0, before[c : c + 1, :], pltpu.roll(value, 1, 0))
        up = jnp.where(z == depth - 1, after[c : c + 1, :], pltpu.roll(value, depth - 1, 0))
        smooth[at, :] = value - SMOOTHING * (2.0 * value - down - up)


def smoothed(cells, before, after):
    outs = [(cells.shape, jnp.float32)]
    return call(smooth_kernel, [VMEM] * 3, outs, 1 << 20, 4)(cells, before, after)[0]


def merge_kernel(smooth, beside, kept, s1, s2, s3, mine, message):
    _, zh, _, owner = position()
    rows = smooth.shape[0]
    for at, part in ((slice(0, rows), smooth), (slice(rows, 2 * rows), beside)):
        total = kept[at, :]
        for ref in (s1, s2, s3):
            total = total + ref[at, :].astype(jnp.float32)
        total = jnp.where(zh == owner, total + part[...], total)
        mine[at, :] = total
        message[at, :] = total.astype(message.dtype)


def merged(smooth, beside, kept, reached):
    outs = [(kept.shape, jnp.float32), (kept.shape, jnp.bfloat16)]
    return call(merge_kernel, [VMEM] * 6, outs, 1 << 20, 4)(
        smooth, beside, kept, *reached
    )


def finish_kernel(mine, crossed, own, beside, lowered):
    rows, _ = own.shape
    depth = rows // 2
    for slab, out in enumerate((own, beside)):
        for c in range(2):
            at = slice(slab * rows + c * depth, slab * rows + (c + 1) * depth)
            value = mine[at, :] + crossed[at, :].astype(jnp.float32)
            if c == 1:
                value = jnp.maximum(value, 0.0)
            out[c * depth : (c + 1) * depth, :] = value
            lowered[at, :] = value.astype(lowered.dtype)


def finished(mine, crossed):
    rows, share = mine.shape
    outs = [((rows // 2, share), jnp.float32)] * 2 + [(mine.shape, jnp.bfloat16)]
    return call(finish_kernel, [VMEM] * 2, outs, 1 << 20, 4)(mine, crossed)


def turn_kernel(own, received, volume):
    _, zh, _, owner = position()
    depth = volume.shape[2]
    for c in range(2):
        at = slice(c * depth, (c + 1) * depth)
        volume[:, c, :] = jnp.where(zh == owner, own[at, :], received[at, :]).T


def turned(own, received, shape):
    return call(turn_kernel, [VMEM] * 2, [(shape, jnp.float32)], 1 << 20, 4)(own, received)[0]


PARTS = ((0,), (2, 1), (3,))


def spread_kernel(table, starts, tiles, after, *outs):
    block = tiles.shape[3]
    zeros = jnp.zeros((block, block), tiles.dtype)

    def angle(a, carry):
        for out, ds in zip(outs, PARTS):
            for g, d in enumerate(ds):
                for k in range(LINE):
                    j = table[place(d) + k]
                    first = starts[a, j]
                    column = slice((g * LINE + k) * block, (g * LINE + k + 1) * block)
                    for empty in (jnp.where(first == 0, 2, 0), jnp.where(first == 2, 1, 3)):
                        at = pl.ds(pl.multiple_of(empty * block, block), block)
                        out[a, at, column] = zeros
                    at = pl.ds(pl.multiple_of(first * block, block), 2 * block)
                    out[a, at, column] = tiles[a, j]
        return carry

    lax.fori_loop(0, tiles.shape[0], angle, 0)


def spread(tiles, table, starts, detector, after):
    angles, _, _, block = tiles.shape
    outs = [((angles, detector, len(ds) * LINE * block), tiles.dtype) for ds in PARTS]
    return call(spread_kernel, [SMEM, SMEM, VMEM, ANY], outs, 1 << 31, 16)(
        table, starts, tiles, after
    )


def projected(pieces, weights):
    row = jnp.concatenate([piece[k] for piece in pieces for k in range(LINE)], axis=1)
    return lax.dot_general(
        row, weights, (((1,), (1,)), ((), ())), preferred_element_type=jnp.float32
    )


def near_kernel(weights, piece, image):
    for a in range(image.shape[0]):
        image[a] = projected((piece,), weights[a])


def near(piece, weights):
    angles, detector, _ = weights.shape
    rows = piece.shape[1]
    outs = [((angles, rows, detector), jnp.float32)]
    flops = 2 * weights.size * rows
    return call(near_kernel, [VMEM] * 2, outs, flops, 16)(weights, piece)[0]


def next_kernel(weights, before, p1, p2, image):
    for a in range(image.shape[0]):
        image[a] = before[a] + projected((p1, p2), weights[a])


def further(pieces, weights, before):
    outs = [(before.shape, jnp.float32)]
    flops = 2 * weights.size * before.shape[1]
    return call(next_kernel, [VMEM] * 4, outs, flops, 16)(weights, before, *pieces)[0]


def last_kernel(base, weights, before, piece, after, own, message):
    rows = own.shape[1]
    for i in range(own.shape[0]):
        value = before[base + i] + projected((piece,), weights[base + i])
        own[i] = value[:rows]
        message[i] = value[rows:].astype(message.dtype)


def last(piece, weights, before, base, count, after):
    _, rows, detector = before.shape
    shape = (count, rows // 2, detector)
    outs = [(shape, jnp.float32), (shape, jnp.bfloat16)]
    flops = weights.size * rows
    kernel = functools.partial(last_kernel, base)
    return call(kernel, [VMEM] * 3 + [ANY], outs, flops, 16)(
        weights, before, piece, after
    )


def leave_kernel(own0, own1, got0, got1, out, image, done):
    half = own0.shape[0]
    copies = []
    for h, (own, got) in enumerate(((own0, got0), (own1, got1))):
        for i in range(half):
            a = h * half + i
            image[a] = own[i] + got[i].astype(jnp.float32)
            copies.append(pltpu.make_async_copy(image.at[a], out.at[a], done.at[a]))
            copies[-1].start()
    for copy in copies:
        copy.wait()


def leave(own, got):
    half, rows, detector = own[0].shape
    shape = (2 * half, rows, detector)
    return pl.pallas_call(
        leave_kernel,
        in_specs=[VMEM] * 4,
        out_specs=ANY,
        out_shape=jax.ShapeDtypeStruct(shape, jnp.float32),
        scratch_shapes=[pltpu.VMEM(shape, jnp.float32), pltpu.SemaphoreType.DMA((2 * half,))],
        compiler_params=params(16),
        cost_estimate=pl.CostEstimate(flops=1 << 20, bytes_accessed=1 << 20, transcendentals=0),
        name="leave",
    )(*own, *got)


def steps(updates, tiles, starts, ids, weights, volume):
    angles, _, depth, detector = updates.shape
    count = lax.axis_size("slab")
    table = plan()
    scaled = scale(updates, table, ids, weights)
    other = swapped(scaled)
    own2, own1 = own_rows(scaled, tiles, table, starts, (2, 1))
    sent = {}
    sent[2] = joined(other, tiles, table, starts, 2, own2, own1)
    sent[1] = joined(other, tiles, table, starts, 1, own1, sent[2])
    sent[3] = both_rows(scaled, other, tiles, table, starts, 3, jnp.bfloat16, sent[1])
    own = both_rows(scaled, other, tiles, table, starts, 0, jnp.float32, sent[3])
    arrived = []
    for d in FAR:
        arrived.append(moved(sent[d], True, d))

    cells, head, tail = edges(volume, own)
    before = lax.ppermute(tail, "slab", [(i, i + 1) for i in range(count - 1)])
    after = lax.ppermute(head, "slab", [(i + 1, i) for i in range(count - 1)])
    kept, sent = line_sum(own, arrived, cells)
    reached = [moved(sent[d - 1], False, d) for d in FAR]
    smooth = smoothed(cells, before, after)
    mine, message = merged(smooth, swapped(smooth), kept, reached)
    crossed = across(message)
    bands = spread(tiles, table, starts, detector, message)
    own, beside, lowered = finished(mine, crossed)

    came = {}
    for d in FAR:
        came[d] = moved(lowered, False, LINE - d)
    beside, came[1], came[2], came[3] = lax.optimization_barrier(
        (beside, came[1], came[2], came[3])
    )
    line = jnp.stack([lowered] + [came[d] for d in range(1, LINE)])
    rest = {}
    for d in FAR:
        rest[d] = moved(line, True, LINE - d)
    received = swapped(beside)
    volume_next = turned(own, received, volume.shape)
    image = near(line, bands[0])
    image = further([rest[2], rest[1]], bands[1], image)
    half = angles // 2
    own0, message0 = last(rest[3], bands[2], image, 0, half, image)
    got0 = swapped(message0)
    own1, message1 = last(rest[3], bands[2], image, half, half, message0)
    got1 = swapped(message1)
    projection = leave([own0, own1], [got0, got1])
    return volume_next, projection.reshape(angles, 2, depth, detector)


def solution(mesh):
    placed = (
        P("ang", None, "slab", None),
        P("ang", None, None, None),
        P("ang", None),
        P("ang"),
        P(),
        P("ang", None, "slab"),
    )
    return jax.shard_map(
        steps,
        mesh=mesh,
        in_specs=placed,
        out_specs=(P("ang", None, "slab"), P("ang", None, "slab", None)),
        check_vma=False,
    )
```

profile of v0, /device:TPU:161, one launch (start us, length us, event | category | flops | bytes accessed | tf_op | source)
XLA Modules:
  0.0 86.3 jit_solution(14961656192372615768)
XLA Ops:
  0.7 0.6 plan.1.table
  1.3 0.9 %copy-done.2 = f32[4,2,128,512]{3,2,1,0:T(8,128)S(1)} copy-done((f32[4,2,128,512]{3,2,1,0:T(8,128)S(1)}, f32[4,2,128,512]{3,2,1,0:T(8,128)}, u32[]{:S(2)}) %copy-start.2) | copy-done | bytes 2097176
  2.3 0.7 shard_map.77.scaled
  2.9 0.8 collective-permute-start
  3.7 1.2 %slice-done.1 = s8[4194304]{0:T(1024)(128)(4,1)S(1)} async-done(((s8[8388608]{0:T(1024)(128)(4,1)}), s8[4194304]{0:T(1024)(128)(4,1)S(1)}, s32[]{:S(2)}) %slice-start.1) | async-done | bytes 4194328
  4.9 1.8 %shard_map.78 = (bf16[4,256,128]{2,1,0:T(8,128)(2,1)S(1)}, bf16[4,256,128]{2,1,0:T(8,128)(2,1)S(1)}) custom-call(s32[16]{0:T(128)S(1)} %plan.1.table, s32[4,32]{1,0:T(4,128)S(1)} %copy-done.1, bf16[4,256,512]{2,1,0:T(8,128)(2,1)S(1)} %shard_map.77.scaled, bf16[4,32,256,128]{3,2,1,0:T(8,128)(2,1)S(1)} %bitcast.6), custom_call_target="tpu_custom_call" | custom-call | flops 536870912 | bytes 1048576 | tf_op jit(solution)/shard_map/pallas_call | solution.py:149
  6.8 1.3 %shard_map.79.after = bf16[4,512,128]{2,1,0:T(8,128)(2,1)S(1)} custom-call(s32[16]{0:T(128)S(1)} %plan.1.table, s32[4,32]{1,0:T(4,128)S(1)} %copy-done.1, bf16[4,256,512]{2,1,0:T(8,128)(2,1)S(1)} %collective-permute-done.other, bf16[4,32,256,128]{3,2,1,0:T(8,128)(2,1)S(1)} %bitcast.6, bf16[4,256,128]{2,1,0:T(8,128)(2,1)S(1)} %get-tuple-element.28.own, ...), custom_call_target="tpu_custom_call" | custom-call | flops 268435456 | bytes 1048576 | tf_op jit(solution)/shard_map/pallas_call | solution.py:169
  8.1 1.3 %shard_map.80.after = bf16[4,512,128]{2,1,0:T(8,128)(2,1)S(1)} custom-call(s32[16]{0:T(128)S(1)} %plan.1.table, s32[4,32]{1,0:T(4,128)S(1)} %copy-done.1, bf16[4,256,512]{2,1,0:T(8,128)(2,1)S(1)} %collective-permute-done.other, bf16[4,32,256,128]{3,2,1,0:T(8,128)(2,1)S(1)} %bitcast.6, bf16[4,256,128]{2,1,0:T(8,128)(2,1)S(1)} %get-tuple-element.27.after.own, ...), custom_call_target="tpu_custom_call" | custom-call | flops 268435456 | bytes 1048576 | tf_op jit(solution)/shard_map/pallas_call | solution.py:169
  9.4 1.8 %shard_map.81.after = bf16[4,512,128]{2,1,0:T(8,128)(2,1)S(1)} custom-call(s32[16]{0:T(128)S(1)} %plan.1.table, s32[4,32]{1,0:T(4,128)S(1)} %copy-done.1, bf16[4,256,512]{2,1,0:T(8,128)(2,1)S(1)} %shard_map.77.scaled, bf16[4,256,512]{2,1,0:T(8,128)(2,1)S(1)} %collective-permute-done.other, bf16[4,32,256,128]{3,2,1,0:T(8,128)(2,1)S(1)} %bitcast.6, ...), custom_call_target="tpu_custom_call" | custom-call | flops 536870912 | bytes 1048576 | tf_op jit(solution)/shard_map/pallas_call | solution.py:184
  11.2 2.6 %collective-permute-start.6 = (bf16[4,512,128]{2,1,0:T(8,128)(2,1)S(1)}, bf16[4,512,128]{2,1,0:T(8,128)(2,1)S(1)}, u32[]{:S(2)}, u32[]{:S(2)}) collective-permute-start(bf16[4,512,128]{2,1,0:T(8,128)(2,1)S(1)} %shard_map.81.after), channel_id=1, source_target_pairs={{0,192},{1,25},{2,194},{3,27},{4,196},{5,29},{6,198},{7,31},{8,200... | collective-permute-start | bytes 1572872 | tf_op jit(solution)/shard_map/ppermute | solution.py:34
  13.8 1.7 %collective-permute-start.4 = (bf16[4,512,128]{2,1,0:T(8,128)(2,1)S(1)}, bf16[4,512,128]{2,1,0:T(8,128)(2,1)S(1)}, u32[]{:S(2)}, u32[]{:S(2)}) collective-permute-start(bf16[4,512,128]{2,1,0:T(8,128)(2,1)S(1)} %shard_map.79.after), channel_id=1, source_target_pairs={{0,128},{1,17},{2,130},{3,19},{4,132},{5,21},{6,134},{7,23},{8,136... | collective-permute-start | bytes 1572872 | tf_op jit(solution)/shard_map/ppermute | solution.py:34
  15.5 1.8 %shard_map.82.after.own = f32[4,512,128]{2,1,0:T(8,128)S(1)} custom-call(s32[16]{0:T(128)S(1)} %plan.1.table, s32[4,32]{1,0:T(4,128)S(1)} %copy-done.1, bf16[4,256,512]{2,1,0:T(8,128)(2,1)S(1)} %shard_map.77.scaled, bf16[4,256,512]{2,1,0:T(8,128)(2,1)S(1)} %collective-permute-done.other, bf16[4,32,256,128]{3,2,1,0:T(8,128)(2,1)S(1)} %bitcast.6, ...), custom_call_target="tpu_custom_call" | custom-call | flops 536870912 | bytes 1048576 | tf_op jit(solution)/shard_map/pallas_call | solution.py:184
  17.3 0.1 shard_map.83
  17.5 4.2 %collective-permute-start.1 = (f32[2,128]{1,0:T(2,128)S(1)}, f32[2,128]{1,0:T(2,128)S(1)}, u32[]{:S(2)}, u32[]{:S(2)}) collective-permute-start(f32[2,128]{1,0:T(2,128)S(1)} %get-tuple-element.30), channel_id=1, source_target_pairs={{0,1},{1,2},{2,3},{3,4},{4,5},{5,6},{6,7},{8,9},{9,10},{10,11},{11... | collective-permute-start | bytes 3080 | tf_op jit(solution)/shard_map/ppermute | solution.py:403
  21.7 1.9 %collective-permute-start.2 = (f32[2,128]{1,0:T(2,128)S(1)}, f32[2,128]{1,0:T(2,128)S(1)}, u32[]{:S(2)}, u32[]{:S(2)}) collective-permute-start(f32[2,128]{1,0:T(2,128)S(1)} %get-tuple-element.31), channel_id=1, source_target_pairs={{1,0},{2,1},{3,2},{4,3},{5,4},{6,5},{7,6},{9,8},{10,9},{11,10},{12... | collective-permute-start | bytes 3080 | tf_op jit(solution)/shard_map/ppermute | solution.py:404
  23.6 3.2 %collective-permute-done.2.after = f32[2,128]{1,0:T(2,128)S(1)} collective-permute-done((f32[2,128]{1,0:T(2,128)S(1)}, f32[2,128]{1,0:T(2,128)S(1)}, u32[]{:S(2)}, u32[]{:S(2)}) %collective-permute-start.2) | collective-permute-done | bytes 1056 | tf_op jit(solution)/shard_map/ppermute | solution.py:404
  26.9 0.1 collective-permute-start.3
  27.1 1.9 %collective-permute-done.5.s2 = bf16[4,512,128]{2,1,0:T(8,128)(2,1)S(1)} collective-permute-done((bf16[4,512,128]{2,1,0:T(8,128)(2,1)S(1)}, bf16[4,512,128]{2,1,0:T(8,128)(2,1)S(1)}, u32[]{:S(2)}, u32[]{:S(2)}) %collective-permute-start.5) | collective-permute-done | bytes 524320 | tf_op jit(solution)/shard_map/ppermute | solution.py:34
  28.9 0.2 shard_map.85
  29.2 2.7 %collective-permute-start.7 = (bf16[512,128]{1,0:T(8,128)(2,1)S(1)}, bf16[512,128]{1,0:T(8,128)(2,1)S(1)}, u32[]{:S(2)}, u32[]{:S(2)}) collective-permute-start(bf16[512,128]{1,0:T(8,128)(2,1)S(1)} %get-tuple-element.33), channel_id=1, source_target_pairs={{0,16},{1,129},{2,18},{3,131},{4,20},{5,133},{6,22},{7,135},{8,24}... | collective-permute-start | bytes 393224 | tf_op jit(solution)/shard_map/ppermute | solution.py:34
  31.9 0.4 collective-permute-start.8
  32.3 2.3 %collective-permute-start.9 = (bf16[512,128]{1,0:T(8,128)(2,1)S(1)}, bf16[512,128]{1,0:T(8,128)(2,1)S(1)}, u32[]{:S(2)}, u32[]{:S(2)}) collective-permute-start(bf16[512,128]{1,0:T(8,128)(2,1)S(1)} %get-tuple-element.35), channel_id=1, source_target_pairs={{0,24},{1,193},{2,26},{3,195},{4,28},{5,197},{6,30},{7,199},{8,0},... | collective-permute-start | bytes 393224 | tf_op jit(solution)/shard_map/ppermute | solution.py:34
  34.6 2.6 %collective-permute-done.8.s2 = bf16[512,128]{1,0:T(8,128)(2,1)S(1)} collective-permute-done((bf16[512,128]{1,0:T(8,128)(2,1)S(1)}, bf16[512,128]{1,0:T(8,128)(2,1)S(1)}, u32[]{:S(2)}, u32[]{:S(2)}) %collective-permute-start.8) | collective-permute-done | bytes 131104 | tf_op jit(solution)/shard_map/ppermute | solution.py:34
  37.2 0.1 shard_map.86
  37.3 0.1 collective-permute-start.10
  37.4 9.1 %collective-permute-done.10.crossed = bf16[512,128]{1,0:T(8,128)(2,1)S(1)} collective-permute-done((bf16[512,128]{1,0:T(8,128)(2,1)S(1)}, bf16[512,128]{1,0:T(8,128)(2,1)S(1)}, u32[]{:S(2)}, u32[]{:S(2)}) %collective-permute-start.10) | collective-permute-done | bytes 131104 | tf_op jit(solution)/shard_map/ppermute | solution.py:38
  46.5 0.1 collective-permute-start.13
  46.6 3.4 %collective-permute-start.12 = (bf16[512,128]{1,0:T(8,128)(2,1)S(1)}, bf16[512,128]{1,0:T(8,128)(2,1)S(1)}, u32[]{:S(2)}, u32[]{:S(2)}) collective-permute-start(bf16[512,128]{1,0:T(8,128)(2,1)S(1)} %get-tuple-element.40), channel_id=1, source_target_pairs={{0,16},{1,129},{2,18},{3,131},{4,20},{5,133},{6,22},{7,135},{8,24}... | collective-permute-start | bytes 393224 | tf_op jit(solution)/shard_map/ppermute | solution.py:34
  50.0 0.4 collective-permute-start.11
  50.3 1.3 %collective-permute-done.13 = bf16[512,128]{1,0:T(8,128)(2,1)S(1)} collective-permute-done((bf16[512,128]{1,0:T(8,128)(2,1)S(1)}, bf16[512,128]{1,0:T(8,128)(2,1)S(1)}, u32[]{:S(2)}, u32[]{:S(2)}) %collective-permute-start.13) | collective-permute-done | bytes 131104 | tf_op jit(solution)/shard_map/ppermute | solution.py:34
  51.6 2.1 %collective-permute-done.12 = bf16[512,128]{1,0:T(8,128)(2,1)S(1)} collective-permute-done((bf16[512,128]{1,0:T(8,128)(2,1)S(1)}, bf16[512,128]{1,0:T(8,128)(2,1)S(1)}, u32[]{:S(2)}, u32[]{:S(2)}) %collective-permute-start.12) | collective-permute-done | bytes 131104 | tf_op jit(solution)/shard_map/ppermute | solution.py:34
  53.9 0.4 collective-permute-start.16
  54.3 0.8 collective-permute-start.15
  55.1 0.3 collective-permute-start.17
  55.4 2.6 %shard_map.89 = (bf16[4,512,512]{2,1,0:T(8,128)(2,1)S(1)}, bf16[4,512,1024]{2,1,0:T(8,128)(2,1)S(1)}, bf16[4,512,512]{2,1,0:T(8,128)(2,1)S(1)}) custom-call(s32[16]{0:T(128)S(1)} %plan.1.table, s32[4,32]{1,0:T(4,128)S(1)} %copy-done.1, bf16[4,32,256,128]{3,2,1,0:T(8,128)(2,1)S(1)} %bitcast.6, bf16[512,128]{1,0:T(8,128)(2,1)S(1)} %get-tuple-element.37.after), custom_call_target="tpu_custom_call" | custom-call | flops 2147483648 | bytes 1048576 | tf_op jit(solution)/shard_map/pallas_call | solution.py:303
  58.1 1.3 %shard_map.90.before = f32[4,512,512]{2,1,0:T(8,128)S(1)} custom-call(bf16[4,512,512]{2,1,0:T(8,128)(2,1)S(1)} %get-tuple-element.44.weights, bf16[4,512,128]{2,1,0:T(8,128)(2,1)S(1)} %pad_maximum_fusion.piece), custom_call_target="tpu_custom_call" | custom-call | flops 1073741824 | bytes 1048576 | tf_op jit(solution)/shard_map/pallas_call | solution.py:325
  59.4 5.4 %collective-permute-done.16.p2 = bf16[4,512,128]{2,1,0:T(8,128)(2,1)S(1)} collective-permute-done((bf16[4,512,128]{2,1,0:T(8,128)(2,1)S(1)}, bf16[4,512,128]{2,1,0:T(8,128)(2,1)S(1)}, u32[]{:S(2)}, u32[]{:S(2)}) %collective-permute-start.16) | collective-permute-done | bytes 524320 | tf_op jit(solution)/shard_map/ppermute | solution.py:34
  64.7 0.4 collective-permute-done.15.p1
  65.2 2.4 %shard_map.91.before.after = f32[4,512,512]{2,1,0:T(8,128)S(1)} custom-call(bf16[4,512,1024]{2,1,0:T(8,128)(2,1)S(1)} %get-tuple-element.43.weights, f32[4,512,512]{2,1,0:T(8,128)S(1)} %shard_map.90.before, bf16[4,512,128]{2,1,0:T(8,128)(2,1)S(1)} %collective-permute-done.15.p1, bf16[4,512,128]{2,1,0:T(8,128)(2,1)S(1)} %collective-permute-done.16.p2), custom_call_target="tpu_custom_call" | custom-call | flops 2147483648 | bytes 1048576 | tf_op jit(solution)/shard_map/pallas_call | solution.py:336
  67.6 3.4 %collective-permute-done.17.piece = bf16[4,512,128]{2,1,0:T(8,128)(2,1)S(1)} collective-permute-done((bf16[4,512,128]{2,1,0:T(8,128)(2,1)S(1)}, bf16[4,512,128]{2,1,0:T(8,128)(2,1)S(1)}, u32[]{:S(2)}, u32[]{:S(2)}) %collective-permute-start.17) | collective-permute-done | bytes 524320 | tf_op jit(solution)/shard_map/ppermute | solution.py:34
  71.0 0.7 shard_map.92
  71.7 0.7 shard_map.93
  72.5 9.0 %collective-permute-start.19 = (bf16[2,256,512]{2,1,0:T(8,128)(2,1)S(1)}, bf16[2,256,512]{2,1,0:T(8,128)(2,1)S(1)}, u32[]{:S(2)}, u32[]{:S(2)}) collective-permute-start(bf16[2,256,512]{2,1,0:T(8,128)(2,1)S(1)} %get-tuple-element.51), channel_id=1, source_target_pairs={{0,1},{1,0},{2,3},{3,2},{4,5},{5,4},{6,7},{7,6},{8,9},{9,8},{10,11... | collective-permute-start | bytes 1572872 | tf_op jit(solution)/shard_map/ppermute | solution.py:42
  81.4 0.1 collective-permute-start.18
  81.5 0.4 collective-permute-start.14
  82.0 2.0 %collective-permute-done.14.received = f32[256,128]{1,0:T(8,128)S(1)} collective-permute-done((f32[256,128]{1,0:T(8,128)S(1)}, f32[256,128]{1,0:T(8,128)S(1)}, u32[]{:S(2)}, u32[]{:S(2)}) %collective-permute-start.14) | collective-permute-done | bytes 131104 | tf_op jit(solution)/shard_map/ppermute | solution.py:42
  83.9 0.8 shard_map.88
  84.7 1.4 %leave.1 = f32[4,256,512]{2,1,0:T(8,128)} custom-call(f32[2,256,512]{2,1,0:T(8,128)S(1)} %get-tuple-element.48.own0, f32[2,256,512]{2,1,0:T(8,128)S(1)} %get-tuple-element.50.own1, bf16[2,256,512]{2,1,0:T(8,128)(2,1)S(1)} %collective-permute-done.18.got0, bf16[2,256,512]{2,1,0:T(8,128)(2,1)S(1)} %collective-permute-done.19.got1), custom_call_target="tpu_custom_call" | custom-call | flops 1048576 | bytes 1048576 | tf_op jit(solution)/shard_map/leave/pallas_call | solution.py:374
  (27 shorter events, 0.3 us)
Async XLA Ops:
  0.6 0.7 copy-start.4
  0.6 0.7 copy-start.3
  0.6 1.6 %copy-start.2 = (f32[4,2,128,512]{3,2,1,0:T(8,128)S(1)}, f32[4,2,128,512]{3,2,1,0:T(8,128)}, u32[]{:S(2)}) copy-start(f32[4,2,128,512]{3,2,1,0:T(8,128)} %updates.1) | copy-start | bytes 6291460
  0.7 3.0 %slice-start = ((s8[8388608]{0:T(1024)(128)(4,1)}), s8[4194304]{0:T(1024)(128)(4,1)S(1)}, s32[]{:S(2)}) async-start(s8[8388608]{0:T(1024)(128)(4,1)} %bitcast.5), calls=%async_computation | async-start | bytes 8388608
  2.3 2.7 %slice-start.1 = ((s8[8388608]{0:T(1024)(128)(4,1)}), s8[4194304]{0:T(1024)(128)(4,1)S(1)}, s32[]{:S(2)}) async-start(s8[8388608]{0:T(1024)(128)(4,1)} %bitcast.5), calls=%async_computation.1 | async-start | bytes 8388608
  2.3 2.7 %copy-start.1 = (s32[4,32]{1,0:T(4,128)S(1)}, s32[4,32]{1,0:T(4,128)}, u32[]{:S(2)}) copy-start(s32[4,32]{1,0:T(4,128)} %starts.11) | copy-start | bytes 1540
  2.9 3.8 %collective-permute-start = (bf16[4,256,512]{2,1,0:T(8,128)(2,1)S(1)}, bf16[4,256,512]{2,1,0:T(8,128)(2,1)S(1)}, u32[]{:S(2)}, u32[]{:S(2)}) collective-permute-start(bf16[4,256,512]{2,1,0:T(8,128)(2,1)S(1)} %shard_map.77.scaled), channel_id=1, source_target_pairs={{0,1},{1,0},{2,3},{3,2},{4,5},{5,4},{6,7},{7,6},{8,9},{9,8},{10,11... | collective-permute-start | bytes 3145736 | tf_op jit(solution)/shard_map/ppermute | solution.py:42
  11.2 6.1 %copy-start = (f32[128,2,128]{2,1,0:T(2,128)S(1)}, f32[128,2,128]{2,1,0:T(2,128)}, u32[]{:S(2)}) copy-start(f32[128,2,128]{2,1,0:T(2,128)} %volume.1) | copy-start | bytes 393220
  11.2 15.8 %collective-permute-start.6 = (bf16[4,512,128]{2,1,0:T(8,128)(2,1)S(1)}, bf16[4,512,128]{2,1,0:T(8,128)(2,1)S(1)}, u32[]{:S(2)}, u32[]{:S(2)}) collective-permute-start(bf16[4,512,128]{2,1,0:T(8,128)(2,1)S(1)} %shard_map.81.after), channel_id=1, source_target_pairs={{0,192},{1,25},{2,194},{3,27},{4,196},{5,29},{6,198},{7,31},{8,200... | collective-permute-start | bytes 1572872 | tf_op jit(solution)/shard_map/ppermute | solution.py:34
  13.8 15.2 %collective-permute-start.5 = (bf16[4,512,128]{2,1,0:T(8,128)(2,1)S(1)}, bf16[4,512,128]{2,1,0:T(8,128)(2,1)S(1)}, u32[]{:S(2)}, u32[]{:S(2)}) collective-permute-start(bf16[4,512,128]{2,1,0:T(8,128)(2,1)S(1)} %shard_map.80.after), channel_id=1, source_target_pairs={{0,64},{1,9},{2,66},{3,11},{4,68},{5,13},{6,70},{7,15},{8,72},{9,1... | collective-permute-start | bytes 1572872 | tf_op jit(solution)/shard_map/ppermute | solution.py:34
  13.8 15.2 %collective-permute-start.4 = (bf16[4,512,128]{2,1,0:T(8,128)(2,1)S(1)}, bf16[4,512,128]{2,1,0:T(8,128)(2,1)S(1)}, u32[]{:S(2)}, u32[]{:S(2)}) collective-permute-start(bf16[4,512,128]{2,1,0:T(8,128)(2,1)S(1)} %shard_map.79.after), channel_id=1, source_target_pairs={{0,128},{1,17},{2,130},{3,19},{4,132},{5,21},{6,134},{7,23},{8,136... | collective-permute-start | bytes 1572872 | tf_op jit(solution)/shard_map/ppermute | solution.py:34
  17.5 6.2 %collective-permute-start.1 = (f32[2,128]{1,0:T(2,128)S(1)}, f32[2,128]{1,0:T(2,128)S(1)}, u32[]{:S(2)}, u32[]{:S(2)}) collective-permute-start(f32[2,128]{1,0:T(2,128)S(1)} %get-tuple-element.30), channel_id=1, source_target_pairs={{0,1},{1,2},{2,3},{3,4},{4,5},{5,6},{6,7},{8,9},{9,10},{10,11},{11... | collective-permute-start | bytes 3080 | tf_op jit(solution)/shard_map/ppermute | solution.py:403
  21.7 5.2 %collective-permute-start.2 = (f32[2,128]{1,0:T(2,128)S(1)}, f32[2,128]{1,0:T(2,128)S(1)}, u32[]{:S(2)}, u32[]{:S(2)}) collective-permute-start(f32[2,128]{1,0:T(2,128)S(1)} %get-tuple-element.31), channel_id=1, source_target_pairs={{1,0},{2,1},{3,2},{4,3},{5,4},{6,5},{7,6},{9,8},{10,9},{11,10},{12... | collective-permute-start | bytes 3080 | tf_op jit(solution)/shard_map/ppermute | solution.py:404
  26.9 7.6 %collective-permute-start.3 = (f32[256,128]{1,0:T(8,128)S(1)}, f32[256,128]{1,0:T(8,128)S(1)}, u32[]{:S(2)}, u32[]{:S(2)}) collective-permute-start(f32[256,128]{1,0:T(8,128)S(1)} %shard_map.84.smooth), channel_id=1, source_target_pairs={{0,1},{1,0},{2,3},{3,2},{4,5},{5,4},{6,7},{7,6},{8,9},{9,8},{10,11... | collective-permute-start | bytes 393224 | tf_op jit(solution)/shard_map/ppermute | solution.py:42
  29.2 5.4 %collective-permute-start.7 = (bf16[512,128]{1,0:T(8,128)(2,1)S(1)}, bf16[512,128]{1,0:T(8,128)(2,1)S(1)}, u32[]{:S(2)}, u32[]{:S(2)}) collective-permute-start(bf16[512,128]{1,0:T(8,128)(2,1)S(1)} %get-tuple-element.33), channel_id=1, source_target_pairs={{0,16},{1,129},{2,18},{3,131},{4,20},{5,133},{6,22},{7,135},{8,24}... | collective-permute-start | bytes 393224 | tf_op jit(solution)/shard_map/ppermute | solution.py:34
  31.9 5.3 %collective-permute-start.8 = (bf16[512,128]{1,0:T(8,128)(2,1)S(1)}, bf16[512,128]{1,0:T(8,128)(2,1)S(1)}, u32[]{:S(2)}, u32[]{:S(2)}) collective-permute-start(bf16[512,128]{1,0:T(8,128)(2,1)S(1)} %get-tuple-element.34), channel_id=1, source_target_pairs={{0,8},{1,65},{2,10},{3,67},{4,12},{5,69},{6,14},{7,71},{8,16},{9,7... | collective-permute-start | bytes 393224 | tf_op jit(solution)/shard_map/ppermute | solution.py:34
  32.3 4.9 %collective-permute-start.9 = (bf16[512,128]{1,0:T(8,128)(2,1)S(1)}, bf16[512,128]{1,0:T(8,128)(2,1)S(1)}, u32[]{:S(2)}, u32[]{:S(2)}) collective-permute-start(bf16[512,128]{1,0:T(8,128)(2,1)S(1)} %get-tuple-element.35), channel_id=1, source_target_pairs={{0,24},{1,193},{2,26},{3,195},{4,28},{5,197},{6,30},{7,199},{8,0},... | collective-permute-start | bytes 393224 | tf_op jit(solution)/shard_map/ppermute | solution.py:34
  37.3 9.2 %collective-permute-start.10 = (bf16[512,128]{1,0:T(8,128)(2,1)S(1)}, bf16[512,128]{1,0:T(8,128)(2,1)S(1)}, u32[]{:S(2)}, u32[]{:S(2)}) collective-permute-start(bf16[512,128]{1,0:T(8,128)(2,1)S(1)} %get-tuple-element.37.after), channel_id=1, source_target_pairs={{0,32},{8,40},{16,48},{24,56},{32,0},{40,8},{48,16},{56,24},{64,96... | collective-permute-start | bytes 393224 | tf_op jit(solution)/shard_map/ppermute | solution.py:38
  46.5 5.1 %collective-permute-start.13 = (bf16[512,128]{1,0:T(8,128)(2,1)S(1)}, bf16[512,128]{1,0:T(8,128)(2,1)S(1)}, u32[]{:S(2)}, u32[]{:S(2)}) collective-permute-start(bf16[512,128]{1,0:T(8,128)(2,1)S(1)} %get-tuple-element.40), channel_id=1, source_target_pairs={{0,8},{1,65},{2,10},{3,67},{4,12},{5,69},{6,14},{7,71},{8,16},{9,7... | collective-permute-start | bytes 393224 | tf_op jit(solution)/shard_map/ppermute | solution.py:34
  46.6 7.1 %collective-permute-start.12 = (bf16[512,128]{1,0:T(8,128)(2,1)S(1)}, bf16[512,128]{1,0:T(8,128)(2,1)S(1)}, u32[]{:S(2)}, u32[]{:S(2)}) collective-permute-start(bf16[512,128]{1,0:T(8,128)(2,1)S(1)} %get-tuple-element.40), channel_id=1, source_target_pairs={{0,16},{1,129},{2,18},{3,131},{4,20},{5,133},{6,22},{7,135},{8,24}... | collective-permute-start | bytes 393224 | tf_op jit(solution)/shard_map/ppermute | solution.py:34
  50.0 3.8 %collective-permute-start.11 = (bf16[512,128]{1,0:T(8,128)(2,1)S(1)}, bf16[512,128]{1,0:T(8,128)(2,1)S(1)}, u32[]{:S(2)}, u32[]{:S(2)}) collective-permute-start(bf16[512,128]{1,0:T(8,128)(2,1)S(1)} %get-tuple-element.40), channel_id=1, source_target_pairs={{0,24},{1,193},{2,26},{3,195},{4,28},{5,197},{6,30},{7,199},{8,0},... | collective-permute-start | bytes 393224 | tf_op jit(solution)/shard_map/ppermute | solution.py:34
  53.9 10.9 %collective-permute-start.16 = (bf16[4,512,128]{2,1,0:T(8,128)(2,1)S(1)}, bf16[4,512,128]{2,1,0:T(8,128)(2,1)S(1)}, u32[]{:S(2)}, u32[]{:S(2)}) collective-permute-start(bf16[4,512,128]{2,1,0:T(8,128)(2,1)S(1)} %pad_maximum_fusion.piece), channel_id=1, source_target_pairs={{0,192},{1,25},{2,194},{3,27},{4,196},{5,29},{6,198},{7,31},{8,200... | collective-permute-start | bytes 1572872 | tf_op jit(solution)/shard_map/ppermute | solution.py:34
  54.3 10.9 %collective-permute-start.15 = (bf16[4,512,128]{2,1,0:T(8,128)(2,1)S(1)}, bf16[4,512,128]{2,1,0:T(8,128)(2,1)S(1)}, u32[]{:S(2)}, u32[]{:S(2)}) collective-permute-start(bf16[4,512,128]{2,1,0:T(8,128)(2,1)S(1)} %pad_maximum_fusion.piece), channel_id=1, source_target_pairs={{0,128},{1,17},{2,130},{3,19},{4,132},{5,21},{6,134},{7,23},{8,136... | collective-permute-start | bytes 1572872 | tf_op jit(solution)/shard_map/ppermute | solution.py:34
  55.1 15.8 %collective-permute-start.17 = (bf16[4,512,128]{2,1,0:T(8,128)(2,1)S(1)}, bf16[4,512,128]{2,1,0:T(8,128)(2,1)S(1)}, u32[]{:S(2)}, u32[]{:S(2)}) collective-permute-start(bf16[4,512,128]{2,1,0:T(8,128)(2,1)S(1)} %pad_maximum_fusion.piece), channel_id=1, source_target_pairs={{0,64},{1,9},{2,66},{3,11},{4,68},{5,13},{6,70},{7,15},{8,72},{9,1... | collective-permute-start | bytes 1572872 | tf_op jit(solution)/shard_map/ppermute | solution.py:34
  72.5 12.2 %collective-permute-start.19 = (bf16[2,256,512]{2,1,0:T(8,128)(2,1)S(1)}, bf16[2,256,512]{2,1,0:T(8,128)(2,1)S(1)}, u32[]{:S(2)}, u32[]{:S(2)}) collective-permute-start(bf16[2,256,512]{2,1,0:T(8,128)(2,1)S(1)} %get-tuple-element.51), channel_id=1, source_target_pairs={{0,1},{1,0},{2,3},{3,2},{4,5},{5,4},{6,7},{7,6},{8,9},{9,8},{10,11... | collective-permute-start | bytes 1572872 | tf_op jit(solution)/shard_map/ppermute | solution.py:42
  81.4 3.3 %collective-permute-start.18 = (bf16[2,256,512]{2,1,0:T(8,128)(2,1)S(1)}, bf16[2,256,512]{2,1,0:T(8,128)(2,1)S(1)}, u32[]{:S(2)}, u32[]{:S(2)}) collective-permute-start(bf16[2,256,512]{2,1,0:T(8,128)(2,1)S(1)} %get-tuple-element.49.after), channel_id=1, source_target_pairs={{0,1},{1,0},{2,3},{3,2},{4,5},{5,4},{6,7},{7,6},{8,9},{9,8},{10,11... | collective-permute-start | bytes 1572872 | tf_op jit(solution)/shard_map/ppermute | solution.py:42
  81.5 2.4 %collective-permute-start.14 = (f32[256,128]{1,0:T(8,128)S(1)}, f32[256,128]{1,0:T(8,128)S(1)}, u32[]{:S(2)}, u32[]{:S(2)}) collective-permute-start(f32[256,128]{1,0:T(8,128)S(1)} %get-tuple-element.41), channel_id=1, source_target_pairs={{0,1},{1,0},{2,3},{3,2},{4,5},{5,4},{6,7},{7,6},{8,9},{9,8},{10,11... | collective-permute-start | bytes 393224 | tf_op jit(solution)/shard_map/ppermute | solution.py:42
where the time goes:
time: 86.4 us; the launch traced here: 86.3 us
  starting transfers between devices  31.6 us (37%)
  waiting for transfers between devices  31.5 us (36%)
  Pallas kernels  19.9 us (23%)
  local copies, waits for them, and re-layouts  2.18 us (3%)
  between operations  1.04 us (1%)
    ppermute x12, waiting for transfers between devices, moved(): return lax.ppermute(value, ('ang', 'slab'), pairs)  17.2 us
    ppermute x12, starting transfers between devices, moved(): return lax.ppermute(value, ('ang', 'slab'), pairs)  15 us
    ppermute x5, starting transfers between devices, swapped(): return lax.ppermute(value, 'slab', [(i, i ^ 1) for i in range(SLABS)])  10.3 us
    ppermute x1, waiting for transfers between devices, across(): lax.ppermute(value, 'ang', [(a, a ^ XS) for a in range(YS * ZS * XS)])  9.12 us
    ppermute x1, starting transfers between devices, steps(): before = lax.ppermute(tail, 'slab', [(i, i + 1) for i in range(count - 1)])  4.21 us
    pallas_call x2, Pallas kernels, both_rows(): call(kernel, specs, [((LINE, rows, block), dtype)], flops)  3.66 us
    ppermute x1, waiting for transfers between devices, steps(): after = lax.ppermute(head, 'slab', [(i + 1, i) for i in range(count - 1)])  3.25 us
    pallas_call x1, Pallas kernels, spread(): call(spread_kernel, [SMEM, SMEM, VMEM, ANY], outs, 1 << 31, 16)  2.63 us
  transfers between devices with their start and end apart: 20, of which 11 were waited for; matrix products, arithmetic and copies ran while one was open for 0% of the time, Pallas kernels for 13%

commit v1 on v0

--- a/solution.py
+++ b/solution.py
@@ -86,13 +86,15 @@
     )()
 
 
-def edges_kernel(volume, after, cells, head, tail):
+def edges_kernel(volume, after, cells, inner, outer):
     depth = volume.shape[2]
+    core = lax.axis_index("slab") & 1
     for c in range(2):
         turned = volume[:, c, :].T
         cells[c * depth : (c + 1) * depth, :] = turned
-        head[c : c + 1, :] = turned[:1, :]
-        tail[c : c + 1, :] = turned[depth - 1 :, :]
+        head, tail = turned[:1, :], turned[depth - 1 :, :]
+        inner[c : c + 1, :] = jnp.where(core == 0, tail, head)
+        outer[c : c + 1, :] = jnp.where(core == 0, head, tail)
 
 
 def edges(volume, after):
@@ -151,28 +153,30 @@
     )
 
 
-def join_kernel(d, table, starts, other, tiles, own, after, out):
+def join_kernel(d, table, starts, other, tiles, own, after, first, rest):
     rows = other.shape[1]
     for k in range(LINE):
         j = table[place(d) + k]
-        out[k, :rows, :] = own[k]
-        out[k, rows:, :] = product((other,), tiles, starts, j).astype(out.dtype)
+        out = first if k == 0 else rest.at[k - 1]
+        out[:rows, :] = own[k]
+        out[rows:, :] = product((other,), tiles, starts, j).astype(out.dtype)
 
 
 def joined(other, tiles, table, starts, d, own, after):
     angles, _, band, block = tiles.shape
     rows = other.shape[1]
-    outs = [((LINE, 2 * rows, block), jnp.bfloat16)]
+    outs = [((2 * rows, block), jnp.bfloat16), ((LINE - 1, 2 * rows, block), jnp.bfloat16)]
     flops = 2 * LINE * angles * rows * band * block
     kernel = functools.partial(join_kernel, d)
     specs = [SMEM, SMEM, VMEM, VMEM, VMEM, ANY]
-    return call(kernel, specs, outs, flops)(table, starts, other, tiles, own, after)[0]
-
-
-def both_kernel(d, table, starts, scaled, other, tiles, after, out):
+    return call(kernel, specs, outs, flops)(table, starts, other, tiles, own, after)
+
+
+def both_kernel(d, table, starts, scaled, other, tiles, after, first, rest):
     for k in range(LINE):
         j = table[place(d) + k]
-        out[k] = product((scaled, other), tiles, starts, j).astype(out.dtype)
+        out = first if k == 0 else rest.at[k - 1]
+        out[...] = product((scaled, other), tiles, starts, j).astype(out.dtype)
 
 
 def both_rows(scaled, other, tiles, table, starts, d, dtype, after):
@@ -181,34 +185,29 @@
     flops = 2 * LINE * angles * rows * band * block
     kernel = functools.partial(both_kernel, d)
     specs = [SMEM, SMEM, VMEM, VMEM, VMEM, ANY]
-    return call(kernel, specs, [((LINE, rows, block), dtype)], flops)(
-        table, starts, scaled, other, tiles, after
-    )[0]
-
-
-def line_kernel(own, s1, s2, s3, after, kept, *sent):
-    for k in range(LINE):
+    outs = [((rows, block), dtype), ((LINE - 1, rows, block), dtype)]
+    return call(kernel, specs, outs, flops)(table, starts, scaled, other, tiles, after)
+
+
+def line_kernel(own, s1, s2, s3, *sent):
+    for k in range(LINE - 1):
         total = own[k]
         for ref in (s1, s2, s3):
             total = total + ref[k].astype(jnp.float32)
-        if k == 0:
-            kept[...] = total
-        else:
-            sent[k - 1][...] = total.astype(jnp.bfloat16)
-
-
-def line_sum(own, arrived, after):
-    tile = own.shape[1:]
-    outs = [(tile, jnp.float32)] + [(tile, jnp.bfloat16)] * (LINE - 1)
-    kept, *sent = call(line_kernel, [VMEM] * 4 + [ANY], outs, 1 << 20)(
-        own, *arrived, after
-    )
-    return kept, sent
-
-
-def smooth_kernel(cells, before, after, smooth):
+        sent[k][...] = total.astype(jnp.bfloat16)
+
+
+def line_sum(own, arrived):
+    outs = [(own.shape[1:], jnp.bfloat16)] * (LINE - 1)
+    return call(line_kernel, [VMEM] * 4, outs, 1 << 20)(own, *arrived)
+
+
+def smooth_kernel(cells, inner, outer, smooth):
     rows, share = cells.shape
     depth = rows // 2
+    core = lax.axis_index("slab") & 1
+    before = jnp.where(core == 0, outer[...], inner[...])
+    after = jnp.where(core == 0, inner[...], outer[...])
     z = lax.broadcasted_iota(jnp.int32, (depth, share), 0)
     for c in range(2):
         at = slice(c * depth, (c + 1) * depth)
@@ -218,28 +217,26 @@
         smooth[at, :] = value - SMOOTHING * (2.0 * value - down - up)
 
 
-def smoothed(cells, before, after):
+def smoothed(cells, inner, outer):
     outs = [(cells.shape, jnp.float32)]
-    return call(smooth_kernel, [VMEM] * 3, outs, 1 << 20, 4)(cells, before, after)[0]
-
-
-def merge_kernel(smooth, beside, kept, s1, s2, s3, mine, message):
+    return call(smooth_kernel, [VMEM] * 3, outs, 1 << 20, 4)(cells, inner, outer)[0]
+
+
+def merge_kernel(smooth, beside, own, a1, a2, a3, s1, s2, s3, mine, message):
     _, zh, _, owner = position()
     rows = smooth.shape[0]
     for at, part in ((slice(0, rows), smooth), (slice(rows, 2 * rows), beside)):
-        total = kept[at, :]
-        for ref in (s1, s2, s3):
+        total = own[at, :]
+        for ref in (a1, a2, a3, s1, s2, s3):
             total = total + ref[at, :].astype(jnp.float32)
         total = jnp.where(zh == owner, total + part[...], total)
         mine[at, :] = total
         message[at, :] = total.astype(message.dtype)
 
 
-def merged(smooth, beside, kept, reached):
-    outs = [(kept.shape, jnp.float32), (kept.shape, jnp.bfloat16)]
-    return call(merge_kernel, [VMEM] * 6, outs, 1 << 20, 4)(
-        smooth, beside, kept, *reached
-    )
+def merged(smooth, beside, own, first, reached):
+    outs = [(own.shape, jnp.float32), (own.shape, jnp.bfloat16)]
+    return call(merge_kernel, [VMEM] * 9, outs, 1 << 20, 4)(smooth, beside, own, *first, *reached)
 
 
 def finish_kernel(mine, crossed, own, beside, lowered):
@@ -261,7 +258,8 @@
     return call(finish_kernel, [VMEM] * 2, outs, 1 << 20, 4)(mine, crossed)
 
 
-def turn_kernel(own, received, volume):
+def turn_kernel(own, received, volume, token):
+    token[...] = jnp.zeros_like(token)
     _, zh, _, owner = position()
     depth = volume.shape[2]
     for c in range(2):
@@ -270,7 +268,8 @@
 
 
 def turned(own, received, shape):
-    return call(turn_kernel, [VMEM] * 2, [(shape, jnp.float32)], 1 << 20, 4)(own, received)[0]
+    outs = [(shape, jnp.float32), ((8, 128), jnp.float32)]
+    return call(turn_kernel, [VMEM] * 2, outs, 1 << 20, 4)(own, received)
 
 
 PARTS = ((0,), (2, 1), (3,))
@@ -305,41 +304,49 @@
     )
 
 
+def row_of(pieces):
+    blocks = []
+    for first, rest in pieces:
+        blocks += [first[...]] + [rest[k] for k in range(LINE - 1)]
+    return jnp.concatenate(blocks, axis=1)
+
+
 def projected(pieces, weights):
-    row = jnp.concatenate([piece[k] for piece in pieces for k in range(LINE)], axis=1)
     return lax.dot_general(
-        row, weights, (((1,), (1,)), ((), ())), preferred_element_type=jnp.float32
-    )
-
-
-def near_kernel(weights, piece, image):
+        row_of(pieces), weights, (((1,), (1,)), ((), ())), preferred_element_type=jnp.float32
+    )
+
+
+def near_kernel(weights, first, rest, image):
     for a in range(image.shape[0]):
-        image[a] = projected((piece,), weights[a])
+        image[a] = projected(((first, rest),), weights[a])
 
 
 def near(piece, weights):
     angles, detector, _ = weights.shape
-    rows = piece.shape[1]
+    rows = piece[0].shape[0]
     outs = [((angles, rows, detector), jnp.float32)]
     flops = 2 * weights.size * rows
-    return call(near_kernel, [VMEM] * 2, outs, flops, 16)(weights, piece)[0]
-
-
-def next_kernel(weights, before, p1, p2, image):
+    return call(near_kernel, [VMEM] * 3, outs, flops, 16)(weights, *piece)[0]
+
+
+def next_kernel(weights, before, f1, r1, f2, r2, after, image):
     for a in range(image.shape[0]):
-        image[a] = before[a] + projected((p1, p2), weights[a])
-
-
-def further(pieces, weights, before):
+        image[a] = before[a] + projected(((f1, r1), (f2, r2)), weights[a])
+
+
+def further(pieces, weights, before, after):
     outs = [(before.shape, jnp.float32)]
     flops = 2 * weights.size * before.shape[1]
-    return call(next_kernel, [VMEM] * 4, outs, flops, 16)(weights, before, *pieces)[0]
-
-
-def last_kernel(base, weights, before, piece, after, own, message):
+    return call(next_kernel, [VMEM] * 6 + [ANY], outs, flops, 16)(
+        weights, before, *pieces[0], *pieces[1], after
+    )[0]
+
+
+def last_kernel(base, weights, before, first, rest, after, own, message):
     rows = own.shape[1]
     for i in range(own.shape[0]):
-        value = before[base + i] + projected((piece,), weights[base + i])
+        value = before[base + i] + projected(((first, rest),), weights[base + i])
         own[i] = value[:rows]
         message[i] = value[rows:].astype(message.dtype)
 
@@ -350,37 +357,35 @@
     outs = [(shape, jnp.float32), (shape, jnp.bfloat16)]
     flops = weights.size * rows
     kernel = functools.partial(last_kernel, base)
-    return call(kernel, [VMEM] * 3 + [ANY], outs, flops, 16)(
-        weights, before, piece, after
-    )
-
-
-def leave_kernel(own0, own1, got0, got1, out, image, done):
-    half = own0.shape[0]
+    return call(kernel, [VMEM] * 4 + [ANY], outs, flops, 16)(
+        weights, before, *piece, after
+    )
+
+
+def leave_kernel(base, own, got, *refs):
+    out, image, done = refs[-3:]
     copies = []
-    for h, (own, got) in enumerate(((own0, got0), (own1, got1))):
-        for i in range(half):
-            a = h * half + i
-            image[a] = own[i] + got[i].astype(jnp.float32)
-            copies.append(pltpu.make_async_copy(image.at[a], out.at[a], done.at[a]))
-            copies[-1].start()
+    for i in range(own.shape[0]):
+        image[i] = own[i] + got[i].astype(jnp.float32)
+        copies.append(pltpu.make_async_copy(image.at[i], out.at[base + i], done.at[i]))
+        copies[-1].start()
     for copy in copies:
         copy.wait()
 
 
-def leave(own, got):
-    half, rows, detector = own[0].shape
-    shape = (2 * half, rows, detector)
+def leave(own, got, base, shape, held=None):
+    half = own.shape[0]
     return pl.pallas_call(
-        leave_kernel,
-        in_specs=[VMEM] * 4,
+        functools.partial(leave_kernel, base),
+        in_specs=[VMEM] * 2 + [ANY] * (held is not None),
         out_specs=ANY,
         out_shape=jax.ShapeDtypeStruct(shape, jnp.float32),
-        scratch_shapes=[pltpu.VMEM(shape, jnp.float32), pltpu.SemaphoreType.DMA((2 * half,))],
+        scratch_shapes=[pltpu.VMEM(own.shape, jnp.float32), pltpu.SemaphoreType.DMA((half,))],
+        input_output_aliases={} if held is None else {2: 0},
         compiler_params=params(16),
         cost_estimate=pl.CostEstimate(flops=1 << 20, bytes_accessed=1 << 20, transcendentals=0),
         name="leave",
-    )(*own, *got)
+    )(own, got, *([] if held is None else [held]))
 
 
 def steps(updates, tiles, starts, ids, weights, volume):
@@ -389,47 +394,59 @@
     table = plan()
     scaled = scale(updates, table, ids, weights)
     other = swapped(scaled)
+    cells, inner, outer = edges(volume, scaled)
+    inner = swapped(inner)
+    odd = range(1, count - 1, 2)
+    outer = lax.ppermute(outer, "slab", [p for i in odd for p in ((i, i + 1), (i + 1, i))])
     own2, own1 = own_rows(scaled, tiles, table, starts, (2, 1))
     sent = {}
     sent[2] = joined(other, tiles, table, starts, 2, own2, own1)
-    sent[1] = joined(other, tiles, table, starts, 1, own1, sent[2])
-    sent[3] = both_rows(scaled, other, tiles, table, starts, 3, jnp.bfloat16, sent[1])
-    own = both_rows(scaled, other, tiles, table, starts, 0, jnp.float32, sent[3])
-    arrived = []
-    for d in FAR:
-        arrived.append(moved(sent[d], True, d))
-
-    cells, head, tail = edges(volume, own)
-    before = lax.ppermute(tail, "slab", [(i, i + 1) for i in range(count - 1)])
-    after = lax.ppermute(head, "slab", [(i + 1, i) for i in range(count - 1)])
-    kept, sent = line_sum(own, arrived, cells)
-    reached = [moved(sent[d - 1], False, d) for d in FAR]
-    smooth = smoothed(cells, before, after)
-    mine, message = merged(smooth, swapped(smooth), kept, reached)
+    sent[1] = joined(other, tiles, table, starts, 1, own1, sent[2][0])
+    sent[3] = both_rows(scaled, other, tiles, table, starts, 3, jnp.bfloat16, sent[1][0])
+    own = both_rows(scaled, other, tiles, table, starts, 0, jnp.float32, sent[3][0])
+    first, arrived = [], []
+    for d in FAR:
+        arrived.append(moved(sent[d][1], True, d))
+    for d in FAR:
+        first.append(moved(sent[d][0], True, d))
+    passed = line_sum(own[1], arrived)
+    reached = []
+    for d in FAR:
+        reached.append(moved(passed[d - 1], False, d))
+    smooth = smoothed(cells, inner, outer)
+    beside = swapped(smooth)
+    mine, message = merged(smooth, beside, own[0], first, reached)
     crossed = across(message)
     bands = spread(tiles, table, starts, detector, message)
     own, beside, lowered = finished(mine, crossed)
 
-    came = {}
+    came, first = {}, {}
     for d in FAR:
         came[d] = moved(lowered, False, LINE - d)
+    for d in FAR:
+        first[d] = moved(lowered, True, LINE - d)
     beside, came[1], came[2], came[3] = lax.optimization_barrier(
         (beside, came[1], came[2], came[3])
     )
-    line = jnp.stack([lowered] + [came[d] for d in range(1, LINE)])
+    line = jnp.stack([came[d] for d in range(1, LINE)])
     rest = {}
     for d in FAR:
         rest[d] = moved(line, True, LINE - d)
     received = swapped(beside)
-    volume_next = turned(own, received, volume.shape)
-    image = near(line, bands[0])
-    image = further([rest[2], rest[1]], bands[1], image)
+    volume_next, token = turned(own, received, volume.shape)
+    image = near((lowered, line), bands[0])
+    image = further(
+        [(first[2], rest[2]), (first[1], rest[1])], bands[1], image, token
+    )
     half = angles // 2
-    own0, message0 = last(rest[3], bands[2], image, 0, half, image)
+    piece = first[3], rest[3]
+    own0, message0 = last(piece, bands[2], image, 0, half, image)
     got0 = swapped(message0)
-    own1, message1 = last(rest[3], bands[2], image, half, half, message0)
+    own1, message1 = last(piece, bands[2], image, half, half, message0)
     got1 = swapped(message1)
-    projection = leave([own0, own1], [got0, got1])
+    shape = (angles, 2 * depth, detector)
+    projection = leave(own0, got0, 0, shape)
+    projection = leave(own1, got1, half, shape, projection)
     return volume_next, projection.reshape(angles, 2, depth, detector)
 
 

time: 86.4 us -> 86.7 us (level)
  the two profiles are of different devices: /device:TPU:161 before, /device:TPU:1 now
where the time goes in v1:
time: 86.7 us; the launch traced here: 86.6 us
  starting transfers between devices  44.9 us (52%)
  Pallas kernels  20.6 us (24%)
  waiting for transfers between devices  19 us (22%)
  between operations  1.02 us (1%)
  local copies, waits for them, and re-layouts  0.94 us (1%)
    ppermute x18, starting transfers between devices, moved(): return lax.ppermute(value, ('ang', 'slab'), pairs)  21.4 us
    ppermute x6, starting transfers between devices, swapped(): return lax.ppermute(value, 'slab', [(i, i ^ 1) for i in range(SLABS)])  13.1 us
    ppermute x18, waiting for transfers between devices, moved(): return lax.ppermute(value, ('ang', 'slab'), pairs)  13 us
    ppermute x1, starting transfers between devices, across(): lax.ppermute(value, 'ang', [(a, a ^ XS) for a in range(YS * ZS * XS)])  7 us
    pallas_call x2, Pallas kernels, both_rows(): call(kernel, specs, outs, flops)(table, starts, scaled, other, tiles, after)  3.66 us
    ppermute x1, starting transfers between devices, steps(): lax.ppermute(outer, 'slab', [p for i in odd for p in ((i, i + 1), (i + 1,...  3.44 us
    ppermute x1, waiting for transfers between devices, across(): lax.ppermute(value, 'ang', [(a, a ^ XS) for a in range(YS * ZS * XS)])  2.94 us
    pallas_call x1, Pallas kernels, spread(): call(spread_kernel, [SMEM, SMEM, VMEM, ANY], outs, 1 << 31, 16)  2.63 us
  transfers between devices with their start and end apart: 26, of which 12 were waited for; matrix products, arithmetic and copies ran while one was open for 0% of the time, Pallas kernels for 17%

profile of v1, /device:TPU:1, one launch (start us, length us, event | category | flops | bytes accessed | tf_op | source)
XLA Modules:
  0.0 86.6 jit_solution(10637626843553948163)
XLA Ops:
  0.7 0.6 plan.1.table
  1.3 0.9 %copy-done.2 = f32[4,2,128,512]{3,2,1,0:T(8,128)S(1)} copy-done((f32[4,2,128,512]{3,2,1,0:T(8,128)S(1)}, f32[4,2,128,512]{3,2,1,0:T(8,128)}, u32[]{:S(2)}) %copy-start.2) | copy-done | bytes 2097176
  2.3 0.7 shard_map.77.after.scaled
  2.9 3.3 %collective-permute-start.3 = (bf16[4,256,512]{2,1,0:T(8,128)(2,1)S(1)}, bf16[4,256,512]{2,1,0:T(8,128)(2,1)S(1)}, u32[]{:S(2)}, u32[]{:S(2)}) collective-permute-start(bf16[4,256,512]{2,1,0:T(8,128)(2,1)S(1)} %shard_map.77.after.scaled), channel_id=1, source_target_pairs={{0,1},{1,0},{2,3},{3,2},{4,5},{5,4},{6,7},{7,6},{8,9},{9,8},{10,11... | collective-permute-start | bytes 3145736 | tf_op jit(solution)/shard_map/ppermute | solution.py:42
  6.2 1.8 %shard_map.80 = (bf16[4,256,128]{2,1,0:T(8,128)(2,1)S(1)}, bf16[4,256,128]{2,1,0:T(8,128)(2,1)S(1)}) custom-call(s32[16]{0:T(128)S(1)} %plan.1.table, s32[4,32]{1,0:T(4,128)S(1)} %copy-done.1, bf16[4,256,512]{2,1,0:T(8,128)(2,1)S(1)} %shard_map.77.after.scaled, bf16[4,32,256,128]{3,2,1,0:T(8,128)(2,1)S(1)} %bitcast.5), custom_call_target="tpu_custom_call" | custom-call | flops 536870912 | bytes 1048576 | tf_op jit(solution)/shard_map/pallas_call | solution.py:151
  8.1 0.4 collective-permute-done.3.other
  8.5 1.3 %shard_map.81 = (bf16[512,128]{1,0:T(8,128)(2,1)S(1)}, bf16[3,512,128]{2,1,0:T(8,128)(2,1)S(1)}) custom-call(s32[16]{0:T(128)S(1)} %plan.1.table, s32[4,32]{1,0:T(4,128)S(1)} %copy-done.1, bf16[4,256,512]{2,1,0:T(8,128)(2,1)S(1)} %collective-permute-done.3.other, bf16[4,32,256,128]{3,2,1,0:T(8,128)(2,1)S(1)} %bitcast.5, ...), custom_call_target="tpu_custom_call" | custom-call | flops 268435456 | bytes 1048576 | tf_op jit(solution)/shard_map/pallas_call | solution.py:172
  9.8 1.3 %shard_map.82 = (bf16[512,128]{1,0:T(8,128)(2,1)S(1)}, bf16[3,512,128]{2,1,0:T(8,128)(2,1)S(1)}) custom-call(s32[16]{0:T(128)S(1)} %plan.1.table, s32[4,32]{1,0:T(4,128)S(1)} %copy-done.1, bf16[4,256,512]{2,1,0:T(8,128)(2,1)S(1)} %collective-permute-done.3.other, bf16[4,32,256,128]{3,2,1,0:T(8,128)(2,1)S(1)} %bitcast.5, ...), custom_call_target="tpu_custom_call" | custom-call | flops 268435456 | bytes 1048576 | tf_op jit(solution)/shard_map/pallas_call | solution.py:172
  11.1 0.4 collective-permute-start.8
  11.5 2.5 %collective-permute-start.7 = (bf16[3,512,128]{2,1,0:T(8,128)(2,1)S(1)}, bf16[3,512,128]{2,1,0:T(8,128)(2,1)S(1)}, u32[]{:S(2)}, u32[]{:S(2)}) collective-permute-start(bf16[3,512,128]{2,1,0:T(8,128)(2,1)S(1)} %get-tuple-element.46), channel_id=1, source_target_pairs={{0,128},{1,17},{2,130},{3,19},{4,132},{5,21},{6,134},{7,23},{8,136... | collective-permute-start | bytes 1179656 | tf_op jit(solution)/shard_map/ppermute | solution.py:34
  13.9 1.8 %shard_map.83 = (bf16[512,128]{1,0:T(8,128)(2,1)S(1)}, bf16[3,512,128]{2,1,0:T(8,128)(2,1)S(1)}) custom-call(s32[16]{0:T(128)S(1)} %plan.1.table, s32[4,32]{1,0:T(4,128)S(1)} %copy-done.1, bf16[4,256,512]{2,1,0:T(8,128)(2,1)S(1)} %shard_map.77.after.scaled, bf16[4,256,512]{2,1,0:T(8,128)(2,1)S(1)} %collective-permute-done.3.other, ...), custom_call_target="tpu_custom_call" | custom-call | flops 536870912 | bytes 1048576 | tf_op jit(solution)/shard_map/pallas_call | solution.py:189
  15.7 1.2 %collective-permute-start.9 = (bf16[3,512,128]{2,1,0:T(8,128)(2,1)S(1)}, bf16[3,512,128]{2,1,0:T(8,128)(2,1)S(1)}, u32[]{:S(2)}, u32[]{:S(2)}) collective-permute-start(bf16[3,512,128]{2,1,0:T(8,128)(2,1)S(1)} %get-tuple-element.48), channel_id=1, source_target_pairs={{0,192},{1,25},{2,194},{3,27},{4,196},{5,29},{6,198},{7,31},{8,200... | collective-permute-start | bytes 1179656 | tf_op jit(solution)/shard_map/ppermute | solution.py:34
  17.1 1.8 %collective-permute-start = (f32[2,128]{1,0:T(2,128)S(1)}, f32[2,128]{1,0:T(2,128)S(1)}, u32[]{:S(2)}, u32[]{:S(2)}) collective-permute-start(f32[2,128]{1,0:T(2,128)S(1)} %get-tuple-element.37), channel_id=1, source_target_pairs={{0,1},{1,0},{2,3},{3,2},{4,5},{5,4},{6,7},{7,6},{8,9},{9,8},{10,11... | collective-permute-start | bytes 3080 | tf_op jit(solution)/shard_map/ppermute | solution.py:42
  18.9 3.4 %collective-permute-start.1 = (f32[2,128]{1,0:T(2,128)S(1)}, f32[2,128]{1,0:T(2,128)S(1)}, u32[]{:S(2)}, u32[]{:S(2)}) collective-permute-start(f32[2,128]{1,0:T(2,128)S(1)} %get-tuple-element.38), channel_id=1, source_target_pairs={{1,2},{2,1},{3,4},{4,3},{5,6},{6,5},{9,10},{10,9},{11,12},{12,11},... | collective-permute-start | bytes 3080 | tf_op jit(solution)/shard_map/ppermute | solution.py:400
  22.4 1.7 %collective-permute-done.1.outer = f32[2,128]{1,0:T(2,128)S(1)} collective-permute-done((f32[2,128]{1,0:T(2,128)S(1)}, f32[2,128]{1,0:T(2,128)S(1)}, u32[]{:S(2)}, u32[]{:S(2)}) %collective-permute-start.1) | collective-permute-done | bytes 1056 | tf_op jit(solution)/shard_map/ppermute | solution.py:400
  24.2 2.8 %collective-permute-start.4 = (bf16[512,128]{1,0:T(8,128)(2,1)S(1)}, bf16[512,128]{1,0:T(8,128)(2,1)S(1)}, u32[]{:S(2)}, u32[]{:S(2)}) collective-permute-start(bf16[512,128]{1,0:T(8,128)(2,1)S(1)} %get-tuple-element.41.after), channel_id=1, source_target_pairs={{0,128},{1,17},{2,130},{3,19},{4,132},{5,21},{6,134},{7,23},{8,136... | collective-permute-start | bytes 393224 | tf_op jit(solution)/shard_map/ppermute | solution.py:34
  27.0 1.8 %shard_map.84 = (f32[512,128]{1,0:T(8,128)S(1)}, f32[3,512,128]{2,1,0:T(8,128)S(1)}) custom-call(s32[16]{0:T(128)S(1)} %plan.1.table, s32[4,32]{1,0:T(4,128)S(1)} %copy-done.1, bf16[4,256,512]{2,1,0:T(8,128)(2,1)S(1)} %shard_map.77.after.scaled, bf16[4,256,512]{2,1,0:T(8,128)(2,1)S(1)} %collective-permute-done.3.other, ...), custom_call_target="tpu_custom_call" | custom-call | flops 536870912 | bytes 1048576 | tf_op jit(solution)/shard_map/pallas_call | solution.py:189
  28.9 0.4 collective-permute-start.5
  29.3 2.3 %collective-permute-start.6 = (bf16[512,128]{1,0:T(8,128)(2,1)S(1)}, bf16[512,128]{1,0:T(8,128)(2,1)S(1)}, u32[]{:S(2)}, u32[]{:S(2)}) collective-permute-start(bf16[512,128]{1,0:T(8,128)(2,1)S(1)} %get-tuple-element.43.after), channel_id=1, source_target_pairs={{0,192},{1,25},{2,194},{3,27},{4,196},{5,29},{6,198},{7,31},{8,200... | collective-permute-start | bytes 393224 | tf_op jit(solution)/shard_map/ppermute | solution.py:34
  32.0 0.4 collective-permute-start.11
  32.5 2.6 %collective-permute-start.12 = (bf16[512,128]{1,0:T(8,128)(2,1)S(1)}, bf16[512,128]{1,0:T(8,128)(2,1)S(1)}, u32[]{:S(2)}, u32[]{:S(2)}) collective-permute-start(bf16[512,128]{1,0:T(8,128)(2,1)S(1)} %get-tuple-element.51), channel_id=1, source_target_pairs={{0,24},{1,193},{2,26},{3,195},{4,28},{5,197},{6,30},{7,199},{8,0},... | collective-permute-start | bytes 393224 | tf_op jit(solution)/shard_map/ppermute | solution.py:34
  35.0 2.6 %collective-permute-done.10.s1 = bf16[512,128]{1,0:T(8,128)(2,1)S(1)} collective-permute-done((bf16[512,128]{1,0:T(8,128)(2,1)S(1)}, bf16[512,128]{1,0:T(8,128)(2,1)S(1)}, u32[]{:S(2)}, u32[]{:S(2)}) %collective-permute-start.10) | collective-permute-done | bytes 131104 | tf_op jit(solution)/shard_map/ppermute | solution.py:34
  37.6 1.2 %collective-permute-done.11.s2 = bf16[512,128]{1,0:T(8,128)(2,1)S(1)} collective-permute-done((bf16[512,128]{1,0:T(8,128)(2,1)S(1)}, bf16[512,128]{1,0:T(8,128)(2,1)S(1)}, u32[]{:S(2)}, u32[]{:S(2)}) %collective-permute-start.11) | collective-permute-done | bytes 131104 | tf_op jit(solution)/shard_map/ppermute | solution.py:34
  39.0 7.0 %collective-permute-start.13 = (bf16[512,128]{1,0:T(8,128)(2,1)S(1)}, bf16[512,128]{1,0:T(8,128)(2,1)S(1)}, u32[]{:S(2)}, u32[]{:S(2)}) collective-permute-start(bf16[512,128]{1,0:T(8,128)(2,1)S(1)} %get-tuple-element.53.after), channel_id=1, source_target_pairs={{0,32},{8,40},{16,48},{24,56},{32,0},{40,8},{48,16},{56,24},{64,96... | collective-permute-start | bytes 393224 | tf_op jit(solution)/shard_map/ppermute | solution.py:38
  46.0 2.9 %collective-permute-done.13.crossed = bf16[512,128]{1,0:T(8,128)(2,1)S(1)} collective-permute-done((bf16[512,128]{1,0:T(8,128)(2,1)S(1)}, bf16[512,128]{1,0:T(8,128)(2,1)S(1)}, u32[]{:S(2)}, u32[]{:S(2)}) %collective-permute-start.13) | collective-permute-done | bytes 131104 | tf_op jit(solution)/shard_map/ppermute | solution.py:38
  48.9 1.0 %collective-permute-start.16 = (bf16[512,128]{1,0:T(8,128)(2,1)S(1)}, bf16[512,128]{1,0:T(8,128)(2,1)S(1)}, u32[]{:S(2)}, u32[]{:S(2)}) collective-permute-start(bf16[512,128]{1,0:T(8,128)(2,1)S(1)} %get-tuple-element.56.first), channel_id=1, source_target_pairs={{0,8},{1,65},{2,10},{3,67},{4,12},{5,69},{6,14},{7,71},{8,16},{9,7... | collective-permute-start | bytes 393224 | tf_op jit(solution)/shard_map/ppermute | solution.py:34
  49.9 1.8 %collective-permute-start.15 = (bf16[512,128]{1,0:T(8,128)(2,1)S(1)}, bf16[512,128]{1,0:T(8,128)(2,1)S(1)}, u32[]{:S(2)}, u32[]{:S(2)}) collective-permute-start(bf16[512,128]{1,0:T(8,128)(2,1)S(1)} %get-tuple-element.56.first), channel_id=1, source_target_pairs={{0,16},{1,129},{2,18},{3,131},{4,20},{5,133},{6,22},{7,135},{8,24}... | collective-permute-start | bytes 393224 | tf_op jit(solution)/shard_map/ppermute | solution.py:34
  51.7 0.7 collective-permute-start.14
  52.4 1.6 %collective-permute-done.16 = bf16[512,128]{1,0:T(8,128)(2,1)S(1)} collective-permute-done((bf16[512,128]{1,0:T(8,128)(2,1)S(1)}, bf16[512,128]{1,0:T(8,128)(2,1)S(1)}, u32[]{:S(2)}, u32[]{:S(2)}) %collective-permute-start.16) | collective-permute-done | bytes 131104 | tf_op jit(solution)/shard_map/ppermute | solution.py:34
  54.0 1.5 %collective-permute-done.15 = bf16[512,128]{1,0:T(8,128)(2,1)S(1)} collective-permute-done((bf16[512,128]{1,0:T(8,128)(2,1)S(1)}, bf16[512,128]{1,0:T(8,128)(2,1)S(1)}, u32[]{:S(2)}, u32[]{:S(2)}) %collective-permute-start.15) | collective-permute-done | bytes 131104 | tf_op jit(solution)/shard_map/ppermute | solution.py:34
  55.5 0.8 collective-permute-done.14
  56.3 4.6 %collective-permute-start.17 = (f32[256,128]{1,0:T(8,128)S(1)}, f32[256,128]{1,0:T(8,128)S(1)}, u32[]{:S(2)}, u32[]{:S(2)}) collective-permute-start(f32[256,128]{1,0:T(8,128)S(1)} %get-tuple-element.57), channel_id=1, source_target_pairs={{0,1},{1,0},{2,3},{3,2},{4,5},{5,4},{6,7},{7,6},{8,9},{9,8},{10,11... | collective-permute-start | bytes 393224 | tf_op jit(solution)/shard_map/ppermute | solution.py:42
  61.0 1.3 %collective-permute-start.21 = (bf16[3,512,128]{2,1,0:T(8,128)(2,1)S(1)}, bf16[3,512,128]{2,1,0:T(8,128)(2,1)S(1)}, u32[]{:S(2)}, u32[]{:S(2)}) collective-permute-start(bf16[3,512,128]{2,1,0:T(8,128)(2,1)S(1)} %pad_maximum_fusion.rest), channel_id=1, source_target_pairs={{0,192},{1,25},{2,194},{3,27},{4,196},{5,29},{6,198},{7,31},{8,200... | collective-permute-start | bytes 1179656 | tf_op jit(solution)/shard_map/ppermute | solution.py:34
  62.4 2.5 %collective-permute-start.20 = (bf16[512,128]{1,0:T(8,128)(2,1)S(1)}, bf16[512,128]{1,0:T(8,128)(2,1)S(1)}, u32[]{:S(2)}, u32[]{:S(2)}) collective-permute-start(bf16[512,128]{1,0:T(8,128)(2,1)S(1)} %get-tuple-element.56.first), channel_id=1, source_target_pairs={{0,192},{1,25},{2,194},{3,27},{4,196},{5,29},{6,198},{7,31},{8,200... | collective-permute-start | bytes 393224 | tf_op jit(solution)/shard_map/ppermute | solution.py:34
  64.9 0.4 collective-permute-start.18
  65.3 0.9 collective-permute-start.23
  66.2 2.6 %shard_map.89 = (bf16[4,512,512]{2,1,0:T(8,128)(2,1)S(1)}, bf16[4,512,1024]{2,1,0:T(8,128)(2,1)S(1)}, bf16[4,512,512]{2,1,0:T(8,128)(2,1)S(1)}) custom-call(s32[16]{0:T(128)S(1)} %plan.1.table, s32[4,32]{1,0:T(4,128)S(1)} %copy-done.1, bf16[4,32,256,128]{3,2,1,0:T(8,128)(2,1)S(1)} %bitcast.5, bf16[512,128]{1,0:T(8,128)(2,1)S(1)} %get-tuple-element.53.after), custom_call_target="tpu_custom_call" | custom-call | flops 2147483648 | bytes 1048576 | tf_op jit(solution)/shard_map/pallas_call | solution.py:302
  68.8 1.3 %shard_map.90.before = f32[4,512,512]{2,1,0:T(8,128)S(1)} custom-call(bf16[4,512,512]{2,1,0:T(8,128)(2,1)S(1)} %get-tuple-element.61.weights, bf16[512,128]{1,0:T(8,128)(2,1)S(1)} %get-tuple-element.56.first, bf16[3,512,128]{2,1,0:T(8,128)(2,1)S(1)} %pad_maximum_fusion.rest), custom_call_target="tpu_custom_call" | custom-call | flops 1073741824 | bytes 1048576 | tf_op jit(solution)/shard_map/pallas_call | solution.py:330
  70.1 0.8 shard_map.88
  70.9 2.7 %collective-permute-done.20.f2 = bf16[512,128]{1,0:T(8,128)(2,1)S(1)} collective-permute-done((bf16[512,128]{1,0:T(8,128)(2,1)S(1)}, bf16[512,128]{1,0:T(8,128)(2,1)S(1)}, u32[]{:S(2)}, u32[]{:S(2)}) %collective-permute-start.20) | collective-permute-done | bytes 131104 | tf_op jit(solution)/shard_map/ppermute | solution.py:34
  73.7 2.4 %shard_map.91.before.after = f32[4,512,512]{2,1,0:T(8,128)S(1)} custom-call(bf16[4,512,1024]{2,1,0:T(8,128)(2,1)S(1)} %get-tuple-element.60.weights, f32[4,512,512]{2,1,0:T(8,128)S(1)} %shard_map.90.before, bf16[512,128]{1,0:T(8,128)(2,1)S(1)} %collective-permute-done.18.f1, bf16[3,512,128]{2,1,0:T(8,128)(2,1)S(1)} %collective-permute-done.19.r1, ...), custom_call_target="tpu_custom_call" | custom-call | flops 2147483648 | bytes 1048576 | tf_op jit(solution)/shard_map/pallas_call | solution.py:341
  76.1 2.6 %collective-permute-done.22.first = bf16[512,128]{1,0:T(8,128)(2,1)S(1)} collective-permute-done((bf16[512,128]{1,0:T(8,128)(2,1)S(1)}, bf16[512,128]{1,0:T(8,128)(2,1)S(1)}, u32[]{:S(2)}, u32[]{:S(2)}) %collective-permute-start.22) | collective-permute-done | bytes 131104 | tf_op jit(solution)/shard_map/ppermute | solution.py:34
  78.7 0.8 shard_map.92
  79.4 3.2 %collective-permute-start.25 = (bf16[2,256,512]{2,1,0:T(8,128)(2,1)S(1)}, bf16[2,256,512]{2,1,0:T(8,128)(2,1)S(1)}, u32[]{:S(2)}, u32[]{:S(2)}) collective-permute-start(bf16[2,256,512]{2,1,0:T(8,128)(2,1)S(1)} %get-tuple-element.66.after), channel_id=1, source_target_pairs={{0,1},{1,0},{2,3},{3,2},{4,5},{5,4},{6,7},{7,6},{8,9},{9,8},{10,11... | collective-permute-start | bytes 1572872 | tf_op jit(solution)/shard_map/ppermute | solution.py:42
  82.6 0.8 shard_map.93
  83.5 0.7 collective-permute-done.25.got
  84.2 1.0 %leave.2.refs_0_ = f32[4,256,512]{2,1,0:T(8,128)} custom-call(f32[2,256,512]{2,1,0:T(8,128)S(1)} %get-tuple-element.69.own, bf16[2,256,512]{2,1,0:T(8,128)(2,1)S(1)} %collective-permute-done.25.got), custom_call_target="tpu_custom_call" | custom-call | flops 1048576 | bytes 1048576 | tf_op jit(solution)/shard_map/leave/pallas_call | solution.py:378
  85.4 1.0 %leave.3 = f32[4,256,512]{2,1,0:T(8,128)} custom-call(f32[2,256,512]{2,1,0:T(8,128)S(1)} %get-tuple-element.67.own, bf16[2,256,512]{2,1,0:T(8,128)(2,1)S(1)} %collective-permute-done.24.got, f32[4,256,512]{2,1,0:T(8,128)} %leave.2.refs_0_), custom_call_target="tpu_custom_call", output_to_operand_aliasing={{}: (2, {})} | custom-call | flops 1048576 | bytes 1048576 | tf_op jit(solution)/shard_map/leave/pallas_call | solution.py:378
  (40 shorter events, 1.3 us)
Async XLA Ops:
  0.6 0.7 copy-start.4
  0.6 0.7 copy-start.3
  0.6 1.6 %copy-start.2 = (f32[4,2,128,512]{3,2,1,0:T(8,128)S(1)}, f32[4,2,128,512]{3,2,1,0:T(8,128)}, u32[]{:S(2)}) copy-start(f32[4,2,128,512]{3,2,1,0:T(8,128)} %updates.1) | copy-start | bytes 6291460
  0.7 5.6 %slice-start = ((s8[8388608]{0:T(1024)(128)(4,1)}), s8[4194304]{0:T(1024)(128)(4,1)S(1)}, s32[]{:S(2)}) async-start(s8[8388608]{0:T(1024)(128)(4,1)} %bitcast.4), calls=%async_computation | async-start | bytes 8388608
  2.3 4.0 %slice-start.1 = ((s8[8388608]{0:T(1024)(128)(4,1)}), s8[4194304]{0:T(1024)(128)(4,1)S(1)}, s32[]{:S(2)}) async-start(s8[8388608]{0:T(1024)(128)(4,1)} %bitcast.4), calls=%async_computation.1 | async-start | bytes 8388608
  2.3 4.0 %copy-start.1 = (s32[4,32]{1,0:T(4,128)S(1)}, s32[4,32]{1,0:T(4,128)}, u32[]{:S(2)}) copy-start(s32[4,32]{1,0:T(4,128)} %starts.11) | copy-start | bytes 1540
  2.9 5.6 %collective-permute-start.3 = (bf16[4,256,512]{2,1,0:T(8,128)(2,1)S(1)}, bf16[4,256,512]{2,1,0:T(8,128)(2,1)S(1)}, u32[]{:S(2)}, u32[]{:S(2)}) collective-permute-start(bf16[4,256,512]{2,1,0:T(8,128)(2,1)S(1)} %shard_map.77.after.scaled), channel_id=1, source_target_pairs={{0,1},{1,0},{2,3},{3,2},{4,5},{5,4},{6,7},{7,6},{8,9},{9,8},{10,11... | collective-permute-start | bytes 3145736 | tf_op jit(solution)/shard_map/ppermute | solution.py:42
  11.1 17.8 %collective-permute-start.8 = (bf16[3,512,128]{2,1,0:T(8,128)(2,1)S(1)}, bf16[3,512,128]{2,1,0:T(8,128)(2,1)S(1)}, u32[]{:S(2)}, u32[]{:S(2)}) collective-permute-start(bf16[3,512,128]{2,1,0:T(8,128)(2,1)S(1)} %get-tuple-element.47), channel_id=1, source_target_pairs={{0,64},{1,9},{2,66},{3,11},{4,68},{5,13},{6,70},{7,15},{8,72},{9,1... | collective-permute-start | bytes 1179656 | tf_op jit(solution)/shard_map/ppermute | solution.py:34
  11.5 17.9 %collective-permute-start.7 = (bf16[3,512,128]{2,1,0:T(8,128)(2,1)S(1)}, bf16[3,512,128]{2,1,0:T(8,128)(2,1)S(1)}, u32[]{:S(2)}, u32[]{:S(2)}) collective-permute-start(bf16[3,512,128]{2,1,0:T(8,128)(2,1)S(1)} %get-tuple-element.46), channel_id=1, source_target_pairs={{0,128},{1,17},{2,130},{3,19},{4,132},{5,21},{6,134},{7,23},{8,136... | collective-permute-start | bytes 1179656 | tf_op jit(solution)/shard_map/ppermute | solution.py:34
  13.9 3.1 %copy-start = (f32[128,2,128]{2,1,0:T(2,128)S(1)}, f32[128,2,128]{2,1,0:T(2,128)}, u32[]{:S(2)}) copy-start(f32[128,2,128]{2,1,0:T(2,128)} %volume.1) | copy-start | bytes 393220
  15.7 15.9 %collective-permute-start.9 = (bf16[3,512,128]{2,1,0:T(8,128)(2,1)S(1)}, bf16[3,512,128]{2,1,0:T(8,128)(2,1)S(1)}, u32[]{:S(2)}, u32[]{:S(2)}) collective-permute-start(bf16[3,512,128]{2,1,0:T(8,128)(2,1)S(1)} %get-tuple-element.48), channel_id=1, source_target_pairs={{0,192},{1,25},{2,194},{3,27},{4,196},{5,29},{6,198},{7,31},{8,200... | collective-permute-start | bytes 1179656 | tf_op jit(solution)/shard_map/ppermute | solution.py:34
  17.1 5.2 %collective-permute-start = (f32[2,128]{1,0:T(2,128)S(1)}, f32[2,128]{1,0:T(2,128)S(1)}, u32[]{:S(2)}, u32[]{:S(2)}) collective-permute-start(f32[2,128]{1,0:T(2,128)S(1)} %get-tuple-element.37), channel_id=1, source_target_pairs={{0,1},{1,0},{2,3},{3,2},{4,5},{5,4},{6,7},{7,6},{8,9},{9,8},{10,11... | collective-permute-start | bytes 3080 | tf_op jit(solution)/shard_map/ppermute | solution.py:42
  18.9 5.2 %collective-permute-start.1 = (f32[2,128]{1,0:T(2,128)S(1)}, f32[2,128]{1,0:T(2,128)S(1)}, u32[]{:S(2)}, u32[]{:S(2)}) collective-permute-start(f32[2,128]{1,0:T(2,128)S(1)} %get-tuple-element.38), channel_id=1, source_target_pairs={{1,2},{2,1},{3,4},{4,3},{5,6},{6,5},{9,10},{10,9},{11,12},{12,11},... | collective-permute-start | bytes 3080 | tf_op jit(solution)/shard_map/ppermute | solution.py:400
  24.1 7.9 %collective-permute-start.2 = (f32[256,128]{1,0:T(8,128)S(1)}, f32[256,128]{1,0:T(8,128)S(1)}, u32[]{:S(2)}, u32[]{:S(2)}) collective-permute-start(f32[256,128]{1,0:T(8,128)S(1)} %shard_map.79.smooth), channel_id=1, source_target_pairs={{0,1},{1,0},{2,3},{3,2},{4,5},{5,4},{6,7},{7,6},{8,9},{9,8},{10,11... | collective-permute-start | bytes 393224 | tf_op jit(solution)/shard_map/ppermute | solution.py:42
  24.2 8.2 %collective-permute-start.4 = (bf16[512,128]{1,0:T(8,128)(2,1)S(1)}, bf16[512,128]{1,0:T(8,128)(2,1)S(1)}, u32[]{:S(2)}, u32[]{:S(2)}) collective-permute-start(bf16[512,128]{1,0:T(8,128)(2,1)S(1)} %get-tuple-element.41.after), channel_id=1, source_target_pairs={{0,128},{1,17},{2,130},{3,19},{4,132},{5,21},{6,134},{7,23},{8,136... | collective-permute-start | bytes 393224 | tf_op jit(solution)/shard_map/ppermute | solution.py:34
  28.9 6.1 %collective-permute-start.5 = (bf16[512,128]{1,0:T(8,128)(2,1)S(1)}, bf16[512,128]{1,0:T(8,128)(2,1)S(1)}, u32[]{:S(2)}, u32[]{:S(2)}) collective-permute-start(bf16[512,128]{1,0:T(8,128)(2,1)S(1)} %get-tuple-element.42.after), channel_id=1, source_target_pairs={{0,64},{1,9},{2,66},{3,11},{4,68},{5,13},{6,70},{7,15},{8,72},{9,1... | collective-permute-start | bytes 393224 | tf_op jit(solution)/shard_map/ppermute | solution.py:34
  29.3 5.7 %collective-permute-start.6 = (bf16[512,128]{1,0:T(8,128)(2,1)S(1)}, bf16[512,128]{1,0:T(8,128)(2,1)S(1)}, u32[]{:S(2)}, u32[]{:S(2)}) collective-permute-start(bf16[512,128]{1,0:T(8,128)(2,1)S(1)} %get-tuple-element.43.after), channel_id=1, source_target_pairs={{0,192},{1,25},{2,194},{3,27},{4,196},{5,29},{6,198},{7,31},{8,200... | collective-permute-start | bytes 393224 | tf_op jit(solution)/shard_map/ppermute | solution.py:34
  31.9 5.8 %collective-permute-start.10 = (bf16[512,128]{1,0:T(8,128)(2,1)S(1)}, bf16[512,128]{1,0:T(8,128)(2,1)S(1)}, u32[]{:S(2)}, u32[]{:S(2)}) collective-permute-start(bf16[512,128]{1,0:T(8,128)(2,1)S(1)} %get-tuple-element.49), channel_id=1, source_target_pairs={{0,16},{1,129},{2,18},{3,131},{4,20},{5,133},{6,22},{7,135},{8,24}... | collective-permute-start | bytes 393224 | tf_op jit(solution)/shard_map/ppermute | solution.py:34
  32.0 6.8 %collective-permute-start.11 = (bf16[512,128]{1,0:T(8,128)(2,1)S(1)}, bf16[512,128]{1,0:T(8,128)(2,1)S(1)}, u32[]{:S(2)}, u32[]{:S(2)}) collective-permute-start(bf16[512,128]{1,0:T(8,128)(2,1)S(1)} %get-tuple-element.50), channel_id=1, source_target_pairs={{0,8},{1,65},{2,10},{3,67},{4,12},{5,69},{6,14},{7,71},{8,16},{9,7... | collective-permute-start | bytes 393224 | tf_op jit(solution)/shard_map/ppermute | solution.py:34
  32.5 6.3 %collective-permute-start.12 = (bf16[512,128]{1,0:T(8,128)(2,1)S(1)}, bf16[512,128]{1,0:T(8,128)(2,1)S(1)}, u32[]{:S(2)}, u32[]{:S(2)}) collective-permute-start(bf16[512,128]{1,0:T(8,128)(2,1)S(1)} %get-tuple-element.51), channel_id=1, source_target_pairs={{0,24},{1,193},{2,26},{3,195},{4,28},{5,197},{6,30},{7,199},{8,0},... | collective-permute-start | bytes 393224 | tf_op jit(solution)/shard_map/ppermute | solution.py:34
  39.0 9.9 %collective-permute-start.13 = (bf16[512,128]{1,0:T(8,128)(2,1)S(1)}, bf16[512,128]{1,0:T(8,128)(2,1)S(1)}, u32[]{:S(2)}, u32[]{:S(2)}) collective-permute-start(bf16[512,128]{1,0:T(8,128)(2,1)S(1)} %get-tuple-element.53.after), channel_id=1, source_target_pairs={{0,32},{8,40},{16,48},{24,56},{32,0},{40,8},{48,16},{56,24},{64,96... | collective-permute-start | bytes 393224 | tf_op jit(solution)/shard_map/ppermute | solution.py:38
  48.9 5.1 %collective-permute-start.16 = (bf16[512,128]{1,0:T(8,128)(2,1)S(1)}, bf16[512,128]{1,0:T(8,128)(2,1)S(1)}, u32[]{:S(2)}, u32[]{:S(2)}) collective-permute-start(bf16[512,128]{1,0:T(8,128)(2,1)S(1)} %get-tuple-element.56.first), channel_id=1, source_target_pairs={{0,8},{1,65},{2,10},{3,67},{4,12},{5,69},{6,14},{7,71},{8,16},{9,7... | collective-permute-start | bytes 393224 | tf_op jit(solution)/shard_map/ppermute | solution.py:34
  49.9 5.6 %collective-permute-start.15 = (bf16[512,128]{1,0:T(8,128)(2,1)S(1)}, bf16[512,128]{1,0:T(8,128)(2,1)S(1)}, u32[]{:S(2)}, u32[]{:S(2)}) collective-permute-start(bf16[512,128]{1,0:T(8,128)(2,1)S(1)} %get-tuple-element.56.first), channel_id=1, source_target_pairs={{0,16},{1,129},{2,18},{3,131},{4,20},{5,133},{6,22},{7,135},{8,24}... | collective-permute-start | bytes 393224 | tf_op jit(solution)/shard_map/ppermute | solution.py:34
  51.7 4.6 %collective-permute-start.14 = (bf16[512,128]{1,0:T(8,128)(2,1)S(1)}, bf16[512,128]{1,0:T(8,128)(2,1)S(1)}, u32[]{:S(2)}, u32[]{:S(2)}) collective-permute-start(bf16[512,128]{1,0:T(8,128)(2,1)S(1)} %get-tuple-element.56.first), channel_id=1, source_target_pairs={{0,24},{1,193},{2,26},{3,195},{4,28},{5,197},{6,30},{7,199},{8,0},... | collective-permute-start | bytes 393224 | tf_op jit(solution)/shard_map/ppermute | solution.py:34
  56.3 9.0 %collective-permute-start.17 = (f32[256,128]{1,0:T(8,128)S(1)}, f32[256,128]{1,0:T(8,128)S(1)}, u32[]{:S(2)}, u32[]{:S(2)}) collective-permute-start(f32[256,128]{1,0:T(8,128)S(1)} %get-tuple-element.57), channel_id=1, source_target_pairs={{0,1},{1,0},{2,3},{3,2},{4,5},{5,4},{6,7},{7,6},{8,9},{9,8},{10,11... | collective-permute-start | bytes 393224 | tf_op jit(solution)/shard_map/ppermute | solution.py:42
  61.0 12.7 %collective-permute-start.21 = (bf16[3,512,128]{2,1,0:T(8,128)(2,1)S(1)}, bf16[3,512,128]{2,1,0:T(8,128)(2,1)S(1)}, u32[]{:S(2)}, u32[]{:S(2)}) collective-permute-start(bf16[3,512,128]{2,1,0:T(8,128)(2,1)S(1)} %pad_maximum_fusion.rest), channel_id=1, source_target_pairs={{0,192},{1,25},{2,194},{3,27},{4,196},{5,29},{6,198},{7,31},{8,200... | collective-permute-start | bytes 1179656 | tf_op jit(solution)/shard_map/ppermute | solution.py:34
  62.3 11.3 %collective-permute-start.19 = (bf16[3,512,128]{2,1,0:T(8,128)(2,1)S(1)}, bf16[3,512,128]{2,1,0:T(8,128)(2,1)S(1)}, u32[]{:S(2)}, u32[]{:S(2)}) collective-permute-start(bf16[3,512,128]{2,1,0:T(8,128)(2,1)S(1)} %pad_maximum_fusion.rest), channel_id=1, source_target_pairs={{0,128},{1,17},{2,130},{3,19},{4,132},{5,21},{6,134},{7,23},{8,136... | collective-permute-start | bytes 1179656 | tf_op jit(solution)/shard_map/ppermute | solution.py:34
  62.4 11.3 %collective-permute-start.20 = (bf16[512,128]{1,0:T(8,128)(2,1)S(1)}, bf16[512,128]{1,0:T(8,128)(2,1)S(1)}, u32[]{:S(2)}, u32[]{:S(2)}) collective-permute-start(bf16[512,128]{1,0:T(8,128)(2,1)S(1)} %get-tuple-element.56.first), channel_id=1, source_target_pairs={{0,192},{1,25},{2,194},{3,27},{4,196},{5,29},{6,198},{7,31},{8,200... | collective-permute-start | bytes 393224 | tf_op jit(solution)/shard_map/ppermute | solution.py:34
  64.9 8.7 %collective-permute-start.18 = (bf16[512,128]{1,0:T(8,128)(2,1)S(1)}, bf16[512,128]{1,0:T(8,128)(2,1)S(1)}, u32[]{:S(2)}, u32[]{:S(2)}) collective-permute-start(bf16[512,128]{1,0:T(8,128)(2,1)S(1)} %get-tuple-element.56.first), channel_id=1, source_target_pairs={{0,128},{1,17},{2,130},{3,19},{4,132},{5,21},{6,134},{7,23},{8,136... | collective-permute-start | bytes 393224 | tf_op jit(solution)/shard_map/ppermute | solution.py:34
  65.3 13.4 %collective-permute-start.23 = (bf16[3,512,128]{2,1,0:T(8,128)(2,1)S(1)}, bf16[3,512,128]{2,1,0:T(8,128)(2,1)S(1)}, u32[]{:S(2)}, u32[]{:S(2)}) collective-permute-start(bf16[3,512,128]{2,1,0:T(8,128)(2,1)S(1)} %pad_maximum_fusion.rest), channel_id=1, source_target_pairs={{0,64},{1,9},{2,66},{3,11},{4,68},{5,13},{6,70},{7,15},{8,72},{9,1... | collective-permute-start | bytes 1179656 | tf_op jit(solution)/shard_map/ppermute | solution.py:34
  73.7 5.0 %collective-permute-start.22 = (bf16[512,128]{1,0:T(8,128)(2,1)S(1)}, bf16[512,128]{1,0:T(8,128)(2,1)S(1)}, u32[]{:S(2)}, u32[]{:S(2)}) collective-permute-start(bf16[512,128]{1,0:T(8,128)(2,1)S(1)} %get-tuple-element.56.first), channel_id=1, source_target_pairs={{0,64},{1,9},{2,66},{3,11},{4,68},{5,13},{6,70},{7,15},{8,72},{9,1... | collective-permute-start | bytes 393224 | tf_op jit(solution)/shard_map/ppermute | solution.py:34
  79.4 4.7 %collective-permute-start.25 = (bf16[2,256,512]{2,1,0:T(8,128)(2,1)S(1)}, bf16[2,256,512]{2,1,0:T(8,128)(2,1)S(1)}, u32[]{:S(2)}, u32[]{:S(2)}) collective-permute-start(bf16[2,256,512]{2,1,0:T(8,128)(2,1)S(1)} %get-tuple-element.66.after), channel_id=1, source_target_pairs={{0,1},{1,0},{2,3},{3,2},{4,5},{5,4},{6,7},{7,6},{8,9},{9,8},{10,11... | collective-permute-start | bytes 1572872 | tf_op jit(solution)/shard_map/ppermute | solution.py:42
  83.4 2.0 %collective-permute-start.24 = (bf16[2,256,512]{2,1,0:T(8,128)(2,1)S(1)}, bf16[2,256,512]{2,1,0:T(8,128)(2,1)S(1)}, u32[]{:S(2)}, u32[]{:S(2)}) collective-permute-start(bf16[2,256,512]{2,1,0:T(8,128)(2,1)S(1)} %get-tuple-element.68), channel_id=1, source_target_pairs={{0,1},{1,0},{2,3},{3,2},{4,5},{5,4},{6,7},{7,6},{8,9},{9,8},{10,11... | collective-permute-start | bytes 1572872 | tf_op jit(solution)/shard_map/ppermute | solution.py:42

commit v2 on v1

--- a/solution.py
+++ b/solution.py
@@ -68,18 +68,20 @@
 
 
 def plan_kernel(table):
-    y, _, x, owner = position()
-    for i, (d, k) in enumerate((d, k) for d in ORDER for k in range(LINE)):
-        dy = k + owner * (d - k)
-        dx = d + owner * (k - d)
-        table[i] = ((y + dy) & 3) * 8 + owner * 4 + ((x + dx) & 3)
+    y, _, x, own = position()
+    for half, owner in enumerate((own, 1 - own)):
+        for i, (d, k) in enumerate((d, k) for d in ORDER for k in range(LINE)):
+            dy = k + owner * (d - k)
+            dx = d + owner * (k - d)
+            at = half * len(ORDER) * LINE + i
+            table[at] = ((y + dy) & 3) * 8 + owner * 4 + ((x + dx) & 3)
 
 
 def plan():
     return pl.pallas_call(
         plan_kernel,
         out_specs=SMEM,
-        out_shape=jax.ShapeDtypeStruct((len(ORDER) * LINE,), jnp.int32),
+        out_shape=jax.ShapeDtypeStruct((2 * len(ORDER) * LINE,), jnp.int32),
         compiler_params=params(4),
         cost_estimate=AHEAD,
         name="plan",
@@ -272,7 +274,7 @@
     return call(turn_kernel, [VMEM] * 2, outs, 1 << 20, 4)(own, received)
 
 
-PARTS = ((0,), (2, 1), (3,))
+GROUPS = (0, *FAR)
 
 
 def spread_kernel(table, starts, tiles, after, *outs):
@@ -280,17 +282,17 @@
     zeros = jnp.zeros((block, block), tiles.dtype)
 
     def angle(a, carry):
-        for out, ds in zip(outs, PARTS):
-            for g, d in enumerate(ds):
-                for k in range(LINE):
-                    j = table[place(d) + k]
-                    first = starts[a, j]
-                    column = slice((g * LINE + k) * block, (g * LINE + k + 1) * block)
-                    for empty in (jnp.where(first == 0, 2, 0), jnp.where(first == 2, 1, 3)):
-                        at = pl.ds(pl.multiple_of(empty * block, block), block)
-                        out[a, at, column] = zeros
-                    at = pl.ds(pl.multiple_of(first * block, block), 2 * block)
-                    out[a, at, column] = tiles[a, j]
+        for out, d in zip(outs, GROUPS):
+            for i in range(2 * LINE):
+                half, k = divmod(i, LINE)
+                j = table[half * len(ORDER) * LINE + place(d) + k]
+                first = starts[a, j]
+                column = slice(i * block, (i + 1) * block)
+                for empty in (jnp.where(first == 0, 2, 0), jnp.where(first == 2, 1, 3)):
+                    at = pl.ds(pl.multiple_of(empty * block, block), block)
+                    out[a, at, column] = zeros
+                at = pl.ds(pl.multiple_of(first * block, block), 2 * block)
+                out[a, at, column] = tiles[a, j]
         return carry
 
     lax.fori_loop(0, tiles.shape[0], angle, 0)
@@ -298,94 +300,83 @@
 
 def spread(tiles, table, starts, detector, after):
     angles, _, _, block = tiles.shape
-    outs = [((angles, detector, len(ds) * LINE * block), tiles.dtype) for ds in PARTS]
+    outs = [((angles, detector, 2 * LINE * block), tiles.dtype)] * len(GROUPS)
     return call(spread_kernel, [SMEM, SMEM, VMEM, ANY], outs, 1 << 31, 16)(
         table, starts, tiles, after
     )
 
 
-def row_of(pieces):
-    blocks = []
-    for first, rest in pieces:
-        blocks += [first[...]] + [rest[k] for k in range(LINE - 1)]
-    return jnp.concatenate(blocks, axis=1)
-
-
-def projected(pieces, weights):
+def cut_kernel(first, rest, out):
+    rows = out.shape[1]
+    out[0] = first[rows:, :]
+    for k in range(1, LINE):
+        out[k] = rest[k - 1, rows:, :]
+
+
+def cut(first, rest):
+    rows, block = first.shape
+    outs = [((LINE, rows // 2, block), first.dtype)]
+    return call(cut_kernel, [VMEM] * 2, outs, 1 << 18, 4)(first, rest)[0]
+
+
+def own_blocks(first, rest):
+    rows = first.shape[0] // 2
+    return [first[:rows, :]] + [rest[k, :rows, :] for k in range(LINE - 1)]
+
+
+def projected(blocks, weights):
+    row = jnp.concatenate(blocks, axis=1)
     return lax.dot_general(
-        row_of(pieces), weights, (((1,), (1,)), ((), ())), preferred_element_type=jnp.float32
-    )
-
-
-def near_kernel(weights, first, rest, image):
+        row, weights, (((1,), (1,)), ((), ())), preferred_element_type=jnp.float32
+    )
+
+
+def image_kernel(chained, whole, weights, first, rest, *refs):
+    *refs, after, image = refs
+    blocks = own_blocks(first, rest)
+    if whole:
+        blocks += [refs[0][k] for k in range(LINE)]
+    depth = sum(block.shape[1] for block in blocks)
     for a in range(image.shape[0]):
-        image[a] = projected(((first, rest),), weights[a])
-
-
-def near(piece, weights):
+        value = projected(blocks, weights[a, :, :depth])
+        image[a] = refs[-1][a] + value if chained else value
+
+
+def imaged(weights, piece, got, before, after):
     angles, detector, _ = weights.shape
-    rows = piece[0].shape[0]
+    rows = piece[0].shape[0] // 2
+    more = [v for v in (got, before) if v is not None]
     outs = [((angles, rows, detector), jnp.float32)]
-    flops = 2 * weights.size * rows
-    return call(near_kernel, [VMEM] * 3, outs, flops, 16)(weights, *piece)[0]
-
-
-def next_kernel(weights, before, f1, r1, f2, r2, after, image):
+    flops = weights.size * rows * (1 if got is None else 2)
+    kernel = functools.partial(image_kernel, before is not None, got is not None)
+    specs = [VMEM] * (3 + len(more)) + [ANY]
+    return call(kernel, specs, outs, flops)(weights, *piece, *more, after)[0]
+
+
+def leave_kernel(weights, got, before, out, image, done):
+    blocks = [got[k] for k in range(LINE)]
+    depth = sum(block.shape[1] for block in blocks)
+    copies = []
     for a in range(image.shape[0]):
-        image[a] = before[a] + projected(((f1, r1), (f2, r2)), weights[a])
-
-
-def further(pieces, weights, before, after):
-    outs = [(before.shape, jnp.float32)]
-    flops = 2 * weights.size * before.shape[1]
-    return call(next_kernel, [VMEM] * 6 + [ANY], outs, flops, 16)(
-        weights, before, *pieces[0], *pieces[1], after
-    )[0]
-
-
-def last_kernel(base, weights, before, first, rest, after, own, message):
-    rows = own.shape[1]
-    for i in range(own.shape[0]):
-        value = before[base + i] + projected(((first, rest),), weights[base + i])
-        own[i] = value[:rows]
-        message[i] = value[rows:].astype(message.dtype)
-
-
-def last(piece, weights, before, base, count, after):
-    _, rows, detector = before.shape
-    shape = (count, rows // 2, detector)
-    outs = [(shape, jnp.float32), (shape, jnp.bfloat16)]
-    flops = weights.size * rows
-    kernel = functools.partial(last_kernel, base)
-    return call(kernel, [VMEM] * 4 + [ANY], outs, flops, 16)(
-        weights, before, *piece, after
-    )
-
-
-def leave_kernel(base, own, got, *refs):
-    out, image, done = refs[-3:]
-    copies = []
-    for i in range(own.shape[0]):
-        image[i] = own[i] + got[i].astype(jnp.float32)
-        copies.append(pltpu.make_async_copy(image.at[i], out.at[base + i], done.at[i]))
+        image[a] = before[a] + projected(blocks, weights[a, :, depth:])
+        copies.append(pltpu.make_async_copy(image.at[a], out.at[a], done.at[a]))
         copies[-1].start()
     for copy in copies:
         copy.wait()
 
 
-def leave(own, got, base, shape, held=None):
-    half = own.shape[0]
+def leave(weights, got, before):
+    shape = before.shape
     return pl.pallas_call(
-        functools.partial(leave_kernel, base),
-        in_specs=[VMEM] * 2 + [ANY] * (held is not None),
+        leave_kernel,
+        in_specs=[VMEM] * 3,
         out_specs=ANY,
         out_shape=jax.ShapeDtypeStruct(shape, jnp.float32),
-        scratch_shapes=[pltpu.VMEM(own.shape, jnp.float32), pltpu.SemaphoreType.DMA((half,))],
-        input_output_aliases={} if held is None else {2: 0},
+        scratch_shapes=[pltpu.VMEM(shape, jnp.float32), pltpu.SemaphoreType.DMA((shape[0],))],
         compiler_params=params(16),
-        cost_estimate=pl.CostEstimate(flops=1 << 20, bytes_accessed=1 << 20, transcendentals=0),
+        cost_estimate=pl.CostEstimate(flops=1 << 28, bytes_accessed=1 << 20, transcendentals=0),
         name="leave",
-    )(own, got, *([] if held is None else [held]))
+    )(weights, got, before)
 
 
 def steps(updates, tiles, starts, ids, weights, volume):
@@ -417,7 +408,7 @@
     beside = swapped(smooth)
     mine, message = merged(smooth, beside, own[0], first, reached)
     crossed = across(message)
-    bands = spread(tiles, table, starts, detector, message)
+    bands = dict(zip(GROUPS, spread(tiles, table, starts, detector, message)))
     own, beside, lowered = finished(mine, crossed)
 
     came, first = {}, {}
@@ -434,19 +425,14 @@
         rest[d] = moved(line, True, LINE - d)
     received = swapped(beside)
     volume_next, token = turned(own, received, volume.shape)
-    image = near((lowered, line), bands[0])
-    image = further(
-        [(first[2], rest[2]), (first[1], rest[1])], bands[1], image, token
-    )
-    half = angles // 2
-    piece = first[3], rest[3]
-    own0, message0 = last(piece, bands[2], image, 0, half, image)
-    got0 = swapped(message0)
-    own1, message1 = last(piece, bands[2], image, half, half, message0)
-    got1 = swapped(message1)
-    shape = (angles, 2 * depth, detector)
-    projection = leave(own0, got0, 0, shape)
-    projection = leave(own1, got1, half, shape, projection)
+    first[0], rest[0] = lowered, line
+    image, last = None, token
+    for d in GROUPS:
+        piece = first[d], rest[d]
+        got = swapped(cut(*piece))
+        image = imaged(bands[d], piece, None if d == FAR[-1] else got, image, last)
+        last = image
+    projection = leave(bands[FAR[-1]], got, image)
     return volume_next, projection.reshape(angles, 2, depth, detector)
 
 

time: 86.7 us -> 98.2 us (1.13)
  starting transfers between devices: 44.9 us -> 56 us
  Pallas kernels: 20.6 us -> 22.2 us
  waiting for transfers between devices: 19 us -> 17.8 us
    ppermute x6 -> x8, starting transfers between devices: 13.1 us -> 23 us  [swapped(): return lax.ppermute(value, 'slab', [(i, i ^ 1) for i in range(SLABS)])]
    pallas_call x1, Pallas kernels: 2.63 us -> 4.99 us  [spread(): call(spread_kernel, [SMEM, SMEM, VMEM, ANY], outs, 1 << 31, 16)]
    ppermute x18, starting transfers between devices: 21.4 us -> 22.6 us  [moved(): return lax.ppermute(value, ('ang', 'slab'), pairs)]
    pallas_call x6 -> x9, Pallas kernels: 7.27 us -> 6.43 us  [the longest x4 4.67 us: imaged(): return call(kernel, specs, outs, flops)(weights, *piece, *more, after)[0]]
  transfers between devices with their start and end apart: 26 -> 28, of which waited for: 12 -> 10; matrix products, arithmetic and copies ran while one was open for 0% -> 0% of each run, Pallas kernels for 17% -> 15%
where the time goes in v2:
time: 98.2 us; the launch traced here: 98.1 us
  starting transfers between devices  56 us (57%)
  Pallas kernels  22.2 us (23%)
  waiting for transfers between devices  17.8 us (18%)
  between operations  1.13 us (1%)
    ppermute x8, starting transfers between devices, swapped(): return lax.ppermute(value, 'slab', [(i, i ^ 1) for i in range(SLABS)])  23 us
    ppermute x18, starting transfers between devices, moved(): return lax.ppermute(value, ('ang', 'slab'), pairs)  22.6 us
    ppermute x18, waiting for transfers between devices, moved(): return lax.ppermute(value, ('ang', 'slab'), pairs)  13.2 us
    ppermute x1, starting transfers between devices, across(): lax.ppermute(value, 'ang', [(a, a ^ XS) for a in range(YS * ZS * XS)])  6.97 us
    pallas_call x1, Pallas kernels, spread(): call(spread_kernel, [SMEM, SMEM, VMEM, ANY], outs, 1 << 31, 16)  4.99 us
    pallas_call x4, Pallas kernels, imaged(): return call(kernel, specs, outs, flops)(weights, *piece, *more, after)[0]  4.67 us
    pallas_call x2, Pallas kernels, both_rows(): call(kernel, specs, outs, flops)(table, starts, scaled, other, tiles, after)  3.66 us
    ppermute x1, starting transfers between devices, steps(): lax.ppermute(outer, 'slab', [p for i in odd for p in ((i, i + 1), (i + 1,...  3.44 us
  transfers between devices with their start and end apart: 28, of which 10 were waited for; matrix products, arithmetic and copies ran while one was open for 0% of the time, Pallas kernels for 15%

profile of v2, /device:TPU:1, one launch (start us, length us, event | category | flops | bytes accessed | tf_op | source)
XLA Modules:
  0.0 98.1 jit_solution(16022134341604315698)
XLA Ops:
  0.7 0.7 plan.1.table
  1.4 0.9 copy-done.2
  2.2 0.7 shard_map.77.after.scaled
  2.9 3.3 %collective-permute-start.3 = (bf16[4,256,512]{2,1,0:T(8,128)(2,1)S(1)}, bf16[4,256,512]{2,1,0:T(8,128)(2,1)S(1)}, u32[]{:S(2)}, u32[]{:S(2)}) collective-permute-start(bf16[4,256,512]{2,1,0:T(8,128)(2,1)S(1)} %shard_map.77.after.scaled), channel_id=1, source_target_pairs={{0,1},{1,0},{2,3},{3,2},{4,5},{5,4},{6,7},{7,6},{8,9},{9,8},{10,11... | collective-permute-start | bytes 3145736 | tf_op jit(solution)/shard_map/ppermute | solution.py:42
  6.2 1.8 %shard_map.80 = (bf16[4,256,128]{2,1,0:T(8,128)(2,1)S(1)}, bf16[4,256,128]{2,1,0:T(8,128)(2,1)S(1)}) custom-call(s32[32]{0:T(128)S(1)} %plan.1.table, s32[4,32]{1,0:T(4,128)S(1)} %copy-done.1, bf16[4,256,512]{2,1,0:T(8,128)(2,1)S(1)} %shard_map.77.after.scaled, bf16[4,32,256,128]{3,2,1,0:T(8,128)(2,1)S(1)} %bitcast.5), custom_call_target="tpu_custom_call" | custom-call | flops 536870912 | bytes 1048576 | tf_op jit(solution)/shard_map/pallas_call | solution.py:153
  8.1 0.4 collective-permute-done.3.other
  8.5 1.3 %shard_map.81 = (bf16[512,128]{1,0:T(8,128)(2,1)S(1)}, bf16[3,512,128]{2,1,0:T(8,128)(2,1)S(1)}) custom-call(s32[32]{0:T(128)S(1)} %plan.1.table, s32[4,32]{1,0:T(4,128)S(1)} %copy-done.1, bf16[4,256,512]{2,1,0:T(8,128)(2,1)S(1)} %collective-permute-done.3.other, bf16[4,32,256,128]{3,2,1,0:T(8,128)(2,1)S(1)} %bitcast.5, ...), custom_call_target="tpu_custom_call" | custom-call | flops 268435456 | bytes 1048576 | tf_op jit(solution)/shard_map/pallas_call | solution.py:174
  9.8 1.3 %shard_map.82 = (bf16[512,128]{1,0:T(8,128)(2,1)S(1)}, bf16[3,512,128]{2,1,0:T(8,128)(2,1)S(1)}) custom-call(s32[32]{0:T(128)S(1)} %plan.1.table, s32[4,32]{1,0:T(4,128)S(1)} %copy-done.1, bf16[4,256,512]{2,1,0:T(8,128)(2,1)S(1)} %collective-permute-done.3.other, bf16[4,32,256,128]{3,2,1,0:T(8,128)(2,1)S(1)} %bitcast.5, ...), custom_call_target="tpu_custom_call" | custom-call | flops 268435456 | bytes 1048576 | tf_op jit(solution)/shard_map/pallas_call | solution.py:174
  11.1 1.8 %shard_map.83 = (bf16[512,128]{1,0:T(8,128)(2,1)S(1)}, bf16[3,512,128]{2,1,0:T(8,128)(2,1)S(1)}) custom-call(s32[32]{0:T(128)S(1)} %plan.1.table, s32[4,32]{1,0:T(4,128)S(1)} %copy-done.1, bf16[4,256,512]{2,1,0:T(8,128)(2,1)S(1)} %shard_map.77.after.scaled, bf16[4,256,512]{2,1,0:T(8,128)(2,1)S(1)} %collective-permute-done.3.other, ...), custom_call_target="tpu_custom_call" | custom-call | flops 536870912 | bytes 1048576 | tf_op jit(solution)/shard_map/pallas_call | solution.py:191
  12.9 1.7 %collective-permute-start.9 = (bf16[3,512,128]{2,1,0:T(8,128)(2,1)S(1)}, bf16[3,512,128]{2,1,0:T(8,128)(2,1)S(1)}, u32[]{:S(2)}, u32[]{:S(2)}) collective-permute-start(bf16[3,512,128]{2,1,0:T(8,128)(2,1)S(1)} %get-tuple-element.45), channel_id=1, source_target_pairs={{0,192},{1,25},{2,194},{3,27},{4,196},{5,29},{6,198},{7,31},{8,200... | collective-permute-start | bytes 1179656 | tf_op jit(solution)/shard_map/ppermute | solution.py:34
  14.6 1.7 %collective-permute-start.7 = (bf16[3,512,128]{2,1,0:T(8,128)(2,1)S(1)}, bf16[3,512,128]{2,1,0:T(8,128)(2,1)S(1)}, u32[]{:S(2)}, u32[]{:S(2)}) collective-permute-start(bf16[3,512,128]{2,1,0:T(8,128)(2,1)S(1)} %get-tuple-element.43), channel_id=1, source_target_pairs={{0,128},{1,17},{2,130},{3,19},{4,132},{5,21},{6,134},{7,23},{8,136... | collective-permute-start | bytes 1179656 | tf_op jit(solution)/shard_map/ppermute | solution.py:34
  16.3 0.1 shard_map.78
  16.5 1.8 %collective-permute-start = (f32[2,128]{1,0:T(2,128)S(1)}, f32[2,128]{1,0:T(2,128)S(1)}, u32[]{:S(2)}, u32[]{:S(2)}) collective-permute-start(f32[2,128]{1,0:T(2,128)S(1)} %get-tuple-element.34), channel_id=1, source_target_pairs={{0,1},{1,0},{2,3},{3,2},{4,5},{5,4},{6,7},{7,6},{8,9},{9,8},{10,11... | collective-permute-start | bytes 3080 | tf_op jit(solution)/shard_map/ppermute | solution.py:42
  18.2 3.4 %collective-permute-start.1 = (f32[2,128]{1,0:T(2,128)S(1)}, f32[2,128]{1,0:T(2,128)S(1)}, u32[]{:S(2)}, u32[]{:S(2)}) collective-permute-start(f32[2,128]{1,0:T(2,128)S(1)} %get-tuple-element.35), channel_id=1, source_target_pairs={{1,2},{2,1},{3,4},{4,3},{5,6},{6,5},{9,10},{10,9},{11,12},{12,11},... | collective-permute-start | bytes 3080 | tf_op jit(solution)/shard_map/ppermute | solution.py:391
  21.7 1.7 %collective-permute-done.1.outer = f32[2,128]{1,0:T(2,128)S(1)} collective-permute-done((f32[2,128]{1,0:T(2,128)S(1)}, f32[2,128]{1,0:T(2,128)S(1)}, u32[]{:S(2)}, u32[]{:S(2)}) %collective-permute-start.1) | collective-permute-done | bytes 1056 | tf_op jit(solution)/shard_map/ppermute | solution.py:391
  23.5 2.6 %collective-permute-start.6 = (bf16[512,128]{1,0:T(8,128)(2,1)S(1)}, bf16[512,128]{1,0:T(8,128)(2,1)S(1)}, u32[]{:S(2)}, u32[]{:S(2)}) collective-permute-start(bf16[512,128]{1,0:T(8,128)(2,1)S(1)} %get-tuple-element.40.after), channel_id=1, source_target_pairs={{0,192},{1,25},{2,194},{3,27},{4,196},{5,29},{6,198},{7,31},{8,200... | collective-permute-start | bytes 393224 | tf_op jit(solution)/shard_map/ppermute | solution.py:34
  26.1 1.8 %shard_map.84 = (f32[512,128]{1,0:T(8,128)S(1)}, f32[3,512,128]{2,1,0:T(8,128)S(1)}) custom-call(s32[32]{0:T(128)S(1)} %plan.1.table, s32[4,32]{1,0:T(4,128)S(1)} %copy-done.1, bf16[4,256,512]{2,1,0:T(8,128)(2,1)S(1)} %shard_map.77.after.scaled, bf16[4,256,512]{2,1,0:T(8,128)(2,1)S(1)} %collective-permute-done.3.other, ...), custom_call_target="tpu_custom_call" | custom-call | flops 536870912 | bytes 1048576 | tf_op jit(solution)/shard_map/pallas_call | solution.py:191
  28.1 1.7 %collective-permute-start.4 = (bf16[512,128]{1,0:T(8,128)(2,1)S(1)}, bf16[512,128]{1,0:T(8,128)(2,1)S(1)}, u32[]{:S(2)}, u32[]{:S(2)}) collective-permute-start(bf16[512,128]{1,0:T(8,128)(2,1)S(1)} %get-tuple-element.38.after), channel_id=1, source_target_pairs={{0,128},{1,17},{2,130},{3,19},{4,132},{5,21},{6,134},{7,23},{8,136... | collective-permute-start | bytes 393224 | tf_op jit(solution)/shard_map/ppermute | solution.py:34
  29.8 0.2 shard_map.85
  29.9 1.2 %collective-permute-start.10 = (bf16[512,128]{1,0:T(8,128)(2,1)S(1)}, bf16[512,128]{1,0:T(8,128)(2,1)S(1)}, u32[]{:S(2)}, u32[]{:S(2)}) collective-permute-start(bf16[512,128]{1,0:T(8,128)(2,1)S(1)} %get-tuple-element.46), channel_id=1, source_target_pairs={{0,16},{1,129},{2,18},{3,131},{4,20},{5,133},{6,22},{7,135},{8,24}... | collective-permute-start | bytes 393224 | tf_op jit(solution)/shard_map/ppermute | solution.py:34
  31.2 0.6 collective-permute-start.11
  31.8 2.6 %collective-permute-start.12 = (bf16[512,128]{1,0:T(8,128)(2,1)S(1)}, bf16[512,128]{1,0:T(8,128)(2,1)S(1)}, u32[]{:S(2)}, u32[]{:S(2)}) collective-permute-start(bf16[512,128]{1,0:T(8,128)(2,1)S(1)} %get-tuple-element.48), channel_id=1, source_target_pairs={{0,24},{1,193},{2,26},{3,195},{4,28},{5,197},{6,30},{7,199},{8,0},... | collective-permute-start | bytes 393224 | tf_op jit(solution)/shard_map/ppermute | solution.py:34
  34.3 0.4 collective-permute-done.5.a2
  34.8 1.6 %collective-permute-done.10.s1 = bf16[512,128]{1,0:T(8,128)(2,1)S(1)} collective-permute-done((bf16[512,128]{1,0:T(8,128)(2,1)S(1)}, bf16[512,128]{1,0:T(8,128)(2,1)S(1)}, u32[]{:S(2)}, u32[]{:S(2)}) %collective-permute-start.10) | collective-permute-done | bytes 131104 | tf_op jit(solution)/shard_map/ppermute | solution.py:34
  36.4 1.2 %collective-permute-done.11.s2 = bf16[512,128]{1,0:T(8,128)(2,1)S(1)} collective-permute-done((bf16[512,128]{1,0:T(8,128)(2,1)S(1)}, bf16[512,128]{1,0:T(8,128)(2,1)S(1)}, u32[]{:S(2)}, u32[]{:S(2)}) %collective-permute-start.11) | collective-permute-done | bytes 131104 | tf_op jit(solution)/shard_map/ppermute | solution.py:34
  37.6 0.1 shard_map.86
  37.7 7.0 %collective-permute-start.13 = (bf16[512,128]{1,0:T(8,128)(2,1)S(1)}, bf16[512,128]{1,0:T(8,128)(2,1)S(1)}, u32[]{:S(2)}, u32[]{:S(2)}) collective-permute-start(bf16[512,128]{1,0:T(8,128)(2,1)S(1)} %get-tuple-element.50.after), channel_id=1, source_target_pairs={{0,32},{8,40},{16,48},{24,56},{32,0},{40,8},{48,16},{56,24},{64,96... | collective-permute-start | bytes 393224 | tf_op jit(solution)/shard_map/ppermute | solution.py:38
  44.7 2.5 %collective-permute-done.13.crossed = bf16[512,128]{1,0:T(8,128)(2,1)S(1)} collective-permute-done((bf16[512,128]{1,0:T(8,128)(2,1)S(1)}, bf16[512,128]{1,0:T(8,128)(2,1)S(1)}, u32[]{:S(2)}, u32[]{:S(2)}) %collective-permute-start.13) | collective-permute-done | bytes 131104 | tf_op jit(solution)/shard_map/ppermute | solution.py:38
  47.2 1.8 %collective-permute-start.14 = (bf16[512,128]{1,0:T(8,128)(2,1)S(1)}, bf16[512,128]{1,0:T(8,128)(2,1)S(1)}, u32[]{:S(2)}, u32[]{:S(2)}) collective-permute-start(bf16[512,128]{1,0:T(8,128)(2,1)S(1)} %get-tuple-element.53.first), channel_id=1, source_target_pairs={{0,24},{1,193},{2,26},{3,195},{4,28},{5,197},{6,30},{7,199},{8,0},... | collective-permute-start | bytes 393224 | tf_op jit(solution)/shard_map/ppermute | solution.py:34
  49.0 1.1 %collective-permute-start.15 = (bf16[512,128]{1,0:T(8,128)(2,1)S(1)}, bf16[512,128]{1,0:T(8,128)(2,1)S(1)}, u32[]{:S(2)}, u32[]{:S(2)}) collective-permute-start(bf16[512,128]{1,0:T(8,128)(2,1)S(1)} %get-tuple-element.53.first), channel_id=1, source_target_pairs={{0,16},{1,129},{2,18},{3,131},{4,20},{5,133},{6,22},{7,135},{8,24}... | collective-permute-start | bytes 393224 | tf_op jit(solution)/shard_map/ppermute | solution.py:34
  50.2 2.2 %collective-permute-done.14 = bf16[512,128]{1,0:T(8,128)(2,1)S(1)} collective-permute-done((bf16[512,128]{1,0:T(8,128)(2,1)S(1)}, bf16[512,128]{1,0:T(8,128)(2,1)S(1)}, u32[]{:S(2)}, u32[]{:S(2)}) %collective-permute-start.14) | collective-permute-done | bytes 131104 | tf_op jit(solution)/shard_map/ppermute | solution.py:34
  52.4 2.1 %collective-permute-done.15 = bf16[512,128]{1,0:T(8,128)(2,1)S(1)} collective-permute-done((bf16[512,128]{1,0:T(8,128)(2,1)S(1)}, bf16[512,128]{1,0:T(8,128)(2,1)S(1)}, u32[]{:S(2)}, u32[]{:S(2)}) %collective-permute-start.15) | collective-permute-done | bytes 131104 | tf_op jit(solution)/shard_map/ppermute | solution.py:34
  54.4 1.3 %collective-permute-done.16 = bf16[512,128]{1,0:T(8,128)(2,1)S(1)} collective-permute-done((bf16[512,128]{1,0:T(8,128)(2,1)S(1)}, bf16[512,128]{1,0:T(8,128)(2,1)S(1)}, u32[]{:S(2)}, u32[]{:S(2)}) %collective-permute-start.16) | collective-permute-done | bytes 131104 | tf_op jit(solution)/shard_map/ppermute | solution.py:34
  55.8 2.7 %collective-permute-start.25 = (bf16[3,512,128]{2,1,0:T(8,128)(2,1)S(1)}, bf16[3,512,128]{2,1,0:T(8,128)(2,1)S(1)}, u32[]{:S(2)}, u32[]{:S(2)}) collective-permute-start(bf16[3,512,128]{2,1,0:T(8,128)(2,1)S(1)} %pad_maximum_fusion.rest), channel_id=1, source_target_pairs={{0,128},{1,17},{2,130},{3,19},{4,132},{5,21},{6,134},{7,23},{8,136... | collective-permute-start | bytes 1179656 | tf_op jit(solution)/shard_map/ppermute | solution.py:34
  58.5 2.1 %collective-permute-start.22 = (bf16[3,512,128]{2,1,0:T(8,128)(2,1)S(1)}, bf16[3,512,128]{2,1,0:T(8,128)(2,1)S(1)}, u32[]{:S(2)}, u32[]{:S(2)}) collective-permute-start(bf16[3,512,128]{2,1,0:T(8,128)(2,1)S(1)} %pad_maximum_fusion.rest), channel_id=1, source_target_pairs={{0,192},{1,25},{2,194},{3,27},{4,196},{5,29},{6,198},{7,31},{8,200... | collective-permute-start | bytes 1179656 | tf_op jit(solution)/shard_map/ppermute | solution.py:34
  60.6 0.6 collective-permute-start.19
  61.2 2.1 %collective-permute-start.21 = (bf16[512,128]{1,0:T(8,128)(2,1)S(1)}, bf16[512,128]{1,0:T(8,128)(2,1)S(1)}, u32[]{:S(2)}, u32[]{:S(2)}) collective-permute-start(bf16[512,128]{1,0:T(8,128)(2,1)S(1)} %get-tuple-element.53.first), channel_id=1, source_target_pairs={{0,192},{1,25},{2,194},{3,27},{4,196},{5,29},{6,198},{7,31},{8,200... | collective-permute-start | bytes 393224 | tf_op jit(solution)/shard_map/ppermute | solution.py:34
  63.3 4.3 %collective-permute-done.24.first = bf16[512,128]{1,0:T(8,128)(2,1)S(1)} collective-permute-done((bf16[512,128]{1,0:T(8,128)(2,1)S(1)}, bf16[512,128]{1,0:T(8,128)(2,1)S(1)}, u32[]{:S(2)}, u32[]{:S(2)}) %collective-permute-start.24) | collective-permute-done | bytes 131104 | tf_op jit(solution)/shard_map/ppermute | solution.py:34
  67.6 10.0 %collective-permute-start.17 = (f32[256,128]{1,0:T(8,128)S(1)}, f32[256,128]{1,0:T(8,128)S(1)}, u32[]{:S(2)}, u32[]{:S(2)}) collective-permute-start(f32[256,128]{1,0:T(8,128)S(1)} %get-tuple-element.54), channel_id=1, source_target_pairs={{0,1},{1,0},{2,3},{3,2},{4,5},{5,4},{6,7},{7,6},{8,9},{9,8},{10,11... | collective-permute-start | bytes 393224 | tf_op jit(solution)/shard_map/ppermute | solution.py:42
  77.8 6.9 %collective-permute-start.26 = (bf16[4,256,128]{2,1,0:T(8,128)(2,1)S(1)}, bf16[4,256,128]{2,1,0:T(8,128)(2,1)S(1)}, u32[]{:S(2)}, u32[]{:S(2)}) collective-permute-start(bf16[4,256,128]{2,1,0:T(8,128)(2,1)S(1)} %shard_map.92), channel_id=1, source_target_pairs={{0,1},{1,0},{2,3},{3,2},{4,5},{5,4},{6,7},{7,6},{8,9},{9,8},{10,11... | collective-permute-start | bytes 786440 | tf_op jit(solution)/shard_map/ppermute | solution.py:42
  84.9 5.0 %shard_map.89 = (bf16[4,512,1024]{2,1,0:T(8,128)(2,1)S(1)}, bf16[4,512,1024]{2,1,0:T(8,128)(2,1)S(1)}, bf16[4,512,1024]{2,1,0:T(8,128)(2,1)S(1)}, bf16[4,512,1024]{2,1,0:T(8,128)(2,1)S(1)}) custom-call(s32[32]{0:T(128)S(1)} %plan.1.table, s32[4,32]{1,0:T(4,128)S(1)} %copy-done.1, bf16[4,32,256,128]{3,2,1,0:T(8,128)(2,1)S(1)} %bitcast.5, ...), custom_call_target="tpu_custom_call" | custom-call | flops 2147483648 | bytes 1048576 | tf_op jit(solution)/shard_map/pallas_call | solution.py:304
  89.9 0.8 shard_map.88
  90.7 0.8 collective-permute-start.20
  91.5 1.3 %shard_map.94.refs_1_.refs_2_ = f32[4,256,512]{2,1,0:T(8,128)S(1)} custom-call(bf16[4,512,1024]{2,1,0:T(8,128)(2,1)S(1)} %get-tuple-element.62.weights, bf16[512,128]{1,0:T(8,128)(2,1)S(1)} %get-tuple-element.53.first, bf16[3,512,128]{2,1,0:T(8,128)(2,1)S(1)} %pad_maximum_fusion.rest, bf16[4,256,128]{2,1,0:T(8,128)(2,1)S(1)} %collective-permute-done.27.refs_0_, ...), custom_call_target="tpu_custom_call" | custom-call | flops 1073741824 | bytes 1048576 | tf_op jit(solution)/shard_map/pallas_call | solution.py:353
  92.8 1.3 %shard_map.95.refs_1_.refs_2_ = f32[4,256,512]{2,1,0:T(8,128)S(1)} custom-call(bf16[4,512,1024]{2,1,0:T(8,128)(2,1)S(1)} %get-tuple-element.61.weights, bf16[512,128]{1,0:T(8,128)(2,1)S(1)} %collective-permute-done.24.first, bf16[3,512,128]{2,1,0:T(8,128)(2,1)S(1)} %collective-permute-done.25.rest, bf16[4,256,128]{2,1,0:T(8,128)(2,1)S(1)} %collective-permute-done.26.refs_0_, ...), custom_call_target="tpu_custom_call" | custom-call | flops 1073741824 | bytes 1048576 | tf_op jit(solution)/shard_map/pallas_call | solution.py:353
  94.1 1.3 %shard_map.96.refs_0_.refs_1_ = f32[4,256,512]{2,1,0:T(8,128)S(1)} custom-call(bf16[4,512,1024]{2,1,0:T(8,128)(2,1)S(1)} %get-tuple-element.60.weights, bf16[512,128]{1,0:T(8,128)(2,1)S(1)} %collective-permute-done.21.first, bf16[3,512,128]{2,1,0:T(8,128)(2,1)S(1)} %collective-permute-done.22.rest, bf16[4,256,128]{2,1,0:T(8,128)(2,1)S(1)} %collective-permute-done.23.refs_0_, ...), custom_call_target="tpu_custom_call" | custom-call | flops 1073741824 | bytes 1048576 | tf_op jit(solution)/shard_map/pallas_call | solution.py:353
  95.4 0.8 shard_map.97.before
  96.2 1.7 %leave.1 = f32[4,256,512]{2,1,0:T(8,128)} custom-call(bf16[4,512,1024]{2,1,0:T(8,128)(2,1)S(1)} %get-tuple-element.56.weights, bf16[4,256,128]{2,1,0:T(8,128)(2,1)S(1)} %collective-permute-done.20.got, f32[4,256,512]{2,1,0:T(8,128)S(1)} %shard_map.97.before), custom_call_target="tpu_custom_call" | custom-call | flops 268435456 | bytes 1048576 | tf_op jit(solution)/shard_map/leave/pallas_call | solution.py:370
  (47 shorter events, 0.7 us)
Async XLA Ops:
  0.6 0.7 copy-start.4
  0.6 1.6 %copy-start.2 = (f32[4,2,128,512]{3,2,1,0:T(8,128)S(1)}, f32[4,2,128,512]{3,2,1,0:T(8,128)}, u32[]{:S(2)}) copy-start(f32[4,2,128,512]{3,2,1,0:T(8,128)} %updates.1) | copy-start | bytes 6291460
  0.6 1.6 %copy-start.3 = (s32[4]{0:T(128)S(1)}, s32[4]{0:T(128)}, u32[]{:S(2)}) copy-start(s32[4]{0:T(128)} %ids.1) | copy-start | bytes 52
  0.7 5.5 %slice-start = ((s8[8388608]{0:T(1024)(128)(4,1)}), s8[4194304]{0:T(1024)(128)(4,1)S(1)}, s32[]{:S(2)}) async-start(s8[8388608]{0:T(1024)(128)(4,1)} %bitcast.4), calls=%async_computation | async-start | bytes 8388608
  2.2 4.0 %slice-start.1 = ((s8[8388608]{0:T(1024)(128)(4,1)}), s8[4194304]{0:T(1024)(128)(4,1)S(1)}, s32[]{:S(2)}) async-start(s8[8388608]{0:T(1024)(128)(4,1)} %bitcast.4), calls=%async_computation.1 | async-start | bytes 8388608
  2.2 4.0 %copy-start.1 = (s32[4,32]{1,0:T(4,128)S(1)}, s32[4,32]{1,0:T(4,128)}, u32[]{:S(2)}) copy-start(s32[4,32]{1,0:T(4,128)} %starts.11) | copy-start | bytes 1540
  2.9 5.6 %collective-permute-start.3 = (bf16[4,256,512]{2,1,0:T(8,128)(2,1)S(1)}, bf16[4,256,512]{2,1,0:T(8,128)(2,1)S(1)}, u32[]{:S(2)}, u32[]{:S(2)}) collective-permute-start(bf16[4,256,512]{2,1,0:T(8,128)(2,1)S(1)} %shard_map.77.after.scaled), channel_id=1, source_target_pairs={{0,1},{1,0},{2,3},{3,2},{4,5},{5,4},{6,7},{7,6},{8,9},{9,8},{10,11... | collective-permute-start | bytes 3145736 | tf_op jit(solution)/shard_map/ppermute | solution.py:42
  11.1 5.2 %copy-start = (f32[128,2,128]{2,1,0:T(2,128)S(1)}, f32[128,2,128]{2,1,0:T(2,128)}, u32[]{:S(2)}) copy-start(f32[128,2,128]{2,1,0:T(2,128)} %volume.1) | copy-start | bytes 393220
  12.9 15.0 %collective-permute-start.9 = (bf16[3,512,128]{2,1,0:T(8,128)(2,1)S(1)}, bf16[3,512,128]{2,1,0:T(8,128)(2,1)S(1)}, u32[]{:S(2)}, u32[]{:S(2)}) collective-permute-start(bf16[3,512,128]{2,1,0:T(8,128)(2,1)S(1)} %get-tuple-element.45), channel_id=1, source_target_pairs={{0,192},{1,25},{2,194},{3,27},{4,196},{5,29},{6,198},{7,31},{8,200... | collective-permute-start | bytes 1179656 | tf_op jit(solution)/shard_map/ppermute | solution.py:34
  14.6 13.5 %collective-permute-start.8 = (bf16[3,512,128]{2,1,0:T(8,128)(2,1)S(1)}, bf16[3,512,128]{2,1,0:T(8,128)(2,1)S(1)}, u32[]{:S(2)}, u32[]{:S(2)}) collective-permute-start(bf16[3,512,128]{2,1,0:T(8,128)(2,1)S(1)} %get-tuple-element.44), channel_id=1, source_target_pairs={{0,64},{1,9},{2,66},{3,11},{4,68},{5,13},{6,70},{7,15},{8,72},{9,1... | collective-permute-start | bytes 1179656 | tf_op jit(solution)/shard_map/ppermute | solution.py:34
  14.6 15.2 %collective-permute-start.7 = (bf16[3,512,128]{2,1,0:T(8,128)(2,1)S(1)}, bf16[3,512,128]{2,1,0:T(8,128)(2,1)S(1)}, u32[]{:S(2)}, u32[]{:S(2)}) collective-permute-start(bf16[3,512,128]{2,1,0:T(8,128)(2,1)S(1)} %get-tuple-element.43), channel_id=1, source_target_pairs={{0,128},{1,17},{2,130},{3,19},{4,132},{5,21},{6,134},{7,23},{8,136... | collective-permute-start | bytes 1179656 | tf_op jit(solution)/shard_map/ppermute | solution.py:34
  16.5 5.2 %collective-permute-start = (f32[2,128]{1,0:T(2,128)S(1)}, f32[2,128]{1,0:T(2,128)S(1)}, u32[]{:S(2)}, u32[]{:S(2)}) collective-permute-start(f32[2,128]{1,0:T(2,128)S(1)} %get-tuple-element.34), channel_id=1, source_target_pairs={{0,1},{1,0},{2,3},{3,2},{4,5},{5,4},{6,7},{7,6},{8,9},{9,8},{10,11... | collective-permute-start | bytes 3080 | tf_op jit(solution)/shard_map/ppermute | solution.py:42
  18.2 5.2 %collective-permute-start.1 = (f32[2,128]{1,0:T(2,128)S(1)}, f32[2,128]{1,0:T(2,128)S(1)}, u32[]{:S(2)}, u32[]{:S(2)}) collective-permute-start(f32[2,128]{1,0:T(2,128)S(1)} %get-tuple-element.35), channel_id=1, source_target_pairs={{1,2},{2,1},{3,4},{4,3},{5,6},{6,5},{9,10},{10,9},{11,12},{12,11},... | collective-permute-start | bytes 3080 | tf_op jit(solution)/shard_map/ppermute | solution.py:391
  23.4 7.7 %collective-permute-start.2 = (f32[256,128]{1,0:T(8,128)S(1)}, f32[256,128]{1,0:T(8,128)S(1)}, u32[]{:S(2)}, u32[]{:S(2)}) collective-permute-start(f32[256,128]{1,0:T(8,128)S(1)} %shard_map.79.smooth), channel_id=1, source_target_pairs={{0,1},{1,0},{2,3},{3,2},{4,5},{5,4},{6,7},{7,6},{8,9},{9,8},{10,11... | collective-permute-start | bytes 393224 | tf_op jit(solution)/shard_map/ppermute | solution.py:42
  23.5 8.2 %collective-permute-start.6 = (bf16[512,128]{1,0:T(8,128)(2,1)S(1)}, bf16[512,128]{1,0:T(8,128)(2,1)S(1)}, u32[]{:S(2)}, u32[]{:S(2)}) collective-permute-start(bf16[512,128]{1,0:T(8,128)(2,1)S(1)} %get-tuple-element.40.after), channel_id=1, source_target_pairs={{0,192},{1,25},{2,194},{3,27},{4,196},{5,29},{6,198},{7,31},{8,200... | collective-permute-start | bytes 393224 | tf_op jit(solution)/shard_map/ppermute | solution.py:34
  28.0 6.8 %collective-permute-start.5 = (bf16[512,128]{1,0:T(8,128)(2,1)S(1)}, bf16[512,128]{1,0:T(8,128)(2,1)S(1)}, u32[]{:S(2)}, u32[]{:S(2)}) collective-permute-start(bf16[512,128]{1,0:T(8,128)(2,1)S(1)} %get-tuple-element.39.after), channel_id=1, source_target_pairs={{0,64},{1,9},{2,66},{3,11},{4,68},{5,13},{6,70},{7,15},{8,72},{9,1... | collective-permute-start | bytes 393224 | tf_op jit(solution)/shard_map/ppermute | solution.py:34
  28.1 6.7 %collective-permute-start.4 = (bf16[512,128]{1,0:T(8,128)(2,1)S(1)}, bf16[512,128]{1,0:T(8,128)(2,1)S(1)}, u32[]{:S(2)}, u32[]{:S(2)}) collective-permute-start(bf16[512,128]{1,0:T(8,128)(2,1)S(1)} %get-tuple-element.38.after), channel_id=1, source_target_pairs={{0,128},{1,17},{2,130},{3,19},{4,132},{5,21},{6,134},{7,23},{8,136... | collective-permute-start | bytes 393224 | tf_op jit(solution)/shard_map/ppermute | solution.py:34
  29.9 6.5 %collective-permute-start.10 = (bf16[512,128]{1,0:T(8,128)(2,1)S(1)}, bf16[512,128]{1,0:T(8,128)(2,1)S(1)}, u32[]{:S(2)}, u32[]{:S(2)}) collective-permute-start(bf16[512,128]{1,0:T(8,128)(2,1)S(1)} %get-tuple-element.46), channel_id=1, source_target_pairs={{0,16},{1,129},{2,18},{3,131},{4,20},{5,133},{6,22},{7,135},{8,24}... | collective-permute-start | bytes 393224 | tf_op jit(solution)/shard_map/ppermute | solution.py:34
  31.2 6.4 %collective-permute-start.11 = (bf16[512,128]{1,0:T(8,128)(2,1)S(1)}, bf16[512,128]{1,0:T(8,128)(2,1)S(1)}, u32[]{:S(2)}, u32[]{:S(2)}) collective-permute-start(bf16[512,128]{1,0:T(8,128)(2,1)S(1)} %get-tuple-element.47), channel_id=1, source_target_pairs={{0,8},{1,65},{2,10},{3,67},{4,12},{5,69},{6,14},{7,71},{8,16},{9,7... | collective-permute-start | bytes 393224 | tf_op jit(solution)/shard_map/ppermute | solution.py:34
  31.8 5.8 %collective-permute-start.12 = (bf16[512,128]{1,0:T(8,128)(2,1)S(1)}, bf16[512,128]{1,0:T(8,128)(2,1)S(1)}, u32[]{:S(2)}, u32[]{:S(2)}) collective-permute-start(bf16[512,128]{1,0:T(8,128)(2,1)S(1)} %get-tuple-element.48), channel_id=1, source_target_pairs={{0,24},{1,193},{2,26},{3,195},{4,28},{5,197},{6,30},{7,199},{8,0},... | collective-permute-start | bytes 393224 | tf_op jit(solution)/shard_map/ppermute | solution.py:34
  37.7 9.4 %collective-permute-start.13 = (bf16[512,128]{1,0:T(8,128)(2,1)S(1)}, bf16[512,128]{1,0:T(8,128)(2,1)S(1)}, u32[]{:S(2)}, u32[]{:S(2)}) collective-permute-start(bf16[512,128]{1,0:T(8,128)(2,1)S(1)} %get-tuple-element.50.after), channel_id=1, source_target_pairs={{0,32},{8,40},{16,48},{24,56},{32,0},{40,8},{48,16},{56,24},{64,96... | collective-permute-start | bytes 393224 | tf_op jit(solution)/shard_map/ppermute | solution.py:38
  47.2 5.1 %collective-permute-start.14 = (bf16[512,128]{1,0:T(8,128)(2,1)S(1)}, bf16[512,128]{1,0:T(8,128)(2,1)S(1)}, u32[]{:S(2)}, u32[]{:S(2)}) collective-permute-start(bf16[512,128]{1,0:T(8,128)(2,1)S(1)} %get-tuple-element.53.first), channel_id=1, source_target_pairs={{0,24},{1,193},{2,26},{3,195},{4,28},{5,197},{6,30},{7,199},{8,0},... | collective-permute-start | bytes 393224 | tf_op jit(solution)/shard_map/ppermute | solution.py:34
  49.0 5.4 %collective-permute-start.15 = (bf16[512,128]{1,0:T(8,128)(2,1)S(1)}, bf16[512,128]{1,0:T(8,128)(2,1)S(1)}, u32[]{:S(2)}, u32[]{:S(2)}) collective-permute-start(bf16[512,128]{1,0:T(8,128)(2,1)S(1)} %get-tuple-element.53.first), channel_id=1, source_target_pairs={{0,16},{1,129},{2,18},{3,131},{4,20},{5,133},{6,22},{7,135},{8,24}... | collective-permute-start | bytes 393224 | tf_op jit(solution)/shard_map/ppermute | solution.py:34
  50.2 5.6 %collective-permute-start.16 = (bf16[512,128]{1,0:T(8,128)(2,1)S(1)}, bf16[512,128]{1,0:T(8,128)(2,1)S(1)}, u32[]{:S(2)}, u32[]{:S(2)}) collective-permute-start(bf16[512,128]{1,0:T(8,128)(2,1)S(1)} %get-tuple-element.53.first), channel_id=1, source_target_pairs={{0,8},{1,65},{2,10},{3,67},{4,12},{5,69},{6,14},{7,71},{8,16},{9,7... | collective-permute-start | bytes 393224 | tf_op jit(solution)/shard_map/ppermute | solution.py:34
  55.8 21.8 %collective-permute-start.25 = (bf16[3,512,128]{2,1,0:T(8,128)(2,1)S(1)}, bf16[3,512,128]{2,1,0:T(8,128)(2,1)S(1)}, u32[]{:S(2)}, u32[]{:S(2)}) collective-permute-start(bf16[3,512,128]{2,1,0:T(8,128)(2,1)S(1)} %pad_maximum_fusion.rest), channel_id=1, source_target_pairs={{0,128},{1,17},{2,130},{3,19},{4,132},{5,21},{6,134},{7,23},{8,136... | collective-permute-start | bytes 1179656 | tf_op jit(solution)/shard_map/ppermute | solution.py:34
  58.5 19.3 %collective-permute-start.22 = (bf16[3,512,128]{2,1,0:T(8,128)(2,1)S(1)}, bf16[3,512,128]{2,1,0:T(8,128)(2,1)S(1)}, u32[]{:S(2)}, u32[]{:S(2)}) collective-permute-start(bf16[3,512,128]{2,1,0:T(8,128)(2,1)S(1)} %pad_maximum_fusion.rest), channel_id=1, source_target_pairs={{0,192},{1,25},{2,194},{3,27},{4,196},{5,29},{6,198},{7,31},{8,200... | collective-permute-start | bytes 1179656 | tf_op jit(solution)/shard_map/ppermute | solution.py:34
  60.6 7.0 %collective-permute-start.24 = (bf16[512,128]{1,0:T(8,128)(2,1)S(1)}, bf16[512,128]{1,0:T(8,128)(2,1)S(1)}, u32[]{:S(2)}, u32[]{:S(2)}) collective-permute-start(bf16[512,128]{1,0:T(8,128)(2,1)S(1)} %get-tuple-element.53.first), channel_id=1, source_target_pairs={{0,128},{1,17},{2,130},{3,19},{4,132},{5,21},{6,134},{7,23},{8,136... | collective-permute-start | bytes 393224 | tf_op jit(solution)/shard_map/ppermute | solution.py:34
  60.6 30.1 %collective-permute-start.19 = (bf16[3,512,128]{2,1,0:T(8,128)(2,1)S(1)}, bf16[3,512,128]{2,1,0:T(8,128)(2,1)S(1)}, u32[]{:S(2)}, u32[]{:S(2)}) collective-permute-start(bf16[3,512,128]{2,1,0:T(8,128)(2,1)S(1)} %pad_maximum_fusion.rest), channel_id=1, source_target_pairs={{0,64},{1,9},{2,66},{3,11},{4,68},{5,13},{6,70},{7,15},{8,72},{9,1... | collective-permute-start | bytes 1179656 | tf_op jit(solution)/shard_map/ppermute | solution.py:34
  61.2 16.6 %collective-permute-start.21 = (bf16[512,128]{1,0:T(8,128)(2,1)S(1)}, bf16[512,128]{1,0:T(8,128)(2,1)S(1)}, u32[]{:S(2)}, u32[]{:S(2)}) collective-permute-start(bf16[512,128]{1,0:T(8,128)(2,1)S(1)} %get-tuple-element.53.first), channel_id=1, source_target_pairs={{0,192},{1,25},{2,194},{3,27},{4,196},{5,29},{6,198},{7,31},{8,200... | collective-permute-start | bytes 393224 | tf_op jit(solution)/shard_map/ppermute | solution.py:34
  67.6 17.2 %collective-permute-start.17 = (f32[256,128]{1,0:T(8,128)S(1)}, f32[256,128]{1,0:T(8,128)S(1)}, u32[]{:S(2)}, u32[]{:S(2)}) collective-permute-start(f32[256,128]{1,0:T(8,128)S(1)} %get-tuple-element.54), channel_id=1, source_target_pairs={{0,1},{1,0},{2,3},{3,2},{4,5},{5,4},{6,7},{7,6},{8,9},{9,8},{10,11... | collective-permute-start | bytes 393224 | tf_op jit(solution)/shard_map/ppermute | solution.py:42
  77.6 13.9 %collective-permute-start.27 = (bf16[4,256,128]{2,1,0:T(8,128)(2,1)S(1)}, bf16[4,256,128]{2,1,0:T(8,128)(2,1)S(1)}, u32[]{:S(2)}, u32[]{:S(2)}) collective-permute-start(bf16[4,256,128]{2,1,0:T(8,128)(2,1)S(1)} %shard_map.93), channel_id=1, source_target_pairs={{0,1},{1,0},{2,3},{3,2},{4,5},{5,4},{6,7},{7,6},{8,9},{9,8},{10,11... | collective-permute-start | bytes 786440 | tf_op jit(solution)/shard_map/ppermute | solution.py:42
  77.7 12.9 %collective-permute-start.18 = (bf16[512,128]{1,0:T(8,128)(2,1)S(1)}, bf16[512,128]{1,0:T(8,128)(2,1)S(1)}, u32[]{:S(2)}, u32[]{:S(2)}) collective-permute-start(bf16[512,128]{1,0:T(8,128)(2,1)S(1)} %get-tuple-element.53.first), channel_id=1, source_target_pairs={{0,64},{1,9},{2,66},{3,11},{4,68},{5,13},{6,70},{7,15},{8,72},{9,1... | collective-permute-start | bytes 393224 | tf_op jit(solution)/shard_map/ppermute | solution.py:34
  77.8 15.0 %collective-permute-start.26 = (bf16[4,256,128]{2,1,0:T(8,128)(2,1)S(1)}, bf16[4,256,128]{2,1,0:T(8,128)(2,1)S(1)}, u32[]{:S(2)}, u32[]{:S(2)}) collective-permute-start(bf16[4,256,128]{2,1,0:T(8,128)(2,1)S(1)} %shard_map.92), channel_id=1, source_target_pairs={{0,1},{1,0},{2,3},{3,2},{4,5},{5,4},{6,7},{7,6},{8,9},{9,8},{10,11... | collective-permute-start | bytes 786440 | tf_op jit(solution)/shard_map/ppermute | solution.py:42
  84.8 9.4 %collective-permute-start.23 = (bf16[4,256,128]{2,1,0:T(8,128)(2,1)S(1)}, bf16[4,256,128]{2,1,0:T(8,128)(2,1)S(1)}, u32[]{:S(2)}, u32[]{:S(2)}) collective-permute-start(bf16[4,256,128]{2,1,0:T(8,128)(2,1)S(1)} %shard_map.91), channel_id=1, source_target_pairs={{0,1},{1,0},{2,3},{3,2},{4,5},{5,4},{6,7},{7,6},{8,9},{9,8},{10,11... | collective-permute-start | bytes 786440 | tf_op jit(solution)/shard_map/ppermute | solution.py:42
  90.7 5.5 %collective-permute-start.20 = (bf16[4,256,128]{2,1,0:T(8,128)(2,1)S(1)}, bf16[4,256,128]{2,1,0:T(8,128)(2,1)S(1)}, u32[]{:S(2)}, u32[]{:S(2)}) collective-permute-start(bf16[4,256,128]{2,1,0:T(8,128)(2,1)S(1)} %shard_map.90), channel_id=1, source_target_pairs={{0,1},{1,0},{2,3},{3,2},{4,5},{5,4},{6,7},{7,6},{8,9},{9,8},{10,11... | collective-permute-start | bytes 786440 | tf_op jit(solution)/shard_map/ppermute | solution.py:42

commit v3 on v2

--- a/solution.py
+++ b/solution.py
@@ -137,6 +137,9 @@
     )
 
 
+PAIR = LINE // 2
+
+
 def own_kernel(ds, table, starts, scaled, tiles, *outs):
     for d, out in zip(ds, outs):
         for k in range(LINE):
@@ -144,10 +147,10 @@
             out[k] = product((scaled,), tiles, starts, j).astype(out.dtype)
 
 
-def own_rows(scaled, tiles, table, starts, ds):
+def own_rows(scaled, tiles, table, starts, ds, dtypes):
     angles, _, band, block = tiles.shape
     rows = scaled.shape[1]
-    outs = [((LINE, rows, block), jnp.bfloat16)] * len(ds)
+    outs = [((LINE, rows, block), dtype) for dtype in dtypes]
     flops = 2 * len(ds) * LINE * angles * rows * band * block
     kernel = functools.partial(own_kernel, ds)
     return call(kernel, [SMEM, SMEM, VMEM, VMEM], outs, flops)(
@@ -155,53 +158,67 @@
     )
 
 
-def join_kernel(d, table, starts, other, tiles, own, after, first, rest):
+def join_kernel(d, table, starts, other, tiles, own, after, lower, upper):
     rows = other.shape[1]
     for k in range(LINE):
         j = table[place(d) + k]
-        out = first if k == 0 else rest.at[k - 1]
-        out[:rows, :] = own[k]
+        out = (lower, upper)[k // PAIR].at[k % PAIR]
+        out[:rows, :] = own[k].astype(out.dtype)
         out[rows:, :] = product((other,), tiles, starts, j).astype(out.dtype)
 
 
-def joined(other, tiles, table, starts, d, own, after):
+def joined(other, tiles, table, starts, d, dtypes, own, after):
     angles, _, band, block = tiles.shape
     rows = other.shape[1]
-    outs = [((2 * rows, block), jnp.bfloat16), ((LINE - 1, 2 * rows, block), jnp.bfloat16)]
+    outs = [((PAIR, 2 * rows, block), dtype) for dtype in dtypes]
     flops = 2 * LINE * angles * rows * band * block
     kernel = functools.partial(join_kernel, d)
     specs = [SMEM, SMEM, VMEM, VMEM, VMEM, ANY]
     return call(kernel, specs, outs, flops)(table, starts, other, tiles, own, after)
 
 
-def both_kernel(d, table, starts, scaled, other, tiles, after, first, rest):
+def both_kernel(d, table, starts, scaled, other, tiles, after, lower, upper):
     for k in range(LINE):
         j = table[place(d) + k]
-        out = first if k == 0 else rest.at[k - 1]
-        out[...] = product((scaled, other), tiles, starts, j).astype(out.dtype)
-
-
-def both_rows(scaled, other, tiles, table, starts, d, dtype, after):
+        out = (lower, upper)[k // PAIR]
+        out[k % PAIR] = product((scaled, other), tiles, starts, j).astype(out.dtype)
+
+
+def both_rows(scaled, other, tiles, table, starts, d, dtypes, after):
     angles, _, band, block = tiles.shape
     rows = 2 * scaled.shape[1]
+    outs = [((PAIR, rows, block), dtype) for dtype in dtypes]
     flops = 2 * LINE * angles * rows * band * block
     kernel = functools.partial(both_kernel, d)
     specs = [SMEM, SMEM, VMEM, VMEM, VMEM, ANY]
-    outs = [((rows, block), dtype), ((LINE - 1, rows, block), dtype)]
     return call(kernel, specs, outs, flops)(table, starts, scaled, other, tiles, after)
 
 
-def line_kernel(own, s1, s2, s3, *sent):
-    for k in range(LINE - 1):
-        total = own[k]
-        for ref in (s1, s2, s3):
-            total = total + ref[k].astype(jnp.float32)
-        sent[k][...] = total.astype(jnp.bfloat16)
+def add_kernel(own, came, out):
+    for k in range(PAIR):
+        out[k] = (own[k] + came[k].astype(jnp.float32)).astype(out.dtype)
+
+
+def added(own, came):
+    return call(add_kernel, [VMEM] * 2, [(came.shape, came.dtype)], 1 << 18, 4)(own, came)[0]
+
+
+def line_kernel(lower, upper, l1, l3, h1, h3, kept, *sent):
+    for k in range(LINE):
+        own, one, two = ((lower, l1, l3), (upper, h1, h3))[k // PAIR]
+        i = k % PAIR
+        total = own[i] + one[i].astype(jnp.float32) + two[i].astype(jnp.float32)
+        if k == 0:
+            kept[...] = total
+        else:
+            sent[k - 1][...] = total.astype(jnp.bfloat16)
 
 
 def line_sum(own, arrived):
-    outs = [(own.shape[1:], jnp.bfloat16)] * (LINE - 1)
-    return call(line_kernel, [VMEM] * 4, outs, 1 << 20)(own, *arrived)
+    tile = own[0].shape[1:]
+    outs = [(tile, jnp.float32)] + [(tile, jnp.bfloat16)] * (LINE - 1)
+    kept, *sent = call(line_kernel, [VMEM] * 6, outs, 1 << 20)(*own, *arrived)
+    return kept, sent
 
 
 def smooth_kernel(cells, inner, outer, smooth):
@@ -224,21 +241,23 @@
     return call(smooth_kernel, [VMEM] * 3, outs, 1 << 20, 4)(cells, inner, outer)[0]
 
 
-def merge_kernel(smooth, beside, own, a1, a2, a3, s1, s2, s3, mine, message):
+def merge_kernel(smooth, beside, own, s1, s2, s3, mine, message):
     _, zh, _, owner = position()
     rows = smooth.shape[0]
     for at, part in ((slice(0, rows), smooth), (slice(rows, 2 * rows), beside)):
         total = own[at, :]
-        for ref in (a1, a2, a3, s1, s2, s3):
+        for ref in (s1, s2, s3):
             total = total + ref[at, :].astype(jnp.float32)
         total = jnp.where(zh == owner, total + part[...], total)
         mine[at, :] = total
         message[at, :] = total.astype(message.dtype)
 
 
-def merged(smooth, beside, own, first, reached):
+def merged(smooth, beside, own, reached):
     outs = [(own.shape, jnp.float32), (own.shape, jnp.bfloat16)]
-    return call(merge_kernel, [VMEM] * 9, outs, 1 << 20, 4)(smooth, beside, own, *first, *reached)
+    return call(merge_kernel, [VMEM] * 6, outs, 1 << 20, 4)(
+        smooth, beside, own, *reached
+    )
 
 
 def finish_kernel(mine, crossed, own, beside, lowered):
@@ -274,7 +293,7 @@
     return call(turn_kernel, [VMEM] * 2, outs, 1 << 20, 4)(own, received)
 
 
-GROUPS = (0, *FAR)
+GROUPS = (0, 1, 3, 2)
 
 
 def spread_kernel(table, starts, tiles, after, *outs):
@@ -306,22 +325,21 @@
     )
 
 
-def cut_kernel(first, rest, out):
+def cut_kernel(lower, upper, out):
     rows = out.shape[1]
-    out[0] = first[rows:, :]
-    for k in range(1, LINE):
-        out[k] = rest[k - 1, rows:, :]
-
-
-def cut(first, rest):
-    rows, block = first.shape
-    outs = [((LINE, rows // 2, block), first.dtype)]
-    return call(cut_kernel, [VMEM] * 2, outs, 1 << 18, 4)(first, rest)[0]
-
-
-def own_blocks(first, rest):
-    rows = first.shape[0] // 2
-    return [first[:rows, :]] + [rest[k, :rows, :] for k in range(LINE - 1)]
+    for k in range(LINE):
+        out[k] = (lower, upper)[k // PAIR][k % PAIR, rows:, :]
+
+
+def cut(lower, upper):
+    _, rows, block = lower.shape
+    outs = [((LINE, rows // 2, block), lower.dtype)]
+    return call(cut_kernel, [VMEM] * 2, outs, 1 << 18, 4)(lower, upper)[0]
+
+
+def own_blocks(lower, upper):
+    rows = lower.shape[1] // 2
+    return [(lower, upper)[k // PAIR][k % PAIR, :rows, :] for k in range(LINE)]
 
 
 def projected(blocks, weights):
@@ -331,9 +349,9 @@
     )
 
 
-def image_kernel(chained, whole, weights, first, rest, *refs):
+def image_kernel(chained, whole, weights, lower, upper, *refs):
     *refs, after, image = refs
-    blocks = own_blocks(first, rest)
+    blocks = own_blocks(lower, upper)
     if whole:
         blocks += [refs[0][k] for k in range(LINE)]
     depth = sum(block.shape[1] for block in blocks)
@@ -344,7 +362,7 @@
 
 def imaged(weights, piece, got, before, after):
     angles, detector, _ = weights.shape
-    rows = piece[0].shape[0] // 2
+    rows = piece[0].shape[1] // 2
     more = [v for v in (got, before) if v is not None]
     outs = [((angles, rows, detector), jnp.float32)]
     flops = weights.size * rows * (1 if got is None else 2)
@@ -389,50 +407,54 @@
     inner = swapped(inner)
     odd = range(1, count - 1, 2)
     outer = lax.ppermute(outer, "slab", [p for i in odd for p in ((i, i + 1), (i + 1, i))])
-    own2, own1 = own_rows(scaled, tiles, table, starts, (2, 1))
-    sent = {}
-    sent[2] = joined(other, tiles, table, starts, 2, own2, own1)
-    sent[1] = joined(other, tiles, table, starts, 1, own1, sent[2][0])
-    sent[3] = both_rows(scaled, other, tiles, table, starts, 3, jnp.bfloat16, sent[1][0])
-    own = both_rows(scaled, other, tiles, table, starts, 0, jnp.float32, sent[3][0])
-    first, arrived = [], []
-    for d in FAR:
-        arrived.append(moved(sent[d][1], True, d))
-    for d in FAR:
-        first.append(moved(sent[d][0], True, d))
-    passed = line_sum(own[1], arrived)
+    bf, wide = jnp.bfloat16, jnp.float32
+    own2, own1 = own_rows(scaled, tiles, table, starts, (2, 1), (bf, wide))
+    low2, up2 = joined(other, tiles, table, starts, 2, (bf, bf), own2, own1)
+    low1, up1 = joined(other, tiles, table, starts, 1, (wide, bf), own1, low2)
+    low3, up3 = both_rows(scaled, other, tiles, table, starts, 3, (bf, wide), up1)
+    own = both_rows(scaled, other, tiles, table, starts, 0, (wide, wide), low3)
+    low2 = moved(low2, True, 1)
+    up2 = moved(up2, True, -1)
+    up1 = moved(up1, True, 1)
+    low3 = moved(low3, True, -1)
+    low1, up3 = added(low1, low2), added(up3, up2)
+    low1 = moved(low1, True, 1)
+    up3 = moved(up3, True, -1)
+    kept, passed = line_sum(own, (low1, low3, up1, up3))
     reached = []
     for d in FAR:
         reached.append(moved(passed[d - 1], False, d))
     smooth = smoothed(cells, inner, outer)
     beside = swapped(smooth)
-    mine, message = merged(smooth, beside, own[0], first, reached)
+    mine, message = merged(smooth, beside, kept, reached)
     crossed = across(message)
     bands = dict(zip(GROUPS, spread(tiles, table, starts, detector, message)))
     own, beside, lowered = finished(mine, crossed)
 
-    came, first = {}, {}
+    came = {}
     for d in FAR:
         came[d] = moved(lowered, False, LINE - d)
-    for d in FAR:
-        first[d] = moved(lowered, True, LINE - d)
     beside, came[1], came[2], came[3] = lax.optimization_barrier(
         (beside, came[1], came[2], came[3])
     )
-    line = jnp.stack([came[d] for d in range(1, LINE)])
-    rest = {}
-    for d in FAR:
-        rest[d] = moved(line, True, LINE - d)
+    pieces = {0: (jnp.stack([lowered, came[1]]), jnp.stack([came[2], came[3]]))}
+    lower, upper = pieces[0]
+    low1 = moved(lower, True, -1)
+    up3 = moved(upper, True, 1)
+    up1 = moved(upper, True, -1)
+    low3 = moved(lower, True, 1)
+    low2 = moved(low1, True, -1)
+    up2 = moved(up3, True, 1)
+    pieces |= {1: (low1, up1), 3: (low3, up3), 2: (low2, up2)}
     received = swapped(beside)
     volume_next, token = turned(own, received, volume.shape)
-    first[0], rest[0] = lowered, line
     image, last = None, token
     for d in GROUPS:
-        piece = first[d], rest[d]
-        got = swapped(cut(*piece))
-        image = imaged(bands[d], piece, None if d == FAR[-1] else got, image, last)
+        got = swapped(cut(*pieces[d]))
+        whole = None if d == GROUPS[-1] else got
+        image = imaged(bands[d], pieces[d], whole, image, last)
         last = image
-    projection = leave(bands[FAR[-1]], got, image)
+    projection = leave(bands[GROUPS[-1]], got, image)
     return volume_next, projection.reshape(angles, 2, depth, detector)
 
 

time: 98.2 us -> 89.4 us (0.910)
  starting transfers between devices: 56 us -> 49.9 us
  waiting for transfers between devices: 17.8 us -> 15.1 us
    ppermute x18, waiting for transfers between devices: 13.2 us -> 9.25 us  [moved(): return lax.ppermute(value, ('ang', 'slab'), pairs)]
    ppermute x18, starting transfers between devices: 22.6 us -> 19.3 us  [moved(): return lax.ppermute(value, ('ang', 'slab'), pairs)]
    ppermute x8, starting transfers between devices: 23 us -> 20.7 us  [swapped(): return lax.ppermute(value, 'slab', [(i, i ^ 1) for i in range(SLABS)])]
  transfers between devices with their start and end apart: 28 -> 28, of which waited for: 10 -> 9; matrix products, arithmetic and copies ran while one was open for 0% -> 0% of each run, Pallas kernels for 15% -> 20%
where the time goes in v3:
time: 89.4 us; the launch traced here: 89.2 us
  starting transfers between devices  49.9 us (56%)
  Pallas kernels  22.2 us (25%)
  waiting for transfers between devices  15.1 us (17%)
  between operations  1.12 us (1%)
  local copies, waits for them, and re-layouts  0.91 us (1%)
    ppermute x8, starting transfers between devices, swapped(): return lax.ppermute(value, 'slab', [(i, i ^ 1) for i in range(SLABS)])  20.7 us
    ppermute x18, starting transfers between devices, moved(): return lax.ppermute(value, ('ang', 'slab'), pairs)  19.3 us
    ppermute x18, waiting for transfers between devices, moved(): return lax.ppermute(value, ('ang', 'slab'), pairs)  9.25 us
    ppermute x1, starting transfers between devices, across(): lax.ppermute(value, 'ang', [(a, a ^ XS) for a in range(YS * ZS * XS)])  6.88 us
    pallas_call x1, Pallas kernels, spread(): call(spread_kernel, [SMEM, SMEM, VMEM, ANY], outs, 1 << 31, 16)  4.99 us
    pallas_call x4, Pallas kernels, imaged(): return call(kernel, specs, outs, flops)(weights, *piece, *more, after)[0]  4.65 us
    pallas_call x2, Pallas kernels, both_rows(): call(kernel, specs, outs, flops)(table, starts, scaled, other, tiles, after)  3.66 us
    ppermute x1, starting transfers between devices, steps(): lax.ppermute(outer, 'slab', [p for i in odd for p in ((i, i + 1), (i + 1,...  3.06 us
  transfers between devices with their start and end apart: 28, of which 9 were waited for; matrix products, arithmetic and copies ran while one was open for 0% of the time, Pallas kernels for 20%

profile of v3, /device:TPU:1, one launch (start us, length us, event | category | flops | bytes accessed | tf_op | source)
XLA Modules:
  0.0 89.2 jit_solution(17135052040895793967)
XLA Ops:
  0.7 0.7 plan.1.table
  1.4 0.9 copy-done.2
  2.2 0.7 shard_map.77.after.scaled
  2.9 3.3 %collective-permute-start.3 = (bf16[4,256,512]{2,1,0:T(8,128)(2,1)S(1)}, bf16[4,256,512]{2,1,0:T(8,128)(2,1)S(1)}, u32[]{:S(2)}, u32[]{:S(2)}) collective-permute-start(bf16[4,256,512]{2,1,0:T(8,128)(2,1)S(1)} %shard_map.77.after.scaled), channel_id=1, source_target_pairs={{0,1},{1,0},{2,3},{3,2},{4,5},{5,4},{6,7},{7,6},{8,9},{9,8},{10,11... | collective-permute-start | bytes 3145736 | tf_op jit(solution)/shard_map/ppermute | solution.py:42
  6.2 1.8 %shard_map.80 = (bf16[4,256,128]{2,1,0:T(8,128)(2,1)S(1)}, f32[4,256,128]{2,1,0:T(8,128)S(1)}) custom-call(s32[32]{0:T(128)S(1)} %plan.1.table, s32[4,32]{1,0:T(4,128)S(1)} %copy-done.1, bf16[4,256,512]{2,1,0:T(8,128)(2,1)S(1)} %shard_map.77.after.scaled, bf16[4,32,256,128]{3,2,1,0:T(8,128)(2,1)S(1)} %bitcast.6), custom_call_target="tpu_custom_call" | custom-call | flops 536870912 | bytes 1048576 | tf_op jit(solution)/shard_map/pallas_call | solution.py:156
  8.1 0.4 collective-permute-done.3.other
  8.5 1.3 %shard_map.81 = (bf16[2,512,128]{2,1,0:T(8,128)(2,1)S(1)}, bf16[2,512,128]{2,1,0:T(8,128)(2,1)S(1)}) custom-call(s32[32]{0:T(128)S(1)} %plan.1.table, s32[4,32]{1,0:T(4,128)S(1)} %copy-done.1, bf16[4,256,512]{2,1,0:T(8,128)(2,1)S(1)} %collective-permute-done.3.other, bf16[4,32,256,128]{3,2,1,0:T(8,128)(2,1)S(1)} %bitcast.6, ...), custom_call_target="tpu_custom_call" | custom-call | flops 268435456 | bytes 1048576 | tf_op jit(solution)/shard_map/pallas_call | solution.py:177
  9.8 1.7 %collective-permute-start.8 = (bf16[2,512,128]{2,1,0:T(8,128)(2,1)S(1)}, bf16[2,512,128]{2,1,0:T(8,128)(2,1)S(1)}, u32[]{:S(2)}, u32[]{:S(2)}) collective-permute-start(bf16[2,512,128]{2,1,0:T(8,128)(2,1)S(1)} %get-tuple-element.46), channel_id=1, source_target_pairs={{0,192},{1,25},{2,194},{3,27},{4,196},{5,29},{6,198},{7,31},{8,200... | collective-permute-start | bytes 786440 | tf_op jit(solution)/shard_map/ppermute | solution.py:34
  11.4 1.3 %shard_map.82 = (f32[2,512,128]{2,1,0:T(8,128)S(1)}, bf16[2,512,128]{2,1,0:T(8,128)(2,1)S(1)}) custom-call(s32[32]{0:T(128)S(1)} %plan.1.table, s32[4,32]{1,0:T(4,128)S(1)} %copy-done.1, bf16[4,256,512]{2,1,0:T(8,128)(2,1)S(1)} %collective-permute-done.3.other, bf16[4,32,256,128]{3,2,1,0:T(8,128)(2,1)S(1)} %bitcast.6, ...), custom_call_target="tpu_custom_call" | custom-call | flops 268435456 | bytes 1048576 | tf_op jit(solution)/shard_map/pallas_call | solution.py:177
  12.7 0.3 collective-permute-start.7
  13.0 1.8 %shard_map.83 = (bf16[2,512,128]{2,1,0:T(8,128)(2,1)S(1)}, f32[2,512,128]{2,1,0:T(8,128)S(1)}) custom-call(s32[32]{0:T(128)S(1)} %plan.1.table, s32[4,32]{1,0:T(4,128)S(1)} %copy-done.1, bf16[4,256,512]{2,1,0:T(8,128)(2,1)S(1)} %shard_map.77.after.scaled, bf16[4,256,512]{2,1,0:T(8,128)(2,1)S(1)} %collective-permute-done.3.other, ...), custom_call_target="tpu_custom_call" | custom-call | flops 536870912 | bytes 1048576 | tf_op jit(solution)/shard_map/pallas_call | solution.py:194
  14.8 2.6 %collective-permute-start.6 = (bf16[2,512,128]{2,1,0:T(8,128)(2,1)S(1)}, bf16[2,512,128]{2,1,0:T(8,128)(2,1)S(1)}, u32[]{:S(2)}, u32[]{:S(2)}) collective-permute-start(bf16[2,512,128]{2,1,0:T(8,128)(2,1)S(1)} %get-tuple-element.41.after), channel_id=1, source_target_pairs={{0,192},{1,25},{2,194},{3,27},{4,196},{5,29},{6,198},{7,31},{8,200... | collective-permute-start | bytes 786440 | tf_op jit(solution)/shard_map/ppermute | solution.py:34
  17.5 1.5 %collective-permute-start.9 = (bf16[2,512,128]{2,1,0:T(8,128)(2,1)S(1)}, bf16[2,512,128]{2,1,0:T(8,128)(2,1)S(1)}, u32[]{:S(2)}, u32[]{:S(2)}) collective-permute-start(bf16[2,512,128]{2,1,0:T(8,128)(2,1)S(1)} %shard_map.86), channel_id=1, source_target_pairs={{0,192},{1,25},{2,194},{3,27},{4,196},{5,29},{6,198},{7,31},{8,200... | collective-permute-start | bytes 786440 | tf_op jit(solution)/shard_map/ppermute | solution.py:34
  19.2 0.1 shard_map.78
  19.3 3.1 %collective-permute-start = (f32[2,128]{1,0:T(2,128)S(1)}, f32[2,128]{1,0:T(2,128)S(1)}, u32[]{:S(2)}, u32[]{:S(2)}) collective-permute-start(f32[2,128]{1,0:T(2,128)S(1)} %get-tuple-element.35), channel_id=1, source_target_pairs={{0,1},{1,0},{2,3},{3,2},{4,5},{5,4},{6,7},{7,6},{8,9},{9,8},{10,11... | collective-permute-start | bytes 3080 | tf_op jit(solution)/shard_map/ppermute | solution.py:42
  22.4 0.8 collective-permute-done.inner
  23.2 3.1 %collective-permute-start.1 = (f32[2,128]{1,0:T(2,128)S(1)}, f32[2,128]{1,0:T(2,128)S(1)}, u32[]{:S(2)}, u32[]{:S(2)}) collective-permute-start(f32[2,128]{1,0:T(2,128)S(1)} %get-tuple-element.36), channel_id=1, source_target_pairs={{1,2},{2,1},{3,4},{4,3},{5,6},{6,5},{9,10},{10,9},{11,12},{12,11},... | collective-permute-start | bytes 3080 | tf_op jit(solution)/shard_map/ppermute | solution.py:409
  26.3 2.1 %collective-permute-done.1.outer = f32[2,128]{1,0:T(2,128)S(1)} collective-permute-done((f32[2,128]{1,0:T(2,128)S(1)}, f32[2,128]{1,0:T(2,128)S(1)}, u32[]{:S(2)}, u32[]{:S(2)}) %collective-permute-start.1) | collective-permute-done | bytes 1056 | tf_op jit(solution)/shard_map/ppermute | solution.py:409
  28.6 1.8 %shard_map.84 = (f32[2,512,128]{2,1,0:T(8,128)S(1)}, f32[2,512,128]{2,1,0:T(8,128)S(1)}) custom-call(s32[32]{0:T(128)S(1)} %plan.1.table, s32[4,32]{1,0:T(4,128)S(1)} %copy-done.1, bf16[4,256,512]{2,1,0:T(8,128)(2,1)S(1)} %shard_map.77.after.scaled, bf16[4,256,512]{2,1,0:T(8,128)(2,1)S(1)} %collective-permute-done.3.other, ...), custom_call_target="tpu_custom_call" | custom-call | flops 536870912 | bytes 1048576 | tf_op jit(solution)/shard_map/pallas_call | solution.py:194
  30.4 0.2 shard_map.87
  30.6 0.7 collective-permute-start.10
  31.3 2.0 %collective-permute-start.11 = (bf16[512,128]{1,0:T(8,128)(2,1)S(1)}, bf16[512,128]{1,0:T(8,128)(2,1)S(1)}, u32[]{:S(2)}, u32[]{:S(2)}) collective-permute-start(bf16[512,128]{1,0:T(8,128)(2,1)S(1)} %get-tuple-element.49), channel_id=1, source_target_pairs={{0,8},{1,65},{2,10},{3,67},{4,12},{5,69},{6,14},{7,71},{8,16},{9,7... | collective-permute-start | bytes 393224 | tf_op jit(solution)/shard_map/ppermute | solution.py:34
  33.3 0.7 collective-permute-start.12
  34.0 2.3 %collective-permute-done.10.s1 = bf16[512,128]{1,0:T(8,128)(2,1)S(1)} collective-permute-done((bf16[512,128]{1,0:T(8,128)(2,1)S(1)}, bf16[512,128]{1,0:T(8,128)(2,1)S(1)}, u32[]{:S(2)}, u32[]{:S(2)}) %collective-permute-start.10) | collective-permute-done | bytes 131104 | tf_op jit(solution)/shard_map/ppermute | solution.py:34
  36.3 1.1 %collective-permute-done.11.s2 = bf16[512,128]{1,0:T(8,128)(2,1)S(1)} collective-permute-done((bf16[512,128]{1,0:T(8,128)(2,1)S(1)}, bf16[512,128]{1,0:T(8,128)(2,1)S(1)}, u32[]{:S(2)}, u32[]{:S(2)}) %collective-permute-start.11) | collective-permute-done | bytes 131104 | tf_op jit(solution)/shard_map/ppermute | solution.py:34
  37.5 6.9 %collective-permute-start.13 = (bf16[512,128]{1,0:T(8,128)(2,1)S(1)}, bf16[512,128]{1,0:T(8,128)(2,1)S(1)}, u32[]{:S(2)}, u32[]{:S(2)}) collective-permute-start(bf16[512,128]{1,0:T(8,128)(2,1)S(1)} %get-tuple-element.52.after), channel_id=1, source_target_pairs={{0,32},{8,40},{16,48},{24,56},{32,0},{40,8},{48,16},{56,24},{64,96... | collective-permute-start | bytes 393224 | tf_op jit(solution)/shard_map/ppermute | solution.py:38
  44.4 2.5 %collective-permute-done.13.crossed = bf16[512,128]{1,0:T(8,128)(2,1)S(1)} collective-permute-done((bf16[512,128]{1,0:T(8,128)(2,1)S(1)}, bf16[512,128]{1,0:T(8,128)(2,1)S(1)}, u32[]{:S(2)}, u32[]{:S(2)}) %collective-permute-start.13) | collective-permute-done | bytes 131104 | tf_op jit(solution)/shard_map/ppermute | solution.py:38
  46.9 2.1 %collective-permute-start.14 = (bf16[512,128]{1,0:T(8,128)(2,1)S(1)}, bf16[512,128]{1,0:T(8,128)(2,1)S(1)}, u32[]{:S(2)}, u32[]{:S(2)}) collective-permute-start(bf16[512,128]{1,0:T(8,128)(2,1)S(1)} %get-tuple-element.55), channel_id=1, source_target_pairs={{0,24},{1,193},{2,26},{3,195},{4,28},{5,197},{6,30},{7,199},{8,0},... | collective-permute-start | bytes 393224 | tf_op jit(solution)/shard_map/ppermute | solution.py:34
  49.0 0.7 collective-permute-start.16
  49.7 2.6 %collective-permute-done.14 = bf16[512,128]{1,0:T(8,128)(2,1)S(1)} collective-permute-done((bf16[512,128]{1,0:T(8,128)(2,1)S(1)}, bf16[512,128]{1,0:T(8,128)(2,1)S(1)}, u32[]{:S(2)}, u32[]{:S(2)}) %collective-permute-start.14) | collective-permute-done | bytes 131104 | tf_op jit(solution)/shard_map/ppermute | solution.py:34
  52.3 2.1 %collective-permute-done.15 = bf16[512,128]{1,0:T(8,128)(2,1)S(1)} collective-permute-done((bf16[512,128]{1,0:T(8,128)(2,1)S(1)}, bf16[512,128]{1,0:T(8,128)(2,1)S(1)}, u32[]{:S(2)}, u32[]{:S(2)}) %collective-permute-start.15) | collective-permute-done | bytes 131104 | tf_op jit(solution)/shard_map/ppermute | solution.py:34
  54.4 1.0 %collective-permute-done.16 = bf16[512,128]{1,0:T(8,128)(2,1)S(1)} collective-permute-done((bf16[512,128]{1,0:T(8,128)(2,1)S(1)}, bf16[512,128]{1,0:T(8,128)(2,1)S(1)}, u32[]{:S(2)}, u32[]{:S(2)}) %collective-permute-start.16) | collective-permute-done | bytes 131104 | tf_op jit(solution)/shard_map/ppermute | solution.py:34
  55.5 1.6 %collective-permute-start.20 = (bf16[2,512,128]{2,1,0:T(8,128)(2,1)S(1)}, bf16[2,512,128]{2,1,0:T(8,128)(2,1)S(1)}, u32[]{:S(2)}, u32[]{:S(2)}) collective-permute-start(bf16[2,512,128]{2,1,0:T(8,128)(2,1)S(1)} %pad_maximum_fusion.1.upper), channel_id=1, source_target_pairs={{0,64},{1,9},{2,66},{3,11},{4,68},{5,13},{6,70},{7,15},{8,72},{9,1... | collective-permute-start | bytes 786440 | tf_op jit(solution)/shard_map/ppermute | solution.py:34
  57.1 1.2 %collective-permute-start.18 = (bf16[2,512,128]{2,1,0:T(8,128)(2,1)S(1)}, bf16[2,512,128]{2,1,0:T(8,128)(2,1)S(1)}, u32[]{:S(2)}, u32[]{:S(2)}) collective-permute-start(bf16[2,512,128]{2,1,0:T(8,128)(2,1)S(1)} %pad_maximum_fusion.lower), channel_id=1, source_target_pairs={{0,192},{1,25},{2,194},{3,27},{4,196},{5,29},{6,198},{7,31},{8,200... | collective-permute-start | bytes 786440 | tf_op jit(solution)/shard_map/ppermute | solution.py:34
  58.3 1.3 %collective-permute-start.25 = (bf16[2,512,128]{2,1,0:T(8,128)(2,1)S(1)}, bf16[2,512,128]{2,1,0:T(8,128)(2,1)S(1)}, u32[]{:S(2)}, u32[]{:S(2)}) collective-permute-start(bf16[2,512,128]{2,1,0:T(8,128)(2,1)S(1)} %pad_maximum_fusion.1.upper), channel_id=1, source_target_pairs={{0,192},{1,25},{2,194},{3,27},{4,196},{5,29},{6,198},{7,31},{8,200... | collective-permute-start | bytes 786440 | tf_op jit(solution)/shard_map/ppermute | solution.py:34
  59.6 0.2 collective-permute-start.23
  59.8 8.9 %collective-permute-start.17 = (f32[256,128]{1,0:T(8,128)S(1)}, f32[256,128]{1,0:T(8,128)S(1)}, u32[]{:S(2)}, u32[]{:S(2)}) collective-permute-start(f32[256,128]{1,0:T(8,128)S(1)} %get-tuple-element.56), channel_id=1, source_target_pairs={{0,1},{1,0},{2,3},{3,2},{4,5},{5,4},{6,7},{7,6},{8,9},{9,8},{10,11... | collective-permute-start | bytes 393224 | tf_op jit(solution)/shard_map/ppermute | solution.py:42
  68.7 2.7 %collective-permute-start.19 = (bf16[2,512,128]{2,1,0:T(8,128)(2,1)S(1)}, bf16[2,512,128]{2,1,0:T(8,128)(2,1)S(1)}, u32[]{:S(2)}, u32[]{:S(2)}) collective-permute-start(bf16[2,512,128]{2,1,0:T(8,128)(2,1)S(1)} %collective-permute-done.18.lower), channel_id=1, source_target_pairs={{0,192},{1,25},{2,194},{3,27},{4,196},{5,29},{6,198},{7,31},{8,200... | collective-permute-start | bytes 786440 | tf_op jit(solution)/shard_map/ppermute | solution.py:34
  71.4 3.0 %collective-permute-start.27 = (bf16[4,256,128]{2,1,0:T(8,128)(2,1)S(1)}, bf16[4,256,128]{2,1,0:T(8,128)(2,1)S(1)}, u32[]{:S(2)}, u32[]{:S(2)}) collective-permute-start(bf16[4,256,128]{2,1,0:T(8,128)(2,1)S(1)} %shard_map.95), channel_id=1, source_target_pairs={{0,1},{1,0},{2,3},{3,2},{4,5},{5,4},{6,7},{7,6},{8,9},{9,8},{10,11... | collective-permute-start | bytes 786440 | tf_op jit(solution)/shard_map/ppermute | solution.py:42
  74.4 1.5 %collective-permute-start.26 = (bf16[4,256,128]{2,1,0:T(8,128)(2,1)S(1)}, bf16[4,256,128]{2,1,0:T(8,128)(2,1)S(1)}, u32[]{:S(2)}, u32[]{:S(2)}) collective-permute-start(bf16[4,256,128]{2,1,0:T(8,128)(2,1)S(1)} %shard_map.94), channel_id=1, source_target_pairs={{0,1},{1,0},{2,3},{3,2},{4,5},{5,4},{6,7},{7,6},{8,9},{9,8},{10,11... | collective-permute-start | bytes 786440 | tf_op jit(solution)/shard_map/ppermute | solution.py:42
  76.0 5.0 %shard_map.91 = (bf16[4,512,1024]{2,1,0:T(8,128)(2,1)S(1)}, bf16[4,512,1024]{2,1,0:T(8,128)(2,1)S(1)}, bf16[4,512,1024]{2,1,0:T(8,128)(2,1)S(1)}, bf16[4,512,1024]{2,1,0:T(8,128)(2,1)S(1)}) custom-call(s32[32]{0:T(128)S(1)} %plan.1.table, s32[4,32]{1,0:T(4,128)S(1)} %copy-done.1, bf16[4,32,256,128]{3,2,1,0:T(8,128)(2,1)S(1)} %bitcast.6, ...), custom_call_target="tpu_custom_call" | custom-call | flops 2147483648 | bytes 1048576 | tf_op jit(solution)/shard_map/pallas_call | solution.py:323
  81.0 0.8 shard_map.90
  81.9 0.8 collective-permute-start.22
  82.7 1.3 %shard_map.96.refs_1_.refs_2_ = f32[4,256,512]{2,1,0:T(8,128)S(1)} custom-call(bf16[4,512,1024]{2,1,0:T(8,128)(2,1)S(1)} %get-tuple-element.64.weights, bf16[2,512,128]{2,1,0:T(8,128)(2,1)S(1)} %pad_maximum_fusion.lower, bf16[2,512,128]{2,1,0:T(8,128)(2,1)S(1)} %pad_maximum_fusion.1.upper, bf16[4,256,128]{2,1,0:T(8,128)(2,1)S(1)} %collective-permute-done.27.refs_0_, ...), custom_call_target="tpu_custom_call" | custom-call | flops 1073741824 | bytes 1048576 | tf_op jit(solution)/shard_map/pallas_call | solution.py:371
  84.0 1.3 %shard_map.97.refs_1_.refs_2_ = f32[4,256,512]{2,1,0:T(8,128)S(1)} custom-call(bf16[4,512,1024]{2,1,0:T(8,128)(2,1)S(1)} %get-tuple-element.63.weights, bf16[2,512,128]{2,1,0:T(8,128)(2,1)S(1)} %collective-permute-done.18.lower, bf16[2,512,128]{2,1,0:T(8,128)(2,1)S(1)} %collective-permute-done.25.upper, ...), custom_call_target="tpu_custom_call" | custom-call | flops 1073741824 | bytes 1048576 | tf_op jit(solution)/shard_map/pallas_call | solution.py:371
  85.3 1.3 %shard_map.98.refs_0_.refs_1_ = f32[4,256,512]{2,1,0:T(8,128)S(1)} custom-call(bf16[4,512,1024]{2,1,0:T(8,128)(2,1)S(1)} %get-tuple-element.62.weights, bf16[2,512,128]{2,1,0:T(8,128)(2,1)S(1)} %collective-permute-done.23.lower, bf16[2,512,128]{2,1,0:T(8,128)(2,1)S(1)} %collective-permute-done.20.upper, ...), custom_call_target="tpu_custom_call" | custom-call | flops 1073741824 | bytes 1048576 | tf_op jit(solution)/shard_map/pallas_call | solution.py:371
  86.6 0.8 shard_map.99.before
  87.4 1.7 %leave.1 = f32[4,256,512]{2,1,0:T(8,128)} custom-call(bf16[4,512,1024]{2,1,0:T(8,128)(2,1)S(1)} %get-tuple-element.58.weights, bf16[4,256,128]{2,1,0:T(8,128)(2,1)S(1)} %collective-permute-done.22.got, f32[4,256,512]{2,1,0:T(8,128)S(1)} %shard_map.99.before), custom_call_target="tpu_custom_call" | custom-call | flops 268435456 | bytes 1048576 | tf_op jit(solution)/shard_map/leave/pallas_call | solution.py:388
  (50 shorter events, 0.8 us)
Async XLA Ops:
  0.6 0.7 copy-start.4
  0.6 1.6 %copy-start.2 = (f32[4,2,128,512]{3,2,1,0:T(8,128)S(1)}, f32[4,2,128,512]{3,2,1,0:T(8,128)}, u32[]{:S(2)}) copy-start(f32[4,2,128,512]{3,2,1,0:T(8,128)} %updates.1) | copy-start | bytes 6291460
  0.6 1.6 %copy-start.3 = (s32[4]{0:T(128)S(1)}, s32[4]{0:T(128)}, u32[]{:S(2)}) copy-start(s32[4]{0:T(128)} %ids.1) | copy-start | bytes 52
  0.7 5.5 %slice-start = ((s8[8388608]{0:T(1024)(128)(4,1)}), s8[4194304]{0:T(1024)(128)(4,1)S(1)}, s32[]{:S(2)}) async-start(s8[8388608]{0:T(1024)(128)(4,1)} %bitcast.5), calls=%async_computation | async-start | bytes 8388608
  2.2 4.0 %slice-start.1 = ((s8[8388608]{0:T(1024)(128)(4,1)}), s8[4194304]{0:T(1024)(128)(4,1)S(1)}, s32[]{:S(2)}) async-start(s8[8388608]{0:T(1024)(128)(4,1)} %bitcast.5), calls=%async_computation.1 | async-start | bytes 8388608
  2.2 4.0 %copy-start.1 = (s32[4,32]{1,0:T(4,128)S(1)}, s32[4,32]{1,0:T(4,128)}, u32[]{:S(2)}) copy-start(s32[4,32]{1,0:T(4,128)} %starts.11) | copy-start | bytes 1540
  2.9 5.6 %collective-permute-start.3 = (bf16[4,256,512]{2,1,0:T(8,128)(2,1)S(1)}, bf16[4,256,512]{2,1,0:T(8,128)(2,1)S(1)}, u32[]{:S(2)}, u32[]{:S(2)}) collective-permute-start(bf16[4,256,512]{2,1,0:T(8,128)(2,1)S(1)} %shard_map.77.after.scaled), channel_id=1, source_target_pairs={{0,1},{1,0},{2,3},{3,2},{4,5},{5,4},{6,7},{7,6},{8,9},{9,8},{10,11... | collective-permute-start | bytes 3145736 | tf_op jit(solution)/shard_map/ppermute | solution.py:42
  9.8 7.7 %collective-permute-start.8 = (bf16[2,512,128]{2,1,0:T(8,128)(2,1)S(1)}, bf16[2,512,128]{2,1,0:T(8,128)(2,1)S(1)}, u32[]{:S(2)}, u32[]{:S(2)}) collective-permute-start(bf16[2,512,128]{2,1,0:T(8,128)(2,1)S(1)} %get-tuple-element.46), channel_id=1, source_target_pairs={{0,192},{1,25},{2,194},{3,27},{4,196},{5,29},{6,198},{7,31},{8,200... | collective-permute-start | bytes 786440 | tf_op jit(solution)/shard_map/ppermute | solution.py:34
  11.4 7.6 %collective-permute-start.4 = (bf16[2,512,128]{2,1,0:T(8,128)(2,1)S(1)}, bf16[2,512,128]{2,1,0:T(8,128)(2,1)S(1)}, u32[]{:S(2)}, u32[]{:S(2)}) collective-permute-start(bf16[2,512,128]{2,1,0:T(8,128)(2,1)S(1)} %get-tuple-element.39.after), channel_id=1, source_target_pairs={{0,64},{1,9},{2,66},{3,11},{4,68},{5,13},{6,70},{7,15},{8,72},{9,1... | collective-permute-start | bytes 786440 | tf_op jit(solution)/shard_map/ppermute | solution.py:34
  12.7 17.7 %collective-permute-start.7 = (bf16[2,512,128]{2,1,0:T(8,128)(2,1)S(1)}, bf16[2,512,128]{2,1,0:T(8,128)(2,1)S(1)}, u32[]{:S(2)}, u32[]{:S(2)}) collective-permute-start(bf16[2,512,128]{2,1,0:T(8,128)(2,1)S(1)} %get-tuple-element.40.after), channel_id=1, source_target_pairs={{0,64},{1,9},{2,66},{3,11},{4,68},{5,13},{6,70},{7,15},{8,72},{9,1... | collective-permute-start | bytes 786440 | tf_op jit(solution)/shard_map/ppermute | solution.py:34
  14.8 4.3 %copy-start = (f32[128,2,128]{2,1,0:T(2,128)S(1)}, f32[128,2,128]{2,1,0:T(2,128)}, u32[]{:S(2)}) copy-start(f32[128,2,128]{2,1,0:T(2,128)} %volume.1) | copy-start | bytes 393220
  14.8 15.6 %collective-permute-start.6 = (bf16[2,512,128]{2,1,0:T(8,128)(2,1)S(1)}, bf16[2,512,128]{2,1,0:T(8,128)(2,1)S(1)}, u32[]{:S(2)}, u32[]{:S(2)}) collective-permute-start(bf16[2,512,128]{2,1,0:T(8,128)(2,1)S(1)} %get-tuple-element.41.after), channel_id=1, source_target_pairs={{0,192},{1,25},{2,194},{3,27},{4,196},{5,29},{6,198},{7,31},{8,200... | collective-permute-start | bytes 786440 | tf_op jit(solution)/shard_map/ppermute | solution.py:34
  17.5 12.9 %collective-permute-start.9 = (bf16[2,512,128]{2,1,0:T(8,128)(2,1)S(1)}, bf16[2,512,128]{2,1,0:T(8,128)(2,1)S(1)}, u32[]{:S(2)}, u32[]{:S(2)}) collective-permute-start(bf16[2,512,128]{2,1,0:T(8,128)(2,1)S(1)} %shard_map.86), channel_id=1, source_target_pairs={{0,192},{1,25},{2,194},{3,27},{4,196},{5,29},{6,198},{7,31},{8,200... | collective-permute-start | bytes 786440 | tf_op jit(solution)/shard_map/ppermute | solution.py:34
  19.1 11.4 %collective-permute-start.5 = (bf16[2,512,128]{2,1,0:T(8,128)(2,1)S(1)}, bf16[2,512,128]{2,1,0:T(8,128)(2,1)S(1)}, u32[]{:S(2)}, u32[]{:S(2)}) collective-permute-start(bf16[2,512,128]{2,1,0:T(8,128)(2,1)S(1)} %shard_map.85), channel_id=1, source_target_pairs={{0,64},{1,9},{2,66},{3,11},{4,68},{5,13},{6,70},{7,15},{8,72},{9,1... | collective-permute-start | bytes 786440 | tf_op jit(solution)/shard_map/ppermute | solution.py:34
  19.3 3.9 %collective-permute-start = (f32[2,128]{1,0:T(2,128)S(1)}, f32[2,128]{1,0:T(2,128)S(1)}, u32[]{:S(2)}, u32[]{:S(2)}) collective-permute-start(f32[2,128]{1,0:T(2,128)S(1)} %get-tuple-element.35), channel_id=1, source_target_pairs={{0,1},{1,0},{2,3},{3,2},{4,5},{5,4},{6,7},{7,6},{8,9},{9,8},{10,11... | collective-permute-start | bytes 3080 | tf_op jit(solution)/shard_map/ppermute | solution.py:42
  23.2 5.2 %collective-permute-start.1 = (f32[2,128]{1,0:T(2,128)S(1)}, f32[2,128]{1,0:T(2,128)S(1)}, u32[]{:S(2)}, u32[]{:S(2)}) collective-permute-start(f32[2,128]{1,0:T(2,128)S(1)} %get-tuple-element.36), channel_id=1, source_target_pairs={{1,2},{2,1},{3,4},{4,3},{5,6},{6,5},{9,10},{10,9},{11,12},{12,11},... | collective-permute-start | bytes 3080 | tf_op jit(solution)/shard_map/ppermute | solution.py:409
  28.5 5.5 %collective-permute-start.2 = (f32[256,128]{1,0:T(8,128)S(1)}, f32[256,128]{1,0:T(8,128)S(1)}, u32[]{:S(2)}, u32[]{:S(2)}) collective-permute-start(f32[256,128]{1,0:T(8,128)S(1)} %shard_map.79.smooth), channel_id=1, source_target_pairs={{0,1},{1,0},{2,3},{3,2},{4,5},{5,4},{6,7},{7,6},{8,9},{9,8},{10,11... | collective-permute-start | bytes 393224 | tf_op jit(solution)/shard_map/ppermute | solution.py:42
  30.6 5.7 %collective-permute-start.10 = (bf16[512,128]{1,0:T(8,128)(2,1)S(1)}, bf16[512,128]{1,0:T(8,128)(2,1)S(1)}, u32[]{:S(2)}, u32[]{:S(2)}) collective-permute-start(bf16[512,128]{1,0:T(8,128)(2,1)S(1)} %get-tuple-element.48), channel_id=1, source_target_pairs={{0,16},{1,129},{2,18},{3,131},{4,20},{5,133},{6,22},{7,135},{8,24}... | collective-permute-start | bytes 393224 | tf_op jit(solution)/shard_map/ppermute | solution.py:34
  31.3 6.1 %collective-permute-start.11 = (bf16[512,128]{1,0:T(8,128)(2,1)S(1)}, bf16[512,128]{1,0:T(8,128)(2,1)S(1)}, u32[]{:S(2)}, u32[]{:S(2)}) collective-permute-start(bf16[512,128]{1,0:T(8,128)(2,1)S(1)} %get-tuple-element.49), channel_id=1, source_target_pairs={{0,8},{1,65},{2,10},{3,67},{4,12},{5,69},{6,14},{7,71},{8,16},{9,7... | collective-permute-start | bytes 393224 | tf_op jit(solution)/shard_map/ppermute | solution.py:34
  33.3 4.1 %collective-permute-start.12 = (bf16[512,128]{1,0:T(8,128)(2,1)S(1)}, bf16[512,128]{1,0:T(8,128)(2,1)S(1)}, u32[]{:S(2)}, u32[]{:S(2)}) collective-permute-start(bf16[512,128]{1,0:T(8,128)(2,1)S(1)} %get-tuple-element.50), channel_id=1, source_target_pairs={{0,24},{1,193},{2,26},{3,195},{4,28},{5,197},{6,30},{7,199},{8,0},... | collective-permute-start | bytes 393224 | tf_op jit(solution)/shard_map/ppermute | solution.py:34
  37.5 9.3 %collective-permute-start.13 = (bf16[512,128]{1,0:T(8,128)(2,1)S(1)}, bf16[512,128]{1,0:T(8,128)(2,1)S(1)}, u32[]{:S(2)}, u32[]{:S(2)}) collective-permute-start(bf16[512,128]{1,0:T(8,128)(2,1)S(1)} %get-tuple-element.52.after), channel_id=1, source_target_pairs={{0,32},{8,40},{16,48},{24,56},{32,0},{40,8},{48,16},{56,24},{64,96... | collective-permute-start | bytes 393224 | tf_op jit(solution)/shard_map/ppermute | solution.py:38
  46.9 5.4 %collective-permute-start.14 = (bf16[512,128]{1,0:T(8,128)(2,1)S(1)}, bf16[512,128]{1,0:T(8,128)(2,1)S(1)}, u32[]{:S(2)}, u32[]{:S(2)}) collective-permute-start(bf16[512,128]{1,0:T(8,128)(2,1)S(1)} %get-tuple-element.55), channel_id=1, source_target_pairs={{0,24},{1,193},{2,26},{3,195},{4,28},{5,197},{6,30},{7,199},{8,0},... | collective-permute-start | bytes 393224 | tf_op jit(solution)/shard_map/ppermute | solution.py:34
  49.0 5.4 %collective-permute-start.15 = (bf16[512,128]{1,0:T(8,128)(2,1)S(1)}, bf16[512,128]{1,0:T(8,128)(2,1)S(1)}, u32[]{:S(2)}, u32[]{:S(2)}) collective-permute-start(bf16[512,128]{1,0:T(8,128)(2,1)S(1)} %get-tuple-element.55), channel_id=1, source_target_pairs={{0,16},{1,129},{2,18},{3,131},{4,20},{5,133},{6,22},{7,135},{8,24}... | collective-permute-start | bytes 393224 | tf_op jit(solution)/shard_map/ppermute | solution.py:34
  49.0 6.4 %collective-permute-start.16 = (bf16[512,128]{1,0:T(8,128)(2,1)S(1)}, bf16[512,128]{1,0:T(8,128)(2,1)S(1)}, u32[]{:S(2)}, u32[]{:S(2)}) collective-permute-start(bf16[512,128]{1,0:T(8,128)(2,1)S(1)} %get-tuple-element.55), channel_id=1, source_target_pairs={{0,8},{1,65},{2,10},{3,67},{4,12},{5,69},{6,14},{7,71},{8,16},{9,7... | collective-permute-start | bytes 393224 | tf_op jit(solution)/shard_map/ppermute | solution.py:34
  55.5 13.2 %collective-permute-start.20 = (bf16[2,512,128]{2,1,0:T(8,128)(2,1)S(1)}, bf16[2,512,128]{2,1,0:T(8,128)(2,1)S(1)}, u32[]{:S(2)}, u32[]{:S(2)}) collective-permute-start(bf16[2,512,128]{2,1,0:T(8,128)(2,1)S(1)} %pad_maximum_fusion.1.upper), channel_id=1, source_target_pairs={{0,64},{1,9},{2,66},{3,11},{4,68},{5,13},{6,70},{7,15},{8,72},{9,1... | collective-permute-start | bytes 786440 | tf_op jit(solution)/shard_map/ppermute | solution.py:34
  57.1 11.6 %collective-permute-start.18 = (bf16[2,512,128]{2,1,0:T(8,128)(2,1)S(1)}, bf16[2,512,128]{2,1,0:T(8,128)(2,1)S(1)}, u32[]{:S(2)}, u32[]{:S(2)}) collective-permute-start(bf16[2,512,128]{2,1,0:T(8,128)(2,1)S(1)} %pad_maximum_fusion.lower), channel_id=1, source_target_pairs={{0,192},{1,25},{2,194},{3,27},{4,196},{5,29},{6,198},{7,31},{8,200... | collective-permute-start | bytes 786440 | tf_op jit(solution)/shard_map/ppermute | solution.py:34
  58.3 13.0 %collective-permute-start.25 = (bf16[2,512,128]{2,1,0:T(8,128)(2,1)S(1)}, bf16[2,512,128]{2,1,0:T(8,128)(2,1)S(1)}, u32[]{:S(2)}, u32[]{:S(2)}) collective-permute-start(bf16[2,512,128]{2,1,0:T(8,128)(2,1)S(1)} %pad_maximum_fusion.1.upper), channel_id=1, source_target_pairs={{0,192},{1,25},{2,194},{3,27},{4,196},{5,29},{6,198},{7,31},{8,200... | collective-permute-start | bytes 786440 | tf_op jit(solution)/shard_map/ppermute | solution.py:34
  59.6 14.8 %collective-permute-start.23 = (bf16[2,512,128]{2,1,0:T(8,128)(2,1)S(1)}, bf16[2,512,128]{2,1,0:T(8,128)(2,1)S(1)}, u32[]{:S(2)}, u32[]{:S(2)}) collective-permute-start(bf16[2,512,128]{2,1,0:T(8,128)(2,1)S(1)} %pad_maximum_fusion.lower), channel_id=1, source_target_pairs={{0,64},{1,9},{2,66},{3,11},{4,68},{5,13},{6,70},{7,15},{8,72},{9,1... | collective-permute-start | bytes 786440 | tf_op jit(solution)/shard_map/ppermute | solution.py:34
  59.8 16.1 %collective-permute-start.17 = (f32[256,128]{1,0:T(8,128)S(1)}, f32[256,128]{1,0:T(8,128)S(1)}, u32[]{:S(2)}, u32[]{:S(2)}) collective-permute-start(f32[256,128]{1,0:T(8,128)S(1)} %get-tuple-element.56), channel_id=1, source_target_pairs={{0,1},{1,0},{2,3},{3,2},{4,5},{5,4},{6,7},{7,6},{8,9},{9,8},{10,11... | collective-permute-start | bytes 393224 | tf_op jit(solution)/shard_map/ppermute | solution.py:42
  68.7 13.1 %collective-permute-start.21 = (bf16[2,512,128]{2,1,0:T(8,128)(2,1)S(1)}, bf16[2,512,128]{2,1,0:T(8,128)(2,1)S(1)}, u32[]{:S(2)}, u32[]{:S(2)}) collective-permute-start(bf16[2,512,128]{2,1,0:T(8,128)(2,1)S(1)} %collective-permute-done.20.upper), channel_id=1, source_target_pairs={{0,64},{1,9},{2,66},{3,11},{4,68},{5,13},{6,70},{7,15},{8,72},{9,1... | collective-permute-start | bytes 786440 | tf_op jit(solution)/shard_map/ppermute | solution.py:34
  68.7 13.1 %collective-permute-start.19 = (bf16[2,512,128]{2,1,0:T(8,128)(2,1)S(1)}, bf16[2,512,128]{2,1,0:T(8,128)(2,1)S(1)}, u32[]{:S(2)}, u32[]{:S(2)}) collective-permute-start(bf16[2,512,128]{2,1,0:T(8,128)(2,1)S(1)} %collective-permute-done.18.lower), channel_id=1, source_target_pairs={{0,192},{1,25},{2,194},{3,27},{4,196},{5,29},{6,198},{7,31},{8,200... | collective-permute-start | bytes 786440 | tf_op jit(solution)/shard_map/ppermute | solution.py:34
  71.4 11.3 %collective-permute-start.27 = (bf16[4,256,128]{2,1,0:T(8,128)(2,1)S(1)}, bf16[4,256,128]{2,1,0:T(8,128)(2,1)S(1)}, u32[]{:S(2)}, u32[]{:S(2)}) collective-permute-start(bf16[4,256,128]{2,1,0:T(8,128)(2,1)S(1)} %shard_map.95), channel_id=1, source_target_pairs={{0,1},{1,0},{2,3},{3,2},{4,5},{5,4},{6,7},{7,6},{8,9},{9,8},{10,11... | collective-permute-start | bytes 786440 | tf_op jit(solution)/shard_map/ppermute | solution.py:42
  74.4 9.6 %collective-permute-start.26 = (bf16[4,256,128]{2,1,0:T(8,128)(2,1)S(1)}, bf16[4,256,128]{2,1,0:T(8,128)(2,1)S(1)}, u32[]{:S(2)}, u32[]{:S(2)}) collective-permute-start(bf16[4,256,128]{2,1,0:T(8,128)(2,1)S(1)} %shard_map.94), channel_id=1, source_target_pairs={{0,1},{1,0},{2,3},{3,2},{4,5},{5,4},{6,7},{7,6},{8,9},{9,8},{10,11... | collective-permute-start | bytes 786440 | tf_op jit(solution)/shard_map/ppermute | solution.py:42
  75.9 9.4 %collective-permute-start.24 = (bf16[4,256,128]{2,1,0:T(8,128)(2,1)S(1)}, bf16[4,256,128]{2,1,0:T(8,128)(2,1)S(1)}, u32[]{:S(2)}, u32[]{:S(2)}) collective-permute-start(bf16[4,256,128]{2,1,0:T(8,128)(2,1)S(1)} %shard_map.93), channel_id=1, source_target_pairs={{0,1},{1,0},{2,3},{3,2},{4,5},{5,4},{6,7},{7,6},{8,9},{9,8},{10,11... | collective-permute-start | bytes 786440 | tf_op jit(solution)/shard_map/ppermute | solution.py:42
  81.9 5.5 %collective-permute-start.22 = (bf16[4,256,128]{2,1,0:T(8,128)(2,1)S(1)}, bf16[4,256,128]{2,1,0:T(8,128)(2,1)S(1)}, u32[]{:S(2)}, u32[]{:S(2)}) collective-permute-start(bf16[4,256,128]{2,1,0:T(8,128)(2,1)S(1)} %shard_map.92), channel_id=1, source_target_pairs={{0,1},{1,0},{2,3},{3,2},{4,5},{5,4},{6,7},{7,6},{8,9},{9,8},{10,11... | collective-permute-start | bytes 786440 | tf_op jit(solution)/shard_map/ppermute | solution.py:42

commit v4 on v2

--- a/solution.py
+++ b/solution.py
@@ -155,30 +155,28 @@
     )
 
 
-def join_kernel(d, table, starts, other, tiles, own, after, first, rest):
+def join_kernel(d, table, starts, other, tiles, own, after, out):
     rows = other.shape[1]
     for k in range(LINE):
         j = table[place(d) + k]
-        out = first if k == 0 else rest.at[k - 1]
-        out[:rows, :] = own[k]
-        out[rows:, :] = product((other,), tiles, starts, j).astype(out.dtype)
+        out[k, :rows, :] = own[k]
+        out[k, rows:, :] = product((other,), tiles, starts, j).astype(out.dtype)
 
 
 def joined(other, tiles, table, starts, d, own, after):
     angles, _, band, block = tiles.shape
     rows = other.shape[1]
-    outs = [((2 * rows, block), jnp.bfloat16), ((LINE - 1, 2 * rows, block), jnp.bfloat16)]
+    outs = [((LINE, 2 * rows, block), jnp.bfloat16)]
     flops = 2 * LINE * angles * rows * band * block
     kernel = functools.partial(join_kernel, d)
     specs = [SMEM, SMEM, VMEM, VMEM, VMEM, ANY]
-    return call(kernel, specs, outs, flops)(table, starts, other, tiles, own, after)
-
-
-def both_kernel(d, table, starts, scaled, other, tiles, after, first, rest):
+    return call(kernel, specs, outs, flops)(table, starts, other, tiles, own, after)[0]
+
+
+def both_kernel(d, table, starts, scaled, other, tiles, after, out):
     for k in range(LINE):
         j = table[place(d) + k]
-        out = first if k == 0 else rest.at[k - 1]
-        out[...] = product((scaled, other), tiles, starts, j).astype(out.dtype)
+        out[k] = product((scaled, other), tiles, starts, j).astype(out.dtype)
 
 
 def both_rows(scaled, other, tiles, table, starts, d, dtype, after):
@@ -187,21 +185,27 @@
     flops = 2 * LINE * angles * rows * band * block
     kernel = functools.partial(both_kernel, d)
     specs = [SMEM, SMEM, VMEM, VMEM, VMEM, ANY]
-    outs = [((rows, block), dtype), ((LINE - 1, rows, block), dtype)]
-    return call(kernel, specs, outs, flops)(table, starts, scaled, other, tiles, after)
-
-
-def line_kernel(own, s1, s2, s3, *sent):
-    for k in range(LINE - 1):
+    return call(kernel, specs, [((LINE, rows, block), dtype)], flops)(
+        table, starts, scaled, other, tiles, after
+    )[0]
+
+
+def line_kernel(own, s1, s2, s3, kept, *sent):
+    for k in range(LINE):
         total = own[k]
         for ref in (s1, s2, s3):
             total = total + ref[k].astype(jnp.float32)
-        sent[k][...] = total.astype(jnp.bfloat16)
+        if k == 0:
+            kept[...] = total
+        else:
+            sent[k - 1][...] = total.astype(jnp.bfloat16)
 
 
 def line_sum(own, arrived):
-    outs = [(own.shape[1:], jnp.bfloat16)] * (LINE - 1)
-    return call(line_kernel, [VMEM] * 4, outs, 1 << 20)(own, *arrived)
+    tile = own.shape[1:]
+    outs = [(tile, jnp.float32)] + [(tile, jnp.bfloat16)] * (LINE - 1)
+    kept, *sent = call(line_kernel, [VMEM] * 4, outs, 1 << 20)(own, *arrived)
+    return kept, sent
 
 
 def smooth_kernel(cells, inner, outer, smooth):
@@ -224,21 +228,23 @@
     return call(smooth_kernel, [VMEM] * 3, outs, 1 << 20, 4)(cells, inner, outer)[0]
 
 
-def merge_kernel(smooth, beside, own, a1, a2, a3, s1, s2, s3, mine, message):
+def merge_kernel(smooth, beside, own, s1, s2, s3, mine, message):
     _, zh, _, owner = position()
     rows = smooth.shape[0]
     for at, part in ((slice(0, rows), smooth), (slice(rows, 2 * rows), beside)):
         total = own[at, :]
-        for ref in (a1, a2, a3, s1, s2, s3):
+        for ref in (s1, s2, s3):
             total = total + ref[at, :].astype(jnp.float32)
         total = jnp.where(zh == owner, total + part[...], total)
         mine[at, :] = total
         message[at, :] = total.astype(message.dtype)
 
 
-def merged(smooth, beside, own, first, reached):
+def merged(smooth, beside, own, reached):
     outs = [(own.shape, jnp.float32), (own.shape, jnp.bfloat16)]
-    return call(merge_kernel, [VMEM] * 9, outs, 1 << 20, 4)(smooth, beside, own, *first, *reached)
+    return call(merge_kernel, [VMEM] * 6, outs, 1 << 20, 4)(
+        smooth, beside, own, *reached
+    )
 
 
 def finish_kernel(mine, crossed, own, beside, lowered):
@@ -306,22 +312,14 @@
     )
 
 
-def cut_kernel(first, rest, out):
-    rows = out.shape[1]
-    out[0] = first[rows:, :]
-    for k in range(1, LINE):
-        out[k] = rest[k - 1, rows:, :]
-
-
-def cut(first, rest):
-    rows, block = first.shape
-    outs = [((LINE, rows // 2, block), first.dtype)]
-    return call(cut_kernel, [VMEM] * 2, outs, 1 << 18, 4)(first, rest)[0]
-
-
-def own_blocks(first, rest):
-    rows = first.shape[0] // 2
-    return [first[:rows, :]] + [rest[k, :rows, :] for k in range(LINE - 1)]
+def cut_kernel(piece, out):
+    out[...] = piece[:, out.shape[1] :, :]
+
+
+def cut(piece):
+    count, rows, block = piece.shape
+    outs = [((count, rows // 2, block), piece.dtype)]
+    return call(cut_kernel, [VMEM], outs, 1 << 18, 4)(piece)[0]
 
 
 def projected(blocks, weights):
@@ -331,9 +329,9 @@
     )
 
 
-def image_kernel(chained, whole, weights, first, rest, *refs):
+def image_kernel(chained, whole, weights, piece, *refs):
     *refs, after, image = refs
-    blocks = own_blocks(first, rest)
+    blocks = [piece[k, : piece.shape[1] // 2, :] for k in range(LINE)]
     if whole:
         blocks += [refs[0][k] for k in range(LINE)]
     depth = sum(block.shape[1] for block in blocks)
@@ -344,13 +342,13 @@
 
 def imaged(weights, piece, got, before, after):
     angles, detector, _ = weights.shape
-    rows = piece[0].shape[0] // 2
+    rows = piece.shape[1] // 2
     more = [v for v in (got, before) if v is not None]
     outs = [((angles, rows, detector), jnp.float32)]
     flops = weights.size * rows * (1 if got is None else 2)
     kernel = functools.partial(image_kernel, before is not None, got is not None)
-    specs = [VMEM] * (3 + len(more)) + [ANY]
-    return call(kernel, specs, outs, flops)(weights, *piece, *more, after)[0]
+    specs = [VMEM] * (2 + len(more)) + [ANY]
+    return call(kernel, specs, outs, flops)(weights, piece, *more, after)[0]
 
 
 def leave_kernel(weights, got, before, out, image, done):
@@ -385,52 +383,47 @@
     table = plan()
     scaled = scale(updates, table, ids, weights)
     other = swapped(scaled)
-    cells, inner, outer = edges(volume, scaled)
+    own2, own1 = own_rows(scaled, tiles, table, starts, (2, 1))
+    sent = {}
+    sent[2] = joined(other, tiles, table, starts, 2, own2, own1)
+    sent[1] = joined(other, tiles, table, starts, 1, own1, sent[2])
+    sent[3] = both_rows(scaled, other, tiles, table, starts, 3, jnp.bfloat16, sent[1])
+    own = both_rows(scaled, other, tiles, table, starts, 0, jnp.float32, sent[3])
+    arrived = []
+    for d in FAR:
+        arrived.append(moved(sent[d], True, d))
+
+    cells, inner, outer = edges(volume, own)
     inner = swapped(inner)
     odd = range(1, count - 1, 2)
     outer = lax.ppermute(outer, "slab", [p for i in odd for p in ((i, i + 1), (i + 1, i))])
-    own2, own1 = own_rows(scaled, tiles, table, starts, (2, 1))
-    sent = {}
-    sent[2] = joined(other, tiles, table, starts, 2, own2, own1)
-    sent[1] = joined(other, tiles, table, starts, 1, own1, sent[2][0])
-    sent[3] = both_rows(scaled, other, tiles, table, starts, 3, jnp.bfloat16, sent[1][0])
-    own = both_rows(scaled, other, tiles, table, starts, 0, jnp.float32, sent[3][0])
-    first, arrived = [], []
-    for d in FAR:
-        arrived.append(moved(sent[d][1], True, d))
-    for d in FAR:
-        first.append(moved(sent[d][0], True, d))
-    passed = line_sum(own[1], arrived)
+    smooth = smoothed(cells, inner, outer)
+    beside = swapped(smooth)
+    kept, passed = line_sum(own, arrived)
     reached = []
     for d in FAR:
         reached.append(moved(passed[d - 1], False, d))
-    smooth = smoothed(cells, inner, outer)
-    beside = swapped(smooth)
-    mine, message = merged(smooth, beside, own[0], first, reached)
+    mine, message = merged(smooth, beside, kept, reached)
     crossed = across(message)
     bands = dict(zip(GROUPS, spread(tiles, table, starts, detector, message)))
     own, beside, lowered = finished(mine, crossed)
 
-    came, first = {}, {}
+    came = {}
     for d in FAR:
         came[d] = moved(lowered, False, LINE - d)
-    for d in FAR:
-        first[d] = moved(lowered, True, LINE - d)
     beside, came[1], came[2], came[3] = lax.optimization_barrier(
         (beside, came[1], came[2], came[3])
     )
-    line = jnp.stack([came[d] for d in range(1, LINE)])
-    rest = {}
+    pieces = {0: jnp.stack([lowered] + [came[d] for d in range(1, LINE)])}
     for d in FAR:
-        rest[d] = moved(line, True, LINE - d)
+        pieces[d] = moved(pieces[0], True, LINE - d)
     received = swapped(beside)
     volume_next, token = turned(own, received, volume.shape)
-    first[0], rest[0] = lowered, line
     image, last = None, token
     for d in GROUPS:
-        piece = first[d], rest[d]
-        got = swapped(cut(*piece))
-        image = imaged(bands[d], piece, None if d == FAR[-1] else got, image, last)
+        got = swapped(cut(pieces[d]))
+        whole = None if d == FAR[-1] else got
+        image = imaged(bands[d], pieces[d], whole, image, last)
         last = image
     projection = leave(bands[FAR[-1]], got, image)
     return volume_next, projection.reshape(angles, 2, depth, detector)

time: 98.2 us -> 93.6 us (0.953)
  the two profiles are of different devices: /device:TPU:1 before, /device:TPU:2 now
where the time goes in v4:
time: 93.6 us; the launch traced here: 92.3 us
  waiting for transfers between devices  33.4 us (36%)
  starting transfers between devices  32.8 us (35%)
  Pallas kernels  22.1 us (24%)
  local copies, waits for them, and re-layouts  2.81 us (3%)
  between operations  1.07 us (1%)
    ppermute x12, waiting for transfers between devices, moved(): return lax.ppermute(value, ('ang', 'slab'), pairs)  29.6 us
    ppermute x12, starting transfers between devices, moved(): return lax.ppermute(value, ('ang', 'slab'), pairs)  18.8 us
    ppermute x1, starting transfers between devices, across(): lax.ppermute(value, 'ang', [(a, a ^ XS) for a in range(YS * ZS * XS)])  7.25 us
    ppermute x8, starting transfers between devices, swapped(): return lax.ppermute(value, 'slab', [(i, i ^ 1) for i in range(SLABS)])  6.15 us
    pallas_call x1, Pallas kernels, spread(): call(spread_kernel, [SMEM, SMEM, VMEM, ANY], outs, 1 << 31, 16)  4.99 us
    pallas_call x4, Pallas kernels, imaged(): return call(kernel, specs, outs, flops)(weights, piece, *more, after)[0]  4.68 us
    pallas_call x2, Pallas kernels, both_rows(): call(kernel, specs, [((LINE, rows, block), dtype)], flops)  3.67 us
    ppermute x1, waiting for transfers between devices, across(): lax.ppermute(value, 'ang', [(a, a ^ XS) for a in range(YS * ZS * XS)])  3.33 us
  transfers between devices with their start and end apart: 22, of which 10 were waited for; matrix products, arithmetic and copies ran while one was open for 0% of the time, Pallas kernels for 16%

profile of v4, /device:TPU:2, one launch (start us, length us, event | category | flops | bytes accessed | tf_op | source)
XLA Modules:
  0.0 92.3 jit_solution(13593881230192416313)
XLA Ops:
  0.7 0.7 plan.1.table
  1.4 0.9 copy-done.2
  2.2 0.7 shard_map.77.scaled
  2.9 0.1 collective-permute-start
  3.0 0.5 slice-done
  3.5 1.4 %slice-done.1 = s8[4194304]{0:T(1024)(128)(4,1)S(1)} async-done(((s8[8388608]{0:T(1024)(128)(4,1)}), s8[4194304]{0:T(1024)(128)(4,1)S(1)}, s32[]{:S(2)}) %slice-start.1) | async-done | bytes 4194328
  4.9 1.8 %shard_map.78 = (bf16[4,256,128]{2,1,0:T(8,128)(2,1)S(1)}, bf16[4,256,128]{2,1,0:T(8,128)(2,1)S(1)}) custom-call(s32[32]{0:T(128)S(1)} %plan.1.table, s32[4,32]{1,0:T(4,128)S(1)} %copy-done.1, bf16[4,256,512]{2,1,0:T(8,128)(2,1)S(1)} %shard_map.77.scaled, bf16[4,32,256,128]{3,2,1,0:T(8,128)(2,1)S(1)} %bitcast.6), custom_call_target="tpu_custom_call" | custom-call | flops 536870912 | bytes 1048576 | tf_op jit(solution)/shard_map/pallas_call | solution.py:153
  6.8 1.3 %shard_map.79.after = bf16[4,512,128]{2,1,0:T(8,128)(2,1)S(1)} custom-call(s32[32]{0:T(128)S(1)} %plan.1.table, s32[4,32]{1,0:T(4,128)S(1)} %copy-done.1, bf16[4,256,512]{2,1,0:T(8,128)(2,1)S(1)} %collective-permute-done.other, bf16[4,32,256,128]{3,2,1,0:T(8,128)(2,1)S(1)} %bitcast.6, bf16[4,256,128]{2,1,0:T(8,128)(2,1)S(1)} %get-tuple-element.27.own, ...), custom_call_target="tpu_custom_call" | custom-call | flops 268435456 | bytes 1048576 | tf_op jit(solution)/shard_map/pallas_call | solution.py:173
  8.0 1.3 %shard_map.80.after = bf16[4,512,128]{2,1,0:T(8,128)(2,1)S(1)} custom-call(s32[32]{0:T(128)S(1)} %plan.1.table, s32[4,32]{1,0:T(4,128)S(1)} %copy-done.1, bf16[4,256,512]{2,1,0:T(8,128)(2,1)S(1)} %collective-permute-done.other, bf16[4,32,256,128]{3,2,1,0:T(8,128)(2,1)S(1)} %bitcast.6, bf16[4,256,128]{2,1,0:T(8,128)(2,1)S(1)} %get-tuple-element.26.after.own, ...), custom_call_target="tpu_custom_call" | custom-call | flops 268435456 | bytes 1048576 | tf_op jit(solution)/shard_map/pallas_call | solution.py:173
  9.3 1.8 %shard_map.81.after = bf16[4,512,128]{2,1,0:T(8,128)(2,1)S(1)} custom-call(s32[32]{0:T(128)S(1)} %plan.1.table, s32[4,32]{1,0:T(4,128)S(1)} %copy-done.1, bf16[4,256,512]{2,1,0:T(8,128)(2,1)S(1)} %shard_map.77.scaled, bf16[4,256,512]{2,1,0:T(8,128)(2,1)S(1)} %collective-permute-done.other, bf16[4,32,256,128]{3,2,1,0:T(8,128)(2,1)S(1)} %bitcast.6, ...), custom_call_target="tpu_custom_call" | custom-call | flops 536870912 | bytes 1048576 | tf_op jit(solution)/shard_map/pallas_call | solution.py:188
  11.2 3.1 %collective-permute-start.6 = (bf16[4,512,128]{2,1,0:T(8,128)(2,1)S(1)}, bf16[4,512,128]{2,1,0:T(8,128)(2,1)S(1)}, u32[]{:S(2)}, u32[]{:S(2)}) collective-permute-start(bf16[4,512,128]{2,1,0:T(8,128)(2,1)S(1)} %shard_map.81.after), channel_id=1, source_target_pairs={{0,192},{1,25},{2,194},{3,27},{4,196},{5,29},{6,198},{7,31},{8,200... | collective-permute-start | bytes 1572872 | tf_op jit(solution)/shard_map/ppermute | solution.py:34
  14.3 2.2 %collective-permute-start.4 = (bf16[4,512,128]{2,1,0:T(8,128)(2,1)S(1)}, bf16[4,512,128]{2,1,0:T(8,128)(2,1)S(1)}, u32[]{:S(2)}, u32[]{:S(2)}) collective-permute-start(bf16[4,512,128]{2,1,0:T(8,128)(2,1)S(1)} %shard_map.79.after), channel_id=1, source_target_pairs={{0,128},{1,17},{2,130},{3,19},{4,132},{5,21},{6,134},{7,23},{8,136... | collective-permute-start | bytes 1572872 | tf_op jit(solution)/shard_map/ppermute | solution.py:34
  16.5 1.8 %shard_map.82.after.own = f32[4,512,128]{2,1,0:T(8,128)S(1)} custom-call(s32[32]{0:T(128)S(1)} %plan.1.table, s32[4,32]{1,0:T(4,128)S(1)} %copy-done.1, bf16[4,256,512]{2,1,0:T(8,128)(2,1)S(1)} %shard_map.77.scaled, bf16[4,256,512]{2,1,0:T(8,128)(2,1)S(1)} %collective-permute-done.other, bf16[4,32,256,128]{3,2,1,0:T(8,128)(2,1)S(1)} %bitcast.6, ...), custom_call_target="tpu_custom_call" | custom-call | flops 536870912 | bytes 1048576 | tf_op jit(solution)/shard_map/pallas_call | solution.py:188
  18.3 0.1 shard_map.83
  18.5 0.1 collective-permute-start.1
  18.6 0.7 collective-permute-start.2
  19.2 0.5 collective-permute-done.1.inner
  19.8 4.6 %collective-permute-start.3 = (f32[256,128]{1,0:T(8,128)S(1)}, f32[256,128]{1,0:T(8,128)S(1)}, u32[]{:S(2)}, u32[]{:S(2)}) collective-permute-start(f32[256,128]{1,0:T(8,128)S(1)} %shard_map.84.smooth), channel_id=1, source_target_pairs={{0,1},{1,0},{2,3},{3,2},{4,5},{5,4},{6,7},{7,6},{8,9},{9,8},{10,11... | collective-permute-start | bytes 393224 | tf_op jit(solution)/shard_map/ppermute | solution.py:42
  24.4 2.2 %collective-permute-done.6.s3 = bf16[4,512,128]{2,1,0:T(8,128)(2,1)S(1)} collective-permute-done((bf16[4,512,128]{2,1,0:T(8,128)(2,1)S(1)}, bf16[4,512,128]{2,1,0:T(8,128)(2,1)S(1)}, u32[]{:S(2)}, u32[]{:S(2)}) %collective-permute-start.6) | collective-permute-done | bytes 524320 | tf_op jit(solution)/shard_map/ppermute | solution.py:34
  26.6 3.7 %collective-permute-done.5.s2 = bf16[4,512,128]{2,1,0:T(8,128)(2,1)S(1)} collective-permute-done((bf16[4,512,128]{2,1,0:T(8,128)(2,1)S(1)}, bf16[4,512,128]{2,1,0:T(8,128)(2,1)S(1)}, u32[]{:S(2)}, u32[]{:S(2)}) %collective-permute-start.5) | collective-permute-done | bytes 524320 | tf_op jit(solution)/shard_map/ppermute | solution.py:34
  30.3 0.2 shard_map.85
  30.5 2.2 %collective-permute-start.7 = (bf16[512,128]{1,0:T(8,128)(2,1)S(1)}, bf16[512,128]{1,0:T(8,128)(2,1)S(1)}, u32[]{:S(2)}, u32[]{:S(2)}) collective-permute-start(bf16[512,128]{1,0:T(8,128)(2,1)S(1)} %get-tuple-element.32), channel_id=1, source_target_pairs={{0,16},{1,129},{2,18},{3,131},{4,20},{5,133},{6,22},{7,135},{8,24}... | collective-permute-start | bytes 393224 | tf_op jit(solution)/shard_map/ppermute | solution.py:34
  32.7 2.0 %collective-permute-start.9 = (bf16[512,128]{1,0:T(8,128)(2,1)S(1)}, bf16[512,128]{1,0:T(8,128)(2,1)S(1)}, u32[]{:S(2)}, u32[]{:S(2)}) collective-permute-start(bf16[512,128]{1,0:T(8,128)(2,1)S(1)} %get-tuple-element.34), channel_id=1, source_target_pairs={{0,24},{1,193},{2,26},{3,195},{4,28},{5,197},{6,30},{7,199},{8,0},... | collective-permute-start | bytes 393224 | tf_op jit(solution)/shard_map/ppermute | solution.py:34
  34.8 2.4 %collective-permute-done.7.s1 = bf16[512,128]{1,0:T(8,128)(2,1)S(1)} collective-permute-done((bf16[512,128]{1,0:T(8,128)(2,1)S(1)}, bf16[512,128]{1,0:T(8,128)(2,1)S(1)}, u32[]{:S(2)}, u32[]{:S(2)}) %collective-permute-start.7) | collective-permute-done | bytes 131104 | tf_op jit(solution)/shard_map/ppermute | solution.py:34
  37.2 1.4 %collective-permute-done.8.s2 = bf16[512,128]{1,0:T(8,128)(2,1)S(1)} collective-permute-done((bf16[512,128]{1,0:T(8,128)(2,1)S(1)}, bf16[512,128]{1,0:T(8,128)(2,1)S(1)}, u32[]{:S(2)}, u32[]{:S(2)}) %collective-permute-start.8) | collective-permute-done | bytes 131104 | tf_op jit(solution)/shard_map/ppermute | solution.py:34
  38.7 7.3 %collective-permute-start.10 = (bf16[512,128]{1,0:T(8,128)(2,1)S(1)}, bf16[512,128]{1,0:T(8,128)(2,1)S(1)}, u32[]{:S(2)}, u32[]{:S(2)}) collective-permute-start(bf16[512,128]{1,0:T(8,128)(2,1)S(1)} %get-tuple-element.36.after), channel_id=1, source_target_pairs={{0,32},{8,40},{16,48},{24,56},{32,0},{40,8},{48,16},{56,24},{64,96... | collective-permute-start | bytes 393224 | tf_op jit(solution)/shard_map/ppermute | solution.py:38
  45.9 3.3 %collective-permute-done.10.crossed = bf16[512,128]{1,0:T(8,128)(2,1)S(1)} collective-permute-done((bf16[512,128]{1,0:T(8,128)(2,1)S(1)}, bf16[512,128]{1,0:T(8,128)(2,1)S(1)}, u32[]{:S(2)}, u32[]{:S(2)}) %collective-permute-start.10) | collective-permute-done | bytes 131104 | tf_op jit(solution)/shard_map/ppermute | solution.py:38
  49.3 2.7 %collective-permute-start.11 = (bf16[512,128]{1,0:T(8,128)(2,1)S(1)}, bf16[512,128]{1,0:T(8,128)(2,1)S(1)}, u32[]{:S(2)}, u32[]{:S(2)}) collective-permute-start(bf16[512,128]{1,0:T(8,128)(2,1)S(1)} %get-tuple-element.39), channel_id=1, source_target_pairs={{0,24},{1,193},{2,26},{3,195},{4,28},{5,197},{6,30},{7,199},{8,0},... | collective-permute-start | bytes 393224 | tf_op jit(solution)/shard_map/ppermute | solution.py:34
  52.0 1.5 %collective-permute-start.12 = (bf16[512,128]{1,0:T(8,128)(2,1)S(1)}, bf16[512,128]{1,0:T(8,128)(2,1)S(1)}, u32[]{:S(2)}, u32[]{:S(2)}) collective-permute-start(bf16[512,128]{1,0:T(8,128)(2,1)S(1)} %get-tuple-element.39), channel_id=1, source_target_pairs={{0,16},{1,129},{2,18},{3,131},{4,20},{5,133},{6,22},{7,135},{8,24}... | collective-permute-start | bytes 393224 | tf_op jit(solution)/shard_map/ppermute | solution.py:34
  53.6 2.5 %collective-permute-start.13 = (bf16[512,128]{1,0:T(8,128)(2,1)S(1)}, bf16[512,128]{1,0:T(8,128)(2,1)S(1)}, u32[]{:S(2)}, u32[]{:S(2)}) collective-permute-start(bf16[512,128]{1,0:T(8,128)(2,1)S(1)} %get-tuple-element.39), channel_id=1, source_target_pairs={{0,8},{1,65},{2,10},{3,67},{4,12},{5,69},{6,14},{7,71},{8,16},{9,7... | collective-permute-start | bytes 393224 | tf_op jit(solution)/shard_map/ppermute | solution.py:34
  56.1 3.4 %collective-permute-done.12 = bf16[512,128]{1,0:T(8,128)(2,1)S(1)} collective-permute-done((bf16[512,128]{1,0:T(8,128)(2,1)S(1)}, bf16[512,128]{1,0:T(8,128)(2,1)S(1)}, u32[]{:S(2)}, u32[]{:S(2)}) %collective-permute-start.12) | collective-permute-done | bytes 131104 | tf_op jit(solution)/shard_map/ppermute | solution.py:34
  59.5 5.2 %collective-permute-done.13 = bf16[512,128]{1,0:T(8,128)(2,1)S(1)} collective-permute-done((bf16[512,128]{1,0:T(8,128)(2,1)S(1)}, bf16[512,128]{1,0:T(8,128)(2,1)S(1)}, u32[]{:S(2)}, u32[]{:S(2)}) %collective-permute-start.13) | collective-permute-done | bytes 131104 | tf_op jit(solution)/shard_map/ppermute | solution.py:34
  64.8 0.4 collective-permute-start.19
  65.2 1.3 %collective-permute-start.17 = (bf16[4,512,128]{2,1,0:T(8,128)(2,1)S(1)}, bf16[4,512,128]{2,1,0:T(8,128)(2,1)S(1)}, u32[]{:S(2)}, u32[]{:S(2)}) collective-permute-start(bf16[4,512,128]{2,1,0:T(8,128)(2,1)S(1)} %pad_maximum_fusion.piece), channel_id=1, source_target_pairs={{0,192},{1,25},{2,194},{3,27},{4,196},{5,29},{6,198},{7,31},{8,200... | collective-permute-start | bytes 1572872 | tf_op jit(solution)/shard_map/ppermute | solution.py:34
  66.5 0.7 collective-permute-start.15
  67.2 0.1 collective-permute-start.21
  67.3 0.5 collective-permute-start.14
  67.8 7.8 %collective-permute-done.19.piece = bf16[4,512,128]{2,1,0:T(8,128)(2,1)S(1)} collective-permute-done((bf16[4,512,128]{2,1,0:T(8,128)(2,1)S(1)}, bf16[4,512,128]{2,1,0:T(8,128)(2,1)S(1)}, u32[]{:S(2)}, u32[]{:S(2)}) %collective-permute-start.19) | collective-permute-done | bytes 524320 | tf_op jit(solution)/shard_map/ppermute | solution.py:34
  75.7 0.1 collective-permute-start.20
  75.8 3.4 %collective-permute-done.17.piece = bf16[4,512,128]{2,1,0:T(8,128)(2,1)S(1)} collective-permute-done((bf16[4,512,128]{2,1,0:T(8,128)(2,1)S(1)}, bf16[4,512,128]{2,1,0:T(8,128)(2,1)S(1)}, u32[]{:S(2)}, u32[]{:S(2)}) %collective-permute-start.17) | collective-permute-done | bytes 524320 | tf_op jit(solution)/shard_map/ppermute | solution.py:34
  79.3 5.0 %shard_map.89 = (bf16[4,512,1024]{2,1,0:T(8,128)(2,1)S(1)}, bf16[4,512,1024]{2,1,0:T(8,128)(2,1)S(1)}, bf16[4,512,1024]{2,1,0:T(8,128)(2,1)S(1)}, bf16[4,512,1024]{2,1,0:T(8,128)(2,1)S(1)}) custom-call(s32[32]{0:T(128)S(1)} %plan.1.table, s32[4,32]{1,0:T(4,128)S(1)} %copy-done.1, bf16[4,32,256,128]{3,2,1,0:T(8,128)(2,1)S(1)} %bitcast.6, ...), custom_call_target="tpu_custom_call" | custom-call | flops 2147483648 | bytes 1048576 | tf_op jit(solution)/shard_map/pallas_call | solution.py:310
  84.3 0.8 shard_map.88
  85.1 0.6 collective-permute-start.16
  85.7 1.3 %shard_map.94.refs_1_.refs_2_ = f32[4,256,512]{2,1,0:T(8,128)S(1)} custom-call(bf16[4,512,1024]{2,1,0:T(8,128)(2,1)S(1)} %get-tuple-element.48.weights, bf16[4,512,128]{2,1,0:T(8,128)(2,1)S(1)} %pad_maximum_fusion.piece, bf16[4,256,128]{2,1,0:T(8,128)(2,1)S(1)} %collective-permute-done.21.refs_0_, f32[8,128]{1,0:T(8,128)S(1)} %get-tuple-element.49.refs_1_), custom_call_target="tpu_custom_call" | custom-call | flops 1073741824 | bytes 1048576 | tf_op jit(solution)/shard_map/pallas_call | solution.py:351
  87.0 1.3 %shard_map.95.refs_1_.refs_2_ = f32[4,256,512]{2,1,0:T(8,128)S(1)} custom-call(bf16[4,512,1024]{2,1,0:T(8,128)(2,1)S(1)} %get-tuple-element.47.weights, bf16[4,512,128]{2,1,0:T(8,128)(2,1)S(1)} %collective-permute-done.19.piece, bf16[4,256,128]{2,1,0:T(8,128)(2,1)S(1)} %collective-permute-done.20.refs_0_, f32[4,256,512]{2,1,0:T(8,128)S(1)} %shard_map.94.refs_1_.refs_2_, ...), custom_call_target="tpu_custom_call" | custom-call | flops 1073741824 | bytes 1048576 | tf_op jit(solution)/shard_map/pallas_call | solution.py:351
  88.4 1.3 %shard_map.96.refs_0_.refs_1_ = f32[4,256,512]{2,1,0:T(8,128)S(1)} custom-call(bf16[4,512,1024]{2,1,0:T(8,128)(2,1)S(1)} %get-tuple-element.46.weights, bf16[4,512,128]{2,1,0:T(8,128)(2,1)S(1)} %collective-permute-done.17.piece, bf16[4,256,128]{2,1,0:T(8,128)(2,1)S(1)} %collective-permute-done.18.refs_0_, f32[4,256,512]{2,1,0:T(8,128)S(1)} %shard_map.95.refs_1_.refs_2_, ...), custom_call_target="tpu_custom_call" | custom-call | flops 1073741824 | bytes 1048576 | tf_op jit(solution)/shard_map/pallas_call | solution.py:351
  89.7 0.8 shard_map.97.before
  90.5 1.7 %leave.1 = f32[4,256,512]{2,1,0:T(8,128)} custom-call(bf16[4,512,1024]{2,1,0:T(8,128)(2,1)S(1)} %get-tuple-element.42.weights, bf16[4,256,128]{2,1,0:T(8,128)(2,1)S(1)} %collective-permute-done.16.got, f32[4,256,512]{2,1,0:T(8,128)S(1)} %shard_map.97.before), custom_call_target="tpu_custom_call" | custom-call | flops 268435456 | bytes 1048576 | tf_op jit(solution)/shard_map/leave/pallas_call | solution.py:368
  (35 shorter events, 0.5 us)
Async XLA Ops:
  0.6 0.7 copy-start.4
  0.6 1.6 %copy-start.2 = (f32[4,2,128,512]{3,2,1,0:T(8,128)S(1)}, f32[4,2,128,512]{3,2,1,0:T(8,128)}, u32[]{:S(2)}) copy-start(f32[4,2,128,512]{3,2,1,0:T(8,128)} %updates.1) | copy-start | bytes 6291460
  0.6 1.6 %copy-start.3 = (s32[4]{0:T(128)S(1)}, s32[4]{0:T(128)}, u32[]{:S(2)}) copy-start(s32[4]{0:T(128)} %ids.1) | copy-start | bytes 52
  0.7 2.8 %slice-start = ((s8[8388608]{0:T(1024)(128)(4,1)}), s8[4194304]{0:T(1024)(128)(4,1)S(1)}, s32[]{:S(2)}) async-start(s8[8388608]{0:T(1024)(128)(4,1)} %bitcast.5), calls=%async_computation | async-start | bytes 8388608
  2.2 2.7 %slice-start.1 = ((s8[8388608]{0:T(1024)(128)(4,1)}), s8[4194304]{0:T(1024)(128)(4,1)S(1)}, s32[]{:S(2)}) async-start(s8[8388608]{0:T(1024)(128)(4,1)} %bitcast.5), calls=%async_computation.1 | async-start | bytes 8388608
  2.2 2.7 %copy-start.1 = (s32[4,32]{1,0:T(4,128)S(1)}, s32[4,32]{1,0:T(4,128)}, u32[]{:S(2)}) copy-start(s32[4,32]{1,0:T(4,128)} %starts.11) | copy-start | bytes 1540
  2.9 3.8 %collective-permute-start = (bf16[4,256,512]{2,1,0:T(8,128)(2,1)S(1)}, bf16[4,256,512]{2,1,0:T(8,128)(2,1)S(1)}, u32[]{:S(2)}, u32[]{:S(2)}) collective-permute-start(bf16[4,256,512]{2,1,0:T(8,128)(2,1)S(1)} %shard_map.77.scaled), channel_id=1, source_target_pairs={{0,1},{1,0},{2,3},{3,2},{4,5},{5,4},{6,7},{7,6},{8,9},{9,8},{10,11... | collective-permute-start | bytes 3145736 | tf_op jit(solution)/shard_map/ppermute | solution.py:42
  11.2 7.1 %copy-start = (f32[128,2,128]{2,1,0:T(2,128)S(1)}, f32[128,2,128]{2,1,0:T(2,128)}, u32[]{:S(2)}) copy-start(f32[128,2,128]{2,1,0:T(2,128)} %volume.1) | copy-start | bytes 393220
  11.2 15.4 %collective-permute-start.6 = (bf16[4,512,128]{2,1,0:T(8,128)(2,1)S(1)}, bf16[4,512,128]{2,1,0:T(8,128)(2,1)S(1)}, u32[]{:S(2)}, u32[]{:S(2)}) collective-permute-start(bf16[4,512,128]{2,1,0:T(8,128)(2,1)S(1)} %shard_map.81.after), channel_id=1, source_target_pairs={{0,192},{1,25},{2,194},{3,27},{4,196},{5,29},{6,198},{7,31},{8,200... | collective-permute-start | bytes 1572872 | tf_op jit(solution)/shard_map/ppermute | solution.py:34
  14.3 16.0 %collective-permute-start.5 = (bf16[4,512,128]{2,1,0:T(8,128)(2,1)S(1)}, bf16[4,512,128]{2,1,0:T(8,128)(2,1)S(1)}, u32[]{:S(2)}, u32[]{:S(2)}) collective-permute-start(bf16[4,512,128]{2,1,0:T(8,128)(2,1)S(1)} %shard_map.80.after), channel_id=1, source_target_pairs={{0,64},{1,9},{2,66},{3,11},{4,68},{5,13},{6,70},{7,15},{8,72},{9,1... | collective-permute-start | bytes 1572872 | tf_op jit(solution)/shard_map/ppermute | solution.py:34
  14.3 16.0 %collective-permute-start.4 = (bf16[4,512,128]{2,1,0:T(8,128)(2,1)S(1)}, bf16[4,512,128]{2,1,0:T(8,128)(2,1)S(1)}, u32[]{:S(2)}, u32[]{:S(2)}) collective-permute-start(bf16[4,512,128]{2,1,0:T(8,128)(2,1)S(1)} %shard_map.79.after), channel_id=1, source_target_pairs={{0,128},{1,17},{2,130},{3,19},{4,132},{5,21},{6,134},{7,23},{8,136... | collective-permute-start | bytes 1572872 | tf_op jit(solution)/shard_map/ppermute | solution.py:34
  18.5 1.2 %collective-permute-start.1 = (f32[2,128]{1,0:T(2,128)S(1)}, f32[2,128]{1,0:T(2,128)S(1)}, u32[]{:S(2)}, u32[]{:S(2)}) collective-permute-start(f32[2,128]{1,0:T(2,128)S(1)} %get-tuple-element.29), channel_id=1, source_target_pairs={{0,1},{1,0},{2,3},{3,2},{4,5},{5,4},{6,7},{7,6},{8,9},{9,8},{10,11... | collective-permute-start | bytes 3080 | tf_op jit(solution)/shard_map/ppermute | solution.py:42
  18.6 1.2 %collective-permute-start.2 = (f32[2,128]{1,0:T(2,128)S(1)}, f32[2,128]{1,0:T(2,128)S(1)}, u32[]{:S(2)}, u32[]{:S(2)}) collective-permute-start(f32[2,128]{1,0:T(2,128)S(1)} %get-tuple-element.30), channel_id=1, source_target_pairs={{1,2},{2,1},{3,4},{4,3},{5,6},{6,5},{9,10},{10,9},{11,12},{12,11},... | collective-permute-start | bytes 3080 | tf_op jit(solution)/shard_map/ppermute | solution.py:399
  19.8 15.0 %collective-permute-start.3 = (f32[256,128]{1,0:T(8,128)S(1)}, f32[256,128]{1,0:T(8,128)S(1)}, u32[]{:S(2)}, u32[]{:S(2)}) collective-permute-start(f32[256,128]{1,0:T(8,128)S(1)} %shard_map.84.smooth), channel_id=1, source_target_pairs={{0,1},{1,0},{2,3},{3,2},{4,5},{5,4},{6,7},{7,6},{8,9},{9,8},{10,11... | collective-permute-start | bytes 393224 | tf_op jit(solution)/shard_map/ppermute | solution.py:42
  30.5 6.6 %collective-permute-start.7 = (bf16[512,128]{1,0:T(8,128)(2,1)S(1)}, bf16[512,128]{1,0:T(8,128)(2,1)S(1)}, u32[]{:S(2)}, u32[]{:S(2)}) collective-permute-start(bf16[512,128]{1,0:T(8,128)(2,1)S(1)} %get-tuple-element.32), channel_id=1, source_target_pairs={{0,16},{1,129},{2,18},{3,131},{4,20},{5,133},{6,22},{7,135},{8,24}... | collective-permute-start | bytes 393224 | tf_op jit(solution)/shard_map/ppermute | solution.py:34
  32.7 5.8 %collective-permute-start.8 = (bf16[512,128]{1,0:T(8,128)(2,1)S(1)}, bf16[512,128]{1,0:T(8,128)(2,1)S(1)}, u32[]{:S(2)}, u32[]{:S(2)}) collective-permute-start(bf16[512,128]{1,0:T(8,128)(2,1)S(1)} %get-tuple-element.33), channel_id=1, source_target_pairs={{0,8},{1,65},{2,10},{3,67},{4,12},{5,69},{6,14},{7,71},{8,16},{9,7... | collective-permute-start | bytes 393224 | tf_op jit(solution)/shard_map/ppermute | solution.py:34
  32.7 5.8 %collective-permute-start.9 = (bf16[512,128]{1,0:T(8,128)(2,1)S(1)}, bf16[512,128]{1,0:T(8,128)(2,1)S(1)}, u32[]{:S(2)}, u32[]{:S(2)}) collective-permute-start(bf16[512,128]{1,0:T(8,128)(2,1)S(1)} %get-tuple-element.34), channel_id=1, source_target_pairs={{0,24},{1,193},{2,26},{3,195},{4,28},{5,197},{6,30},{7,199},{8,0},... | collective-permute-start | bytes 393224 | tf_op jit(solution)/shard_map/ppermute | solution.py:34
  38.7 10.6 %collective-permute-start.10 = (bf16[512,128]{1,0:T(8,128)(2,1)S(1)}, bf16[512,128]{1,0:T(8,128)(2,1)S(1)}, u32[]{:S(2)}, u32[]{:S(2)}) collective-permute-start(bf16[512,128]{1,0:T(8,128)(2,1)S(1)} %get-tuple-element.36.after), channel_id=1, source_target_pairs={{0,32},{8,40},{16,48},{24,56},{32,0},{40,8},{48,16},{56,24},{64,96... | collective-permute-start | bytes 393224 | tf_op jit(solution)/shard_map/ppermute | solution.py:38
  49.3 6.8 %collective-permute-start.11 = (bf16[512,128]{1,0:T(8,128)(2,1)S(1)}, bf16[512,128]{1,0:T(8,128)(2,1)S(1)}, u32[]{:S(2)}, u32[]{:S(2)}) collective-permute-start(bf16[512,128]{1,0:T(8,128)(2,1)S(1)} %get-tuple-element.39), channel_id=1, source_target_pairs={{0,24},{1,193},{2,26},{3,195},{4,28},{5,197},{6,30},{7,199},{8,0},... | collective-permute-start | bytes 393224 | tf_op jit(solution)/shard_map/ppermute | solution.py:34
  52.0 7.5 %collective-permute-start.12 = (bf16[512,128]{1,0:T(8,128)(2,1)S(1)}, bf16[512,128]{1,0:T(8,128)(2,1)S(1)}, u32[]{:S(2)}, u32[]{:S(2)}) collective-permute-start(bf16[512,128]{1,0:T(8,128)(2,1)S(1)} %get-tuple-element.39), channel_id=1, source_target_pairs={{0,16},{1,129},{2,18},{3,131},{4,20},{5,133},{6,22},{7,135},{8,24}... | collective-permute-start | bytes 393224 | tf_op jit(solution)/shard_map/ppermute | solution.py:34
  53.6 11.2 %collective-permute-start.13 = (bf16[512,128]{1,0:T(8,128)(2,1)S(1)}, bf16[512,128]{1,0:T(8,128)(2,1)S(1)}, u32[]{:S(2)}, u32[]{:S(2)}) collective-permute-start(bf16[512,128]{1,0:T(8,128)(2,1)S(1)} %get-tuple-element.39), channel_id=1, source_target_pairs={{0,8},{1,65},{2,10},{3,67},{4,12},{5,69},{6,14},{7,71},{8,16},{9,7... | collective-permute-start | bytes 393224 | tf_op jit(solution)/shard_map/ppermute | solution.py:34
  64.8 10.9 %collective-permute-start.19 = (bf16[4,512,128]{2,1,0:T(8,128)(2,1)S(1)}, bf16[4,512,128]{2,1,0:T(8,128)(2,1)S(1)}, u32[]{:S(2)}, u32[]{:S(2)}) collective-permute-start(bf16[4,512,128]{2,1,0:T(8,128)(2,1)S(1)} %pad_maximum_fusion.piece), channel_id=1, source_target_pairs={{0,128},{1,17},{2,130},{3,19},{4,132},{5,21},{6,134},{7,23},{8,136... | collective-permute-start | bytes 1572872 | tf_op jit(solution)/shard_map/ppermute | solution.py:34
  65.2 14.0 %collective-permute-start.17 = (bf16[4,512,128]{2,1,0:T(8,128)(2,1)S(1)}, bf16[4,512,128]{2,1,0:T(8,128)(2,1)S(1)}, u32[]{:S(2)}, u32[]{:S(2)}) collective-permute-start(bf16[4,512,128]{2,1,0:T(8,128)(2,1)S(1)} %pad_maximum_fusion.piece), channel_id=1, source_target_pairs={{0,192},{1,25},{2,194},{3,27},{4,196},{5,29},{6,198},{7,31},{8,200... | collective-permute-start | bytes 1572872 | tf_op jit(solution)/shard_map/ppermute | solution.py:34
  66.5 18.6 %collective-permute-start.15 = (bf16[4,512,128]{2,1,0:T(8,128)(2,1)S(1)}, bf16[4,512,128]{2,1,0:T(8,128)(2,1)S(1)}, u32[]{:S(2)}, u32[]{:S(2)}) collective-permute-start(bf16[4,512,128]{2,1,0:T(8,128)(2,1)S(1)} %pad_maximum_fusion.piece), channel_id=1, source_target_pairs={{0,64},{1,9},{2,66},{3,11},{4,68},{5,13},{6,70},{7,15},{8,72},{9,1... | collective-permute-start | bytes 1572872 | tf_op jit(solution)/shard_map/ppermute | solution.py:34
  67.2 18.5 %collective-permute-start.21 = (bf16[4,256,128]{2,1,0:T(8,128)(2,1)S(1)}, bf16[4,256,128]{2,1,0:T(8,128)(2,1)S(1)}, u32[]{:S(2)}, u32[]{:S(2)}) collective-permute-start(bf16[4,256,128]{2,1,0:T(8,128)(2,1)S(1)} %shard_map.93), channel_id=1, source_target_pairs={{0,1},{1,0},{2,3},{3,2},{4,5},{5,4},{6,7},{7,6},{8,9},{9,8},{10,11... | collective-permute-start | bytes 786440 | tf_op jit(solution)/shard_map/ppermute | solution.py:42
  67.3 17.0 %collective-permute-start.14 = (f32[256,128]{1,0:T(8,128)S(1)}, f32[256,128]{1,0:T(8,128)S(1)}, u32[]{:S(2)}, u32[]{:S(2)}) collective-permute-start(f32[256,128]{1,0:T(8,128)S(1)} %get-tuple-element.40), channel_id=1, source_target_pairs={{0,1},{1,0},{2,3},{3,2},{4,5},{5,4},{6,7},{7,6},{8,9},{9,8},{10,11... | collective-permute-start | bytes 393224 | tf_op jit(solution)/shard_map/ppermute | solution.py:42
  75.7 11.4 %collective-permute-start.20 = (bf16[4,256,128]{2,1,0:T(8,128)(2,1)S(1)}, bf16[4,256,128]{2,1,0:T(8,128)(2,1)S(1)}, u32[]{:S(2)}, u32[]{:S(2)}) collective-permute-start(bf16[4,256,128]{2,1,0:T(8,128)(2,1)S(1)} %shard_map.92), channel_id=1, source_target_pairs={{0,1},{1,0},{2,3},{3,2},{4,5},{5,4},{6,7},{7,6},{8,9},{9,8},{10,11... | collective-permute-start | bytes 786440 | tf_op jit(solution)/shard_map/ppermute | solution.py:42
  79.2 9.2 %collective-permute-start.18 = (bf16[4,256,128]{2,1,0:T(8,128)(2,1)S(1)}, bf16[4,256,128]{2,1,0:T(8,128)(2,1)S(1)}, u32[]{:S(2)}, u32[]{:S(2)}) collective-permute-start(bf16[4,256,128]{2,1,0:T(8,128)(2,1)S(1)} %shard_map.91), channel_id=1, source_target_pairs={{0,1},{1,0},{2,3},{3,2},{4,5},{5,4},{6,7},{7,6},{8,9},{9,8},{10,11... | collective-permute-start | bytes 786440 | tf_op jit(solution)/shard_map/ppermute | solution.py:42
  85.1 5.3 %collective-permute-start.16 = (bf16[4,256,128]{2,1,0:T(8,128)(2,1)S(1)}, bf16[4,256,128]{2,1,0:T(8,128)(2,1)S(1)}, u32[]{:S(2)}, u32[]{:S(2)}) collective-permute-start(bf16[4,256,128]{2,1,0:T(8,128)(2,1)S(1)} %shard_map.90), channel_id=1, source_target_pairs={{0,1},{1,0},{2,3},{3,2},{4,5},{5,4},{6,7},{7,6},{8,9},{9,8},{10,11... | collective-permute-start | bytes 786440 | tf_op jit(solution)/shard_map/ppermute | solution.py:42

commit v5 on v4

--- a/solution.py
+++ b/solution.py
@@ -280,7 +280,7 @@
     return call(turn_kernel, [VMEM] * 2, outs, 1 << 20, 4)(own, received)
 
 
-GROUPS = (0, *FAR)
+COLUMNS = (((0, 0), (1, 0)), ((0, 2), (1, 2)), ((0, 1), (0, 3)), ((1, 1), (1, 3)))
 
 
 def spread_kernel(table, starts, tiles, after, *outs):
@@ -288,10 +288,10 @@
     zeros = jnp.zeros((block, block), tiles.dtype)
 
     def angle(a, carry):
-        for out, d in zip(outs, GROUPS):
+        for out, groups in zip(outs, COLUMNS):
             for i in range(2 * LINE):
-                half, k = divmod(i, LINE)
-                j = table[half * len(ORDER) * LINE + place(d) + k]
+                half, d = groups[i // LINE]
+                j = table[half * len(ORDER) * LINE + place(d) + i % LINE]
                 first = starts[a, j]
                 column = slice(i * block, (i + 1) * block)
                 for empty in (jnp.where(first == 0, 2, 0), jnp.where(first == 2, 1, 3)):
@@ -306,7 +306,7 @@
 
 def spread(tiles, table, starts, detector, after):
     angles, _, _, block = tiles.shape
-    outs = [((angles, detector, 2 * LINE * block), tiles.dtype)] * len(GROUPS)
+    outs = [((angles, detector, 2 * LINE * block), tiles.dtype)] * len(COLUMNS)
     return call(spread_kernel, [SMEM, SMEM, VMEM, ANY], outs, 1 << 31, 16)(
         table, starts, tiles, after
     )
@@ -329,52 +329,48 @@
     )
 
 
-def image_kernel(chained, whole, weights, piece, *refs):
+def image_kernel(chained, weights, one, two, *refs):
     *refs, after, image = refs
-    blocks = [piece[k, : piece.shape[1] // 2, :] for k in range(LINE)]
-    if whole:
-        blocks += [refs[0][k] for k in range(LINE)]
-    depth = sum(block.shape[1] for block in blocks)
+    rows = image.shape[1]
+    blocks = [piece[k, :rows, :] for piece in (one, two) for k in range(LINE)]
     for a in range(image.shape[0]):
-        value = projected(blocks, weights[a, :, :depth])
-        image[a] = refs[-1][a] + value if chained else value
-
-
-def imaged(weights, piece, got, before, after):
+        value = projected(blocks, weights[a])
+        image[a] = refs[0][a] + value if chained else value
+
+
+def imaged(weights, one, two, before, after):
     angles, detector, _ = weights.shape
-    rows = piece.shape[1] // 2
-    more = [v for v in (got, before) if v is not None]
+    rows = one.shape[1] // 2
+    more = [] if before is None else [before]
     outs = [((angles, rows, detector), jnp.float32)]
-    flops = weights.size * rows * (1 if got is None else 2)
-    kernel = functools.partial(image_kernel, before is not None, got is not None)
-    specs = [VMEM] * (2 + len(more)) + [ANY]
-    return call(kernel, specs, outs, flops)(weights, piece, *more, after)[0]
-
-
-def leave_kernel(weights, got, before, out, image, done):
-    blocks = [got[k] for k in range(LINE)]
-    depth = sum(block.shape[1] for block in blocks)
+    kernel = functools.partial(image_kernel, before is not None)
+    specs = [VMEM] * (3 + len(more)) + [ANY]
+    return call(kernel, specs, outs, 2 * weights.size * rows)(weights, one, two, *more, after)[0]
+
+
+def leave_kernel(weights, one, two, before, out, image, done):
+    blocks = [piece[k] for piece in (one, two) for k in range(LINE)]
     copies = []
     for a in range(image.shape[0]):
-        image[a] = before[a] + projected(blocks, weights[a, :, depth:])
+        image[a] = before[a] + projected(blocks, weights[a])
         copies.append(pltpu.make_async_copy(image.at[a], out.at[a], done.at[a]))
         copies[-1].start()
     for copy in copies:
         copy.wait()
 
 
-def leave(weights, got, before):
+def leave(weights, one, two, before):
     shape = before.shape
     return pl.pallas_call(
         leave_kernel,
-        in_specs=[VMEM] * 3,
+        in_specs=[VMEM] * 4,
         out_specs=ANY,
         out_shape=jax.ShapeDtypeStruct(shape, jnp.float32),
         scratch_shapes=[pltpu.VMEM(shape, jnp.float32), pltpu.SemaphoreType.DMA((shape[0],))],
         compiler_params=params(16),
-        cost_estimate=pl.CostEstimate(flops=1 << 28, bytes_accessed=1 << 20, transcendentals=0),
+        cost_estimate=pl.CostEstimate(flops=1 << 29, bytes_accessed=1 << 20, transcendentals=0),
         name="leave",
-    )(weights, got, before)
+    )(weights, one, two, before)
 
 
 def steps(updates, tiles, starts, ids, weights, volume):
@@ -405,7 +401,7 @@
         reached.append(moved(passed[d - 1], False, d))
     mine, message = merged(smooth, beside, kept, reached)
     crossed = across(message)
-    bands = dict(zip(GROUPS, spread(tiles, table, starts, detector, message)))
+    bands = spread(tiles, table, starts, detector, message)
     own, beside, lowered = finished(mine, crossed)
 
     came = {}
@@ -419,13 +415,13 @@
         pieces[d] = moved(pieces[0], True, LINE - d)
     received = swapped(beside)
     volume_next, token = turned(own, received, volume.shape)
-    image, last = None, token
-    for d in GROUPS:
-        got = swapped(cut(pieces[d]))
-        whole = None if d == FAR[-1] else got
-        image = imaged(bands[d], pieces[d], whole, image, last)
-        last = image
-    projection = leave(bands[FAR[-1]], got, image)
+    got = {}
+    for d in (0, *FAR):
+        got[d] = swapped(cut(pieces[d]))
+    image = imaged(bands[0], pieces[0], got[0], None, token)
+    image = imaged(bands[1], pieces[2], got[2], image, image)
+    image = imaged(bands[2], pieces[1], pieces[3], image, image)
+    projection = leave(bands[3], got[1], got[3], image)
     return volume_next, projection.reshape(angles, 2, depth, detector)
 
 

time: 93.6 us -> 93.3 us (level)
  the two profiles are of different devices: /device:TPU:2 before, /device:TPU:1 now
where the time goes in v5:
time: 93.3 us; the launch traced here: 93.1 us
  starting transfers between devices  51.7 us (55%)
  Pallas kernels  22 us (24%)
  waiting for transfers between devices  17.4 us (19%)
  between operations  1.06 us (1%)
    ppermute x8, starting transfers between devices, swapped(): return lax.ppermute(value, 'slab', [(i, i ^ 1) for i in range(SLABS)])  26.3 us
    ppermute x12, starting transfers between devices, moved(): return lax.ppermute(value, ('ang', 'slab'), pairs)  15 us
    ppermute x12, waiting for transfers between devices, moved(): return lax.ppermute(value, ('ang', 'slab'), pairs)  12.8 us
    ppermute x1, starting transfers between devices, across(): lax.ppermute(value, 'ang', [(a, a ^ XS) for a in range(YS * ZS * XS)])  6.98 us
    pallas_call x1, Pallas kernels, spread(): call(spread_kernel, [SMEM, SMEM, VMEM, ANY], outs, 1 << 31, 16)  5.11 us
    pallas_call x3, Pallas kernels, imaged(): call(kernel, specs, outs, 2 * weights.size * rows)  3.93 us
    pallas_call x2, Pallas kernels, both_rows(): call(kernel, specs, [((LINE, rows, block), dtype)], flops)  3.66 us
    ppermute x1, starting transfers between devices, steps(): lax.ppermute(outer, 'slab', [p for i in odd for p in ((i, i + 1), (i + 1,...  3.44 us
  transfers between devices with their start and end apart: 22, of which 9 were waited for; matrix products, arithmetic and copies ran while one was open for 0% of the time, Pallas kernels for 15%

profile of v5, /device:TPU:1, one launch (start us, length us, event | category | flops | bytes accessed | tf_op | source)
XLA Modules:
  0.0 93.1 jit_solution(16821039328597882188)
XLA Ops:
  0.7 0.7 plan.1.table
  1.4 0.9 copy-done.2
  2.2 0.7 shard_map.77.scaled
  2.9 3.3 %collective-permute-start = (bf16[4,256,512]{2,1,0:T(8,128)(2,1)S(1)}, bf16[4,256,512]{2,1,0:T(8,128)(2,1)S(1)}, u32[]{:S(2)}, u32[]{:S(2)}) collective-permute-start(bf16[4,256,512]{2,1,0:T(8,128)(2,1)S(1)} %shard_map.77.scaled), channel_id=1, source_target_pairs={{0,1},{1,0},{2,3},{3,2},{4,5},{5,4},{6,7},{7,6},{8,9},{9,8},{10,11... | collective-permute-start | bytes 3145736 | tf_op jit(solution)/shard_map/ppermute | solution.py:42
  6.2 1.8 %shard_map.78 = (bf16[4,256,128]{2,1,0:T(8,128)(2,1)S(1)}, bf16[4,256,128]{2,1,0:T(8,128)(2,1)S(1)}) custom-call(s32[32]{0:T(128)S(1)} %plan.1.table, s32[4,32]{1,0:T(4,128)S(1)} %copy-done.1, bf16[4,256,512]{2,1,0:T(8,128)(2,1)S(1)} %shard_map.77.scaled, bf16[4,32,256,128]{3,2,1,0:T(8,128)(2,1)S(1)} %bitcast.6), custom_call_target="tpu_custom_call" | custom-call | flops 536870912 | bytes 1048576 | tf_op jit(solution)/shard_map/pallas_call | solution.py:153
  8.1 0.4 collective-permute-done.other
  8.5 1.3 %shard_map.79.after = bf16[4,512,128]{2,1,0:T(8,128)(2,1)S(1)} custom-call(s32[32]{0:T(128)S(1)} %plan.1.table, s32[4,32]{1,0:T(4,128)S(1)} %copy-done.1, bf16[4,256,512]{2,1,0:T(8,128)(2,1)S(1)} %collective-permute-done.other, bf16[4,32,256,128]{3,2,1,0:T(8,128)(2,1)S(1)} %bitcast.6, bf16[4,256,128]{2,1,0:T(8,128)(2,1)S(1)} %get-tuple-element.27.own, ...), custom_call_target="tpu_custom_call" | custom-call | flops 268435456 | bytes 1048576 | tf_op jit(solution)/shard_map/pallas_call | solution.py:173
  9.8 1.3 %shard_map.80.after = bf16[4,512,128]{2,1,0:T(8,128)(2,1)S(1)} custom-call(s32[32]{0:T(128)S(1)} %plan.1.table, s32[4,32]{1,0:T(4,128)S(1)} %copy-done.1, bf16[4,256,512]{2,1,0:T(8,128)(2,1)S(1)} %collective-permute-done.other, bf16[4,32,256,128]{3,2,1,0:T(8,128)(2,1)S(1)} %bitcast.6, bf16[4,256,128]{2,1,0:T(8,128)(2,1)S(1)} %get-tuple-element.26.after.own, ...), custom_call_target="tpu_custom_call" | custom-call | flops 268435456 | bytes 1048576 | tf_op jit(solution)/shard_map/pallas_call | solution.py:173
  11.1 1.8 %shard_map.81.after = bf16[4,512,128]{2,1,0:T(8,128)(2,1)S(1)} custom-call(s32[32]{0:T(128)S(1)} %plan.1.table, s32[4,32]{1,0:T(4,128)S(1)} %copy-done.1, bf16[4,256,512]{2,1,0:T(8,128)(2,1)S(1)} %shard_map.77.scaled, bf16[4,256,512]{2,1,0:T(8,128)(2,1)S(1)} %collective-permute-done.other, bf16[4,32,256,128]{3,2,1,0:T(8,128)(2,1)S(1)} %bitcast.6, ...), custom_call_target="tpu_custom_call" | custom-call | flops 536870912 | bytes 1048576 | tf_op jit(solution)/shard_map/pallas_call | solution.py:188
  12.9 1.7 %collective-permute-start.6 = (bf16[4,512,128]{2,1,0:T(8,128)(2,1)S(1)}, bf16[4,512,128]{2,1,0:T(8,128)(2,1)S(1)}, u32[]{:S(2)}, u32[]{:S(2)}) collective-permute-start(bf16[4,512,128]{2,1,0:T(8,128)(2,1)S(1)} %shard_map.81.after), channel_id=1, source_target_pairs={{0,192},{1,25},{2,194},{3,27},{4,196},{5,29},{6,198},{7,31},{8,200... | collective-permute-start | bytes 1572872 | tf_op jit(solution)/shard_map/ppermute | solution.py:34
  14.6 1.7 %collective-permute-start.4 = (bf16[4,512,128]{2,1,0:T(8,128)(2,1)S(1)}, bf16[4,512,128]{2,1,0:T(8,128)(2,1)S(1)}, u32[]{:S(2)}, u32[]{:S(2)}) collective-permute-start(bf16[4,512,128]{2,1,0:T(8,128)(2,1)S(1)} %shard_map.79.after), channel_id=1, source_target_pairs={{0,128},{1,17},{2,130},{3,19},{4,132},{5,21},{6,134},{7,23},{8,136... | collective-permute-start | bytes 1572872 | tf_op jit(solution)/shard_map/ppermute | solution.py:34
  16.3 1.8 %shard_map.82.after.own = f32[4,512,128]{2,1,0:T(8,128)S(1)} custom-call(s32[32]{0:T(128)S(1)} %plan.1.table, s32[4,32]{1,0:T(4,128)S(1)} %copy-done.1, bf16[4,256,512]{2,1,0:T(8,128)(2,1)S(1)} %shard_map.77.scaled, bf16[4,256,512]{2,1,0:T(8,128)(2,1)S(1)} %collective-permute-done.other, bf16[4,32,256,128]{3,2,1,0:T(8,128)(2,1)S(1)} %bitcast.6, ...), custom_call_target="tpu_custom_call" | custom-call | flops 536870912 | bytes 1048576 | tf_op jit(solution)/shard_map/pallas_call | solution.py:188
  18.1 0.1 shard_map.83
  18.3 1.8 %collective-permute-start.1 = (f32[2,128]{1,0:T(2,128)S(1)}, f32[2,128]{1,0:T(2,128)S(1)}, u32[]{:S(2)}, u32[]{:S(2)}) collective-permute-start(f32[2,128]{1,0:T(2,128)S(1)} %get-tuple-element.29), channel_id=1, source_target_pairs={{0,1},{1,0},{2,3},{3,2},{4,5},{5,4},{6,7},{7,6},{8,9},{9,8},{10,11... | collective-permute-start | bytes 3080 | tf_op jit(solution)/shard_map/ppermute | solution.py:42
  20.1 3.4 %collective-permute-start.2 = (f32[2,128]{1,0:T(2,128)S(1)}, f32[2,128]{1,0:T(2,128)S(1)}, u32[]{:S(2)}, u32[]{:S(2)}) collective-permute-start(f32[2,128]{1,0:T(2,128)S(1)} %get-tuple-element.30), channel_id=1, source_target_pairs={{1,2},{2,1},{3,4},{4,3},{5,6},{6,5},{9,10},{10,9},{11,12},{12,11},... | collective-permute-start | bytes 3080 | tf_op jit(solution)/shard_map/ppermute | solution.py:395
  23.5 1.7 %collective-permute-done.2.outer = f32[2,128]{1,0:T(2,128)S(1)} collective-permute-done((f32[2,128]{1,0:T(2,128)S(1)}, f32[2,128]{1,0:T(2,128)S(1)}, u32[]{:S(2)}, u32[]{:S(2)}) %collective-permute-start.2) | collective-permute-done | bytes 1056 | tf_op jit(solution)/shard_map/ppermute | solution.py:395
  25.3 0.1 collective-permute-start.3
  25.4 1.0 %collective-permute-done.6.s3 = bf16[4,512,128]{2,1,0:T(8,128)(2,1)S(1)} collective-permute-done((bf16[4,512,128]{2,1,0:T(8,128)(2,1)S(1)}, bf16[4,512,128]{2,1,0:T(8,128)(2,1)S(1)}, u32[]{:S(2)}, u32[]{:S(2)}) %collective-permute-start.6) | collective-permute-done | bytes 524320 | tf_op jit(solution)/shard_map/ppermute | solution.py:34
  26.3 3.4 %collective-permute-done.5.s2 = bf16[4,512,128]{2,1,0:T(8,128)(2,1)S(1)} collective-permute-done((bf16[4,512,128]{2,1,0:T(8,128)(2,1)S(1)}, bf16[4,512,128]{2,1,0:T(8,128)(2,1)S(1)}, u32[]{:S(2)}, u32[]{:S(2)}) %collective-permute-start.5) | collective-permute-done | bytes 524320 | tf_op jit(solution)/shard_map/ppermute | solution.py:34
  29.8 0.2 shard_map.85
  30.0 2.7 %collective-permute-start.7 = (bf16[512,128]{1,0:T(8,128)(2,1)S(1)}, bf16[512,128]{1,0:T(8,128)(2,1)S(1)}, u32[]{:S(2)}, u32[]{:S(2)}) collective-permute-start(bf16[512,128]{1,0:T(8,128)(2,1)S(1)} %get-tuple-element.32), channel_id=1, source_target_pairs={{0,16},{1,129},{2,18},{3,131},{4,20},{5,133},{6,22},{7,135},{8,24}... | collective-permute-start | bytes 393224 | tf_op jit(solution)/shard_map/ppermute | solution.py:34
  32.7 0.4 collective-permute-start.8
  33.1 2.3 %collective-permute-start.9 = (bf16[512,128]{1,0:T(8,128)(2,1)S(1)}, bf16[512,128]{1,0:T(8,128)(2,1)S(1)}, u32[]{:S(2)}, u32[]{:S(2)}) collective-permute-start(bf16[512,128]{1,0:T(8,128)(2,1)S(1)} %get-tuple-element.34), channel_id=1, source_target_pairs={{0,24},{1,193},{2,26},{3,195},{4,28},{5,197},{6,30},{7,199},{8,0},... | collective-permute-start | bytes 393224 | tf_op jit(solution)/shard_map/ppermute | solution.py:34
  35.4 0.0 collective-permute-done.7.s1
  35.4 2.6 %collective-permute-done.8.s2 = bf16[512,128]{1,0:T(8,128)(2,1)S(1)} collective-permute-done((bf16[512,128]{1,0:T(8,128)(2,1)S(1)}, bf16[512,128]{1,0:T(8,128)(2,1)S(1)}, u32[]{:S(2)}, u32[]{:S(2)}) %collective-permute-start.8) | collective-permute-done | bytes 131104 | tf_op jit(solution)/shard_map/ppermute | solution.py:34
  38.0 0.1 shard_map.86
  38.1 7.0 %collective-permute-start.10 = (bf16[512,128]{1,0:T(8,128)(2,1)S(1)}, bf16[512,128]{1,0:T(8,128)(2,1)S(1)}, u32[]{:S(2)}, u32[]{:S(2)}) collective-permute-start(bf16[512,128]{1,0:T(8,128)(2,1)S(1)} %get-tuple-element.36.after), channel_id=1, source_target_pairs={{0,32},{8,40},{16,48},{24,56},{32,0},{40,8},{48,16},{56,24},{64,96... | collective-permute-start | bytes 393224 | tf_op jit(solution)/shard_map/ppermute | solution.py:38
  45.1 2.5 %collective-permute-done.10.crossed = bf16[512,128]{1,0:T(8,128)(2,1)S(1)} collective-permute-done((bf16[512,128]{1,0:T(8,128)(2,1)S(1)}, bf16[512,128]{1,0:T(8,128)(2,1)S(1)}, u32[]{:S(2)}, u32[]{:S(2)}) %collective-permute-start.10) | collective-permute-done | bytes 131104 | tf_op jit(solution)/shard_map/ppermute | solution.py:38
  47.6 3.9 %collective-permute-start.11 = (bf16[512,128]{1,0:T(8,128)(2,1)S(1)}, bf16[512,128]{1,0:T(8,128)(2,1)S(1)}, u32[]{:S(2)}, u32[]{:S(2)}) collective-permute-start(bf16[512,128]{1,0:T(8,128)(2,1)S(1)} %get-tuple-element.39), channel_id=1, source_target_pairs={{0,24},{1,193},{2,26},{3,195},{4,28},{5,197},{6,30},{7,199},{8,0},... | collective-permute-start | bytes 393224 | tf_op jit(solution)/shard_map/ppermute | solution.py:34
  51.5 0.7 collective-permute-start.13
  52.2 2.6 %collective-permute-done.11 = bf16[512,128]{1,0:T(8,128)(2,1)S(1)} collective-permute-done((bf16[512,128]{1,0:T(8,128)(2,1)S(1)}, bf16[512,128]{1,0:T(8,128)(2,1)S(1)}, u32[]{:S(2)}, u32[]{:S(2)}) %collective-permute-start.11) | collective-permute-done | bytes 131104 | tf_op jit(solution)/shard_map/ppermute | solution.py:34
  54.8 2.1 %collective-permute-done.12 = bf16[512,128]{1,0:T(8,128)(2,1)S(1)} collective-permute-done((bf16[512,128]{1,0:T(8,128)(2,1)S(1)}, bf16[512,128]{1,0:T(8,128)(2,1)S(1)}, u32[]{:S(2)}, u32[]{:S(2)}) %collective-permute-start.12) | collective-permute-done | bytes 131104 | tf_op jit(solution)/shard_map/ppermute | solution.py:34
  56.9 1.0 %collective-permute-done.13 = bf16[512,128]{1,0:T(8,128)(2,1)S(1)} collective-permute-done((bf16[512,128]{1,0:T(8,128)(2,1)S(1)}, bf16[512,128]{1,0:T(8,128)(2,1)S(1)}, u32[]{:S(2)}, u32[]{:S(2)}) %collective-permute-start.13) | collective-permute-done | bytes 131104 | tf_op jit(solution)/shard_map/ppermute | solution.py:34
  57.9 0.1 pad_maximum_fusion.piece.one
  58.0 0.1 collective-permute-start.19
  58.1 0.1 collective-permute-start.15
  58.2 1.5 %collective-permute-start.17 = (bf16[4,512,128]{2,1,0:T(8,128)(2,1)S(1)}, bf16[4,512,128]{2,1,0:T(8,128)(2,1)S(1)}, u32[]{:S(2)}, u32[]{:S(2)}) collective-permute-start(bf16[4,512,128]{2,1,0:T(8,128)(2,1)S(1)} %pad_maximum_fusion.piece.one), channel_id=1, source_target_pairs={{0,64},{1,9},{2,66},{3,11},{4,68},{5,13},{6,70},{7,15},{8,72},{9,1... | collective-permute-start | bytes 1572872 | tf_op jit(solution)/shard_map/ppermute | solution.py:34
  59.7 11.9 %collective-permute-start.21 = (bf16[4,256,128]{2,1,0:T(8,128)(2,1)S(1)}, bf16[4,256,128]{2,1,0:T(8,128)(2,1)S(1)}, u32[]{:S(2)}, u32[]{:S(2)}) collective-permute-start(bf16[4,256,128]{2,1,0:T(8,128)(2,1)S(1)} %shard_map.93), channel_id=1, source_target_pairs={{0,1},{1,0},{2,3},{3,2},{4,5},{5,4},{6,7},{7,6},{8,9},{9,8},{10,11... | collective-permute-start | bytes 786440 | tf_op jit(solution)/shard_map/ppermute | solution.py:42
  71.5 0.1 collective-permute-start.14
  71.6 8.5 %collective-permute-start.20 = (bf16[4,256,128]{2,1,0:T(8,128)(2,1)S(1)}, bf16[4,256,128]{2,1,0:T(8,128)(2,1)S(1)}, u32[]{:S(2)}, u32[]{:S(2)}) collective-permute-start(bf16[4,256,128]{2,1,0:T(8,128)(2,1)S(1)} %shard_map.92), channel_id=1, source_target_pairs={{0,1},{1,0},{2,3},{3,2},{4,5},{5,4},{6,7},{7,6},{8,9},{9,8},{10,11... | collective-permute-start | bytes 786440 | tf_op jit(solution)/shard_map/ppermute | solution.py:42
  80.2 5.1 %shard_map.89 = (bf16[4,512,1024]{2,1,0:T(8,128)(2,1)S(1)}, bf16[4,512,1024]{2,1,0:T(8,128)(2,1)S(1)}, bf16[4,512,1024]{2,1,0:T(8,128)(2,1)S(1)}, bf16[4,512,1024]{2,1,0:T(8,128)(2,1)S(1)}) custom-call(s32[32]{0:T(128)S(1)} %plan.1.table, s32[4,32]{1,0:T(4,128)S(1)} %copy-done.1, bf16[4,32,256,128]{3,2,1,0:T(8,128)(2,1)S(1)} %bitcast.6, ...), custom_call_target="tpu_custom_call" | custom-call | flops 2147483648 | bytes 1048576 | tf_op jit(solution)/shard_map/pallas_call | solution.py:310
  85.3 0.8 shard_map.88
  86.1 0.1 collective-permute-start.16
  86.3 0.6 collective-permute-start.18
  86.9 1.3 %shard_map.94.refs_0_.refs_1_ = f32[4,256,512]{2,1,0:T(8,128)S(1)} custom-call(bf16[4,512,1024]{2,1,0:T(8,128)(2,1)S(1)} %get-tuple-element.48.weights, bf16[4,512,128]{2,1,0:T(8,128)(2,1)S(1)} %pad_maximum_fusion.piece.one, bf16[4,256,128]{2,1,0:T(8,128)(2,1)S(1)} %collective-permute-done.21.two, f32[8,128]{1,0:T(8,128)S(1)} %get-tuple-element.49.refs_0_), custom_call_target="tpu_custom_call" | custom-call | flops 1073741824 | bytes 1048576 | tf_op jit(solution)/shard_map/pallas_call | solution.py:348
  88.2 1.3 %shard_map.95.refs_0_.refs_1_ = f32[4,256,512]{2,1,0:T(8,128)S(1)} custom-call(bf16[4,512,1024]{2,1,0:T(8,128)(2,1)S(1)} %get-tuple-element.47.weights, bf16[4,512,128]{2,1,0:T(8,128)(2,1)S(1)} %collective-permute-done.19.piece.one, bf16[4,256,128]{2,1,0:T(8,128)(2,1)S(1)} %collective-permute-done.20.two, f32[4,256,512]{2,1,0:T(8,128)S(1)} %shard_map.94.refs_0_.refs_1_, ...), custom_call_target="tpu_custom_call" | custom-call | flops 1073741824 | bytes 1048576 | tf_op jit(solution)/shard_map/pallas_call | solution.py:348
  89.5 1.3 %shard_map.96.before = f32[4,256,512]{2,1,0:T(8,128)S(1)} custom-call(bf16[4,512,1024]{2,1,0:T(8,128)(2,1)S(1)} %get-tuple-element.46.weights, bf16[4,512,128]{2,1,0:T(8,128)(2,1)S(1)} %collective-permute-done.15.piece.one, bf16[4,512,128]{2,1,0:T(8,128)(2,1)S(1)} %collective-permute-done.17.piece.two, f32[4,256,512]{2,1,0:T(8,128)S(1)} %shard_map.95.refs_0_.refs_1_, ...), custom_call_target="tpu_custom_call" | custom-call | flops 1073741824 | bytes 1048576 | tf_op jit(solution)/shard_map/pallas_call | solution.py:348
  90.8 2.1 %leave.1 = f32[4,256,512]{2,1,0:T(8,128)} custom-call(bf16[4,512,1024]{2,1,0:T(8,128)(2,1)S(1)} %get-tuple-element.42.weights, bf16[4,256,128]{2,1,0:T(8,128)(2,1)S(1)} %collective-permute-done.16.one, bf16[4,256,128]{2,1,0:T(8,128)(2,1)S(1)} %collective-permute-done.18.two, f32[4,256,512]{2,1,0:T(8,128)S(1)} %shard_map.96.before), custom_call_target="tpu_custom_call" | custom-call | flops 536870912 | bytes 1048576 | tf_op jit(solution)/shard_map/leave/pallas_call | solution.py:364
  (34 shorter events, 0.2 us)
Async XLA Ops:
  0.6 0.7 copy-start.4
  0.6 1.6 %copy-start.2 = (f32[4,2,128,512]{3,2,1,0:T(8,128)S(1)}, f32[4,2,128,512]{3,2,1,0:T(8,128)}, u32[]{:S(2)}) copy-start(f32[4,2,128,512]{3,2,1,0:T(8,128)} %updates.1) | copy-start | bytes 6291460
  0.6 1.6 %copy-start.3 = (s32[4]{0:T(128)S(1)}, s32[4]{0:T(128)}, u32[]{:S(2)}) copy-start(s32[4]{0:T(128)} %ids.1) | copy-start | bytes 52
  0.7 5.5 %slice-start = ((s8[8388608]{0:T(1024)(128)(4,1)}), s8[4194304]{0:T(1024)(128)(4,1)S(1)}, s32[]{:S(2)}) async-start(s8[8388608]{0:T(1024)(128)(4,1)} %bitcast.5), calls=%async_computation | async-start | bytes 8388608
  2.2 4.0 %slice-start.1 = ((s8[8388608]{0:T(1024)(128)(4,1)}), s8[4194304]{0:T(1024)(128)(4,1)S(1)}, s32[]{:S(2)}) async-start(s8[8388608]{0:T(1024)(128)(4,1)} %bitcast.5), calls=%async_computation.1 | async-start | bytes 8388608
  2.2 4.0 %copy-start.1 = (s32[4,32]{1,0:T(4,128)S(1)}, s32[4,32]{1,0:T(4,128)}, u32[]{:S(2)}) copy-start(s32[4,32]{1,0:T(4,128)} %starts.11) | copy-start | bytes 1540
  2.9 5.6 %collective-permute-start = (bf16[4,256,512]{2,1,0:T(8,128)(2,1)S(1)}, bf16[4,256,512]{2,1,0:T(8,128)(2,1)S(1)}, u32[]{:S(2)}, u32[]{:S(2)}) collective-permute-start(bf16[4,256,512]{2,1,0:T(8,128)(2,1)S(1)} %shard_map.77.scaled), channel_id=1, source_target_pairs={{0,1},{1,0},{2,3},{3,2},{4,5},{5,4},{6,7},{7,6},{8,9},{9,8},{10,11... | collective-permute-start | bytes 3145736 | tf_op jit(solution)/shard_map/ppermute | solution.py:42
  12.9 5.2 %copy-start = (f32[128,2,128]{2,1,0:T(2,128)S(1)}, f32[128,2,128]{2,1,0:T(2,128)}, u32[]{:S(2)}) copy-start(f32[128,2,128]{2,1,0:T(2,128)} %volume.1) | copy-start | bytes 393220
  12.9 13.4 %collective-permute-start.6 = (bf16[4,512,128]{2,1,0:T(8,128)(2,1)S(1)}, bf16[4,512,128]{2,1,0:T(8,128)(2,1)S(1)}, u32[]{:S(2)}, u32[]{:S(2)}) collective-permute-start(bf16[4,512,128]{2,1,0:T(8,128)(2,1)S(1)} %shard_map.81.after), channel_id=1, source_target_pairs={{0,192},{1,25},{2,194},{3,27},{4,196},{5,29},{6,198},{7,31},{8,200... | collective-permute-start | bytes 1572872 | tf_op jit(solution)/shard_map/ppermute | solution.py:34
  14.6 15.2 %collective-permute-start.5 = (bf16[4,512,128]{2,1,0:T(8,128)(2,1)S(1)}, bf16[4,512,128]{2,1,0:T(8,128)(2,1)S(1)}, u32[]{:S(2)}, u32[]{:S(2)}) collective-permute-start(bf16[4,512,128]{2,1,0:T(8,128)(2,1)S(1)} %shard_map.80.after), channel_id=1, source_target_pairs={{0,64},{1,9},{2,66},{3,11},{4,68},{5,13},{6,70},{7,15},{8,72},{9,1... | collective-permute-start | bytes 1572872 | tf_op jit(solution)/shard_map/ppermute | solution.py:34
  14.6 15.2 %collective-permute-start.4 = (bf16[4,512,128]{2,1,0:T(8,128)(2,1)S(1)}, bf16[4,512,128]{2,1,0:T(8,128)(2,1)S(1)}, u32[]{:S(2)}, u32[]{:S(2)}) collective-permute-start(bf16[4,512,128]{2,1,0:T(8,128)(2,1)S(1)} %shard_map.79.after), channel_id=1, source_target_pairs={{0,128},{1,17},{2,130},{3,19},{4,132},{5,21},{6,134},{7,23},{8,136... | collective-permute-start | bytes 1572872 | tf_op jit(solution)/shard_map/ppermute | solution.py:34
  18.3 5.2 %collective-permute-start.1 = (f32[2,128]{1,0:T(2,128)S(1)}, f32[2,128]{1,0:T(2,128)S(1)}, u32[]{:S(2)}, u32[]{:S(2)}) collective-permute-start(f32[2,128]{1,0:T(2,128)S(1)} %get-tuple-element.29), channel_id=1, source_target_pairs={{0,1},{1,0},{2,3},{3,2},{4,5},{5,4},{6,7},{7,6},{8,9},{9,8},{10,11... | collective-permute-start | bytes 3080 | tf_op jit(solution)/shard_map/ppermute | solution.py:42
  20.1 5.2 %collective-permute-start.2 = (f32[2,128]{1,0:T(2,128)S(1)}, f32[2,128]{1,0:T(2,128)S(1)}, u32[]{:S(2)}, u32[]{:S(2)}) collective-permute-start(f32[2,128]{1,0:T(2,128)S(1)} %get-tuple-element.30), channel_id=1, source_target_pairs={{1,2},{2,1},{3,4},{4,3},{5,6},{6,5},{9,10},{10,9},{11,12},{12,11},... | collective-permute-start | bytes 3080 | tf_op jit(solution)/shard_map/ppermute | solution.py:395
  25.3 10.1 %collective-permute-start.3 = (f32[256,128]{1,0:T(8,128)S(1)}, f32[256,128]{1,0:T(8,128)S(1)}, u32[]{:S(2)}, u32[]{:S(2)}) collective-permute-start(f32[256,128]{1,0:T(8,128)S(1)} %shard_map.84.smooth), channel_id=1, source_target_pairs={{0,1},{1,0},{2,3},{3,2},{4,5},{5,4},{6,7},{7,6},{8,9},{9,8},{10,11... | collective-permute-start | bytes 393224 | tf_op jit(solution)/shard_map/ppermute | solution.py:42
  30.0 5.4 %collective-permute-start.7 = (bf16[512,128]{1,0:T(8,128)(2,1)S(1)}, bf16[512,128]{1,0:T(8,128)(2,1)S(1)}, u32[]{:S(2)}, u32[]{:S(2)}) collective-permute-start(bf16[512,128]{1,0:T(8,128)(2,1)S(1)} %get-tuple-element.32), channel_id=1, source_target_pairs={{0,16},{1,129},{2,18},{3,131},{4,20},{5,133},{6,22},{7,135},{8,24}... | collective-permute-start | bytes 393224 | tf_op jit(solution)/shard_map/ppermute | solution.py:34
  32.7 5.3 %collective-permute-start.8 = (bf16[512,128]{1,0:T(8,128)(2,1)S(1)}, bf16[512,128]{1,0:T(8,128)(2,1)S(1)}, u32[]{:S(2)}, u32[]{:S(2)}) collective-permute-start(bf16[512,128]{1,0:T(8,128)(2,1)S(1)} %get-tuple-element.33), channel_id=1, source_target_pairs={{0,8},{1,65},{2,10},{3,67},{4,12},{5,69},{6,14},{7,71},{8,16},{9,7... | collective-permute-start | bytes 393224 | tf_op jit(solution)/shard_map/ppermute | solution.py:34
  33.1 4.9 %collective-permute-start.9 = (bf16[512,128]{1,0:T(8,128)(2,1)S(1)}, bf16[512,128]{1,0:T(8,128)(2,1)S(1)}, u32[]{:S(2)}, u32[]{:S(2)}) collective-permute-start(bf16[512,128]{1,0:T(8,128)(2,1)S(1)} %get-tuple-element.34), channel_id=1, source_target_pairs={{0,24},{1,193},{2,26},{3,195},{4,28},{5,197},{6,30},{7,199},{8,0},... | collective-permute-start | bytes 393224 | tf_op jit(solution)/shard_map/ppermute | solution.py:34
  38.1 9.4 %collective-permute-start.10 = (bf16[512,128]{1,0:T(8,128)(2,1)S(1)}, bf16[512,128]{1,0:T(8,128)(2,1)S(1)}, u32[]{:S(2)}, u32[]{:S(2)}) collective-permute-start(bf16[512,128]{1,0:T(8,128)(2,1)S(1)} %get-tuple-element.36.after), channel_id=1, source_target_pairs={{0,32},{8,40},{16,48},{24,56},{32,0},{40,8},{48,16},{56,24},{64,96... | collective-permute-start | bytes 393224 | tf_op jit(solution)/shard_map/ppermute | solution.py:38
  47.6 7.2 %collective-permute-start.11 = (bf16[512,128]{1,0:T(8,128)(2,1)S(1)}, bf16[512,128]{1,0:T(8,128)(2,1)S(1)}, u32[]{:S(2)}, u32[]{:S(2)}) collective-permute-start(bf16[512,128]{1,0:T(8,128)(2,1)S(1)} %get-tuple-element.39), channel_id=1, source_target_pairs={{0,24},{1,193},{2,26},{3,195},{4,28},{5,197},{6,30},{7,199},{8,0},... | collective-permute-start | bytes 393224 | tf_op jit(solution)/shard_map/ppermute | solution.py:34
  51.5 5.4 %collective-permute-start.12 = (bf16[512,128]{1,0:T(8,128)(2,1)S(1)}, bf16[512,128]{1,0:T(8,128)(2,1)S(1)}, u32[]{:S(2)}, u32[]{:S(2)}) collective-permute-start(bf16[512,128]{1,0:T(8,128)(2,1)S(1)} %get-tuple-element.39), channel_id=1, source_target_pairs={{0,16},{1,129},{2,18},{3,131},{4,20},{5,133},{6,22},{7,135},{8,24}... | collective-permute-start | bytes 393224 | tf_op jit(solution)/shard_map/ppermute | solution.py:34
  51.5 6.4 %collective-permute-start.13 = (bf16[512,128]{1,0:T(8,128)(2,1)S(1)}, bf16[512,128]{1,0:T(8,128)(2,1)S(1)}, u32[]{:S(2)}, u32[]{:S(2)}) collective-permute-start(bf16[512,128]{1,0:T(8,128)(2,1)S(1)} %get-tuple-element.39), channel_id=1, source_target_pairs={{0,8},{1,65},{2,10},{3,67},{4,12},{5,69},{6,14},{7,71},{8,16},{9,7... | collective-permute-start | bytes 393224 | tf_op jit(solution)/shard_map/ppermute | solution.py:34
  58.0 13.6 %collective-permute-start.19 = (bf16[4,512,128]{2,1,0:T(8,128)(2,1)S(1)}, bf16[4,512,128]{2,1,0:T(8,128)(2,1)S(1)}, u32[]{:S(2)}, u32[]{:S(2)}) collective-permute-start(bf16[4,512,128]{2,1,0:T(8,128)(2,1)S(1)} %pad_maximum_fusion.piece.one), channel_id=1, source_target_pairs={{0,128},{1,17},{2,130},{3,19},{4,132},{5,21},{6,134},{7,23},{8,136... | collective-permute-start | bytes 1572872 | tf_op jit(solution)/shard_map/ppermute | solution.py:34
  58.1 28.0 %collective-permute-start.15 = (bf16[4,512,128]{2,1,0:T(8,128)(2,1)S(1)}, bf16[4,512,128]{2,1,0:T(8,128)(2,1)S(1)}, u32[]{:S(2)}, u32[]{:S(2)}) collective-permute-start(bf16[4,512,128]{2,1,0:T(8,128)(2,1)S(1)} %pad_maximum_fusion.piece.one), channel_id=1, source_target_pairs={{0,192},{1,25},{2,194},{3,27},{4,196},{5,29},{6,198},{7,31},{8,200... | collective-permute-start | bytes 1572872 | tf_op jit(solution)/shard_map/ppermute | solution.py:34
  58.2 28.1 %collective-permute-start.17 = (bf16[4,512,128]{2,1,0:T(8,128)(2,1)S(1)}, bf16[4,512,128]{2,1,0:T(8,128)(2,1)S(1)}, u32[]{:S(2)}, u32[]{:S(2)}) collective-permute-start(bf16[4,512,128]{2,1,0:T(8,128)(2,1)S(1)} %pad_maximum_fusion.piece.one), channel_id=1, source_target_pairs={{0,64},{1,9},{2,66},{3,11},{4,68},{5,13},{6,70},{7,15},{8,72},{9,1... | collective-permute-start | bytes 1572872 | tf_op jit(solution)/shard_map/ppermute | solution.py:34
  59.7 27.2 %collective-permute-start.21 = (bf16[4,256,128]{2,1,0:T(8,128)(2,1)S(1)}, bf16[4,256,128]{2,1,0:T(8,128)(2,1)S(1)}, u32[]{:S(2)}, u32[]{:S(2)}) collective-permute-start(bf16[4,256,128]{2,1,0:T(8,128)(2,1)S(1)} %shard_map.93), channel_id=1, source_target_pairs={{0,1},{1,0},{2,3},{3,2},{4,5},{5,4},{6,7},{7,6},{8,9},{9,8},{10,11... | collective-permute-start | bytes 786440 | tf_op jit(solution)/shard_map/ppermute | solution.py:42
  71.5 13.8 %collective-permute-start.14 = (f32[256,128]{1,0:T(8,128)S(1)}, f32[256,128]{1,0:T(8,128)S(1)}, u32[]{:S(2)}, u32[]{:S(2)}) collective-permute-start(f32[256,128]{1,0:T(8,128)S(1)} %get-tuple-element.40), channel_id=1, source_target_pairs={{0,1},{1,0},{2,3},{3,2},{4,5},{5,4},{6,7},{7,6},{8,9},{9,8},{10,11... | collective-permute-start | bytes 393224 | tf_op jit(solution)/shard_map/ppermute | solution.py:42
  71.6 16.5 %collective-permute-start.20 = (bf16[4,256,128]{2,1,0:T(8,128)(2,1)S(1)}, bf16[4,256,128]{2,1,0:T(8,128)(2,1)S(1)}, u32[]{:S(2)}, u32[]{:S(2)}) collective-permute-start(bf16[4,256,128]{2,1,0:T(8,128)(2,1)S(1)} %shard_map.92), channel_id=1, source_target_pairs={{0,1},{1,0},{2,3},{3,2},{4,5},{5,4},{6,7},{7,6},{8,9},{9,8},{10,11... | collective-permute-start | bytes 786440 | tf_op jit(solution)/shard_map/ppermute | solution.py:42
  86.1 4.7 %collective-permute-start.16 = (bf16[4,256,128]{2,1,0:T(8,128)(2,1)S(1)}, bf16[4,256,128]{2,1,0:T(8,128)(2,1)S(1)}, u32[]{:S(2)}, u32[]{:S(2)}) collective-permute-start(bf16[4,256,128]{2,1,0:T(8,128)(2,1)S(1)} %shard_map.90), channel_id=1, source_target_pairs={{0,1},{1,0},{2,3},{3,2},{4,5},{5,4},{6,7},{7,6},{8,9},{9,8},{10,11... | collective-permute-start | bytes 786440 | tf_op jit(solution)/shard_map/ppermute | solution.py:42
  86.3 4.5 %collective-permute-start.18 = (bf16[4,256,128]{2,1,0:T(8,128)(2,1)S(1)}, bf16[4,256,128]{2,1,0:T(8,128)(2,1)S(1)}, u32[]{:S(2)}, u32[]{:S(2)}) collective-permute-start(bf16[4,256,128]{2,1,0:T(8,128)(2,1)S(1)} %shard_map.91), channel_id=1, source_target_pairs={{0,1},{1,0},{2,3},{3,2},{4,5},{5,4},{6,7},{7,6},{8,9},{9,8},{10,11... | collective-permute-start | bytes 786440 | tf_op jit(solution)/shard_map/ppermute | solution.py:42

commit v6 on v5

--- a/solution.py
+++ b/solution.py
@@ -312,14 +312,19 @@
     )
 
 
-def cut_kernel(piece, out):
-    out[...] = piece[:, out.shape[1] :, :]
-
-
-def cut(piece):
-    count, rows, block = piece.shape
-    outs = [((count, rows // 2, block), piece.dtype)]
-    return call(cut_kernel, [VMEM], outs, 1 << 18, 4)(piece)[0]
+def cut_kernel(*refs):
+    *parts, out = refs
+    at = 0
+    for part in parts:
+        count = part.shape[0]
+        out[at : at + count] = part[:, out.shape[1] :, :]
+        at += count
+
+
+def cut(parts):
+    _, rows, block = parts[0].shape
+    outs = [((LINE, rows // 2, block), parts[0].dtype)]
+    return call(cut_kernel, [VMEM] * len(parts), outs, 1 << 18, 4)(*parts)[0]
 
 
 def projected(blocks, weights):
@@ -329,23 +334,24 @@
     )
 
 
-def image_kernel(chained, weights, one, two, *refs):
+def image_kernel(chained, weights, *refs):
     *refs, after, image = refs
+    *parts, before = refs if chained else (*refs, None)
     rows = image.shape[1]
-    blocks = [piece[k, :rows, :] for piece in (one, two) for k in range(LINE)]
+    blocks = [part[k, :rows, :] for part in parts for k in range(part.shape[0])]
     for a in range(image.shape[0]):
         value = projected(blocks, weights[a])
-        image[a] = refs[0][a] + value if chained else value
-
-
-def imaged(weights, one, two, before, after):
+        image[a] = before[a] + value if chained else value
+
+
+def imaged(weights, parts, before, after):
     angles, detector, _ = weights.shape
-    rows = one.shape[1] // 2
+    rows = parts[0].shape[1] // 2
     more = [] if before is None else [before]
     outs = [((angles, rows, detector), jnp.float32)]
     kernel = functools.partial(image_kernel, before is not None)
-    specs = [VMEM] * (3 + len(more)) + [ANY]
-    return call(kernel, specs, outs, 2 * weights.size * rows)(weights, one, two, *more, after)[0]
+    specs = [VMEM] * (1 + len(parts) + len(more)) + [ANY]
+    return call(kernel, specs, outs, 2 * weights.size * rows)(weights, *parts, *more, after)[0]
 
 
 def leave_kernel(weights, one, two, before, out, image, done):
@@ -407,20 +413,26 @@
     came = {}
     for d in FAR:
         came[d] = moved(lowered, False, LINE - d)
+    early = {}
+    for d in FAR[1:]:
+        early[d] = moved(lowered, True, LINE - d)
     beside, came[1], came[2], came[3] = lax.optimization_barrier(
         (beside, came[1], came[2], came[3])
     )
-    pieces = {0: jnp.stack([lowered] + [came[d] for d in range(1, LINE)])}
+    short = [came[d] for d in range(1, LINE)]
+    line, rest = jnp.stack([lowered, *short]), jnp.stack(short)
+    pieces = {0: [line]}
     for d in FAR:
-        pieces[d] = moved(pieces[0], True, LINE - d)
+        came = moved(rest if d in early else line, True, LINE - d)
+        pieces[d] = [early[d][None], came] if d in early else [came]
     received = swapped(beside)
     volume_next, token = turned(own, received, volume.shape)
     got = {}
     for d in (0, *FAR):
         got[d] = swapped(cut(pieces[d]))
-    image = imaged(bands[0], pieces[0], got[0], None, token)
-    image = imaged(bands[1], pieces[2], got[2], image, image)
-    image = imaged(bands[2], pieces[1], pieces[3], image, image)
+    image = imaged(bands[0], [*pieces[0], got[0]], None, token)
+    image = imaged(bands[1], [*pieces[2], got[2]], image, image)
+    image = imaged(bands[2], [*pieces[1], *pieces[3]], image, image)
     projection = leave(bands[3], got[1], got[3], image)
     return volume_next, projection.reshape(angles, 2, depth, detector)
 

time: 93.3 us -> 99.8 us (1.070)
  starting transfers between devices: 51.7 us -> 58.1 us
    ppermute x8, starting transfers between devices: 26.3 us -> 31.4 us  [swapped(): return lax.ppermute(value, 'slab', [(i, i ^ 1) for i in range(SLABS)])]
    ppermute x12 -> x14, starting transfers between devices: 15 us -> 16.3 us  [moved(): return lax.ppermute(value, ('ang', 'slab'), pairs)]
    ppermute x12 -> x14, waiting for transfers between devices: 12.8 us -> 12.8 us  [moved(): return lax.ppermute(value, ('ang', 'slab'), pairs)]
  transfers between devices with their start and end apart: 22 -> 24, of which waited for: 9 -> 9; matrix products, arithmetic and copies ran while one was open for 0% -> 0% of each run, Pallas kernels for 15% -> 14%
where the time goes in v6:
time: 99.8 us; the launch traced here: 99.7 us
  starting transfers between devices  58.1 us (58%)
  Pallas kernels  22 us (22%)
  waiting for transfers between devices  17.4 us (17%)
  between operations  1.13 us (1%)
    ppermute x8, starting transfers between devices, swapped(): return lax.ppermute(value, 'slab', [(i, i ^ 1) for i in range(SLABS)])  31.4 us
    ppermute x14, starting transfers between devices, moved(): return lax.ppermute(value, ('ang', 'slab'), pairs)  16.3 us
    ppermute x14, waiting for transfers between devices, moved(): return lax.ppermute(value, ('ang', 'slab'), pairs)  12.8 us
    ppermute x1, starting transfers between devices, across(): lax.ppermute(value, 'ang', [(a, a ^ XS) for a in range(YS * ZS * XS)])  6.98 us
    pallas_call x1, Pallas kernels, spread(): call(spread_kernel, [SMEM, SMEM, VMEM, ANY], outs, 1 << 31, 16)  5.11 us
    pallas_call x3, Pallas kernels, imaged(): call(kernel, specs, outs, 2 * weights.size * rows)  3.93 us
    pallas_call x2, Pallas kernels, both_rows(): call(kernel, specs, [((LINE, rows, block), dtype)], flops)  3.66 us
    ppermute x1, starting transfers between devices, steps(): lax.ppermute(outer, 'slab', [p for i in odd for p in ((i, i + 1), (i + 1,...  3.44 us
  transfers between devices with their start and end apart: 24, of which 9 were waited for; matrix products, arithmetic and copies ran while one was open for 0% of the time, Pallas kernels for 14%

profile of v6, /device:TPU:1, one launch (start us, length us, event | category | flops | bytes accessed | tf_op | source)
XLA Modules:
  0.0 99.7 jit_solution(7624047092404550552)
XLA Ops:
  0.7 0.7 plan.1.table
  1.4 0.9 copy-done.2
  2.2 0.7 shard_map.77.scaled
  2.9 3.3 %collective-permute-start = (bf16[4,256,512]{2,1,0:T(8,128)(2,1)S(1)}, bf16[4,256,512]{2,1,0:T(8,128)(2,1)S(1)}, u32[]{:S(2)}, u32[]{:S(2)}) collective-permute-start(bf16[4,256,512]{2,1,0:T(8,128)(2,1)S(1)} %shard_map.77.scaled), channel_id=1, source_target_pairs={{0,1},{1,0},{2,3},{3,2},{4,5},{5,4},{6,7},{7,6},{8,9},{9,8},{10,11... | collective-permute-start | bytes 3145736 | tf_op jit(solution)/shard_map/ppermute | solution.py:42
  6.2 1.8 %shard_map.78 = (bf16[4,256,128]{2,1,0:T(8,128)(2,1)S(1)}, bf16[4,256,128]{2,1,0:T(8,128)(2,1)S(1)}) custom-call(s32[32]{0:T(128)S(1)} %plan.1.table, s32[4,32]{1,0:T(4,128)S(1)} %copy-done.1, bf16[4,256,512]{2,1,0:T(8,128)(2,1)S(1)} %shard_map.77.scaled, bf16[4,32,256,128]{3,2,1,0:T(8,128)(2,1)S(1)} %bitcast.8), custom_call_target="tpu_custom_call" | custom-call | flops 536870912 | bytes 1048576 | tf_op jit(solution)/shard_map/pallas_call | solution.py:153
  8.1 0.4 collective-permute-done.other
  8.5 1.3 %shard_map.79.after = bf16[4,512,128]{2,1,0:T(8,128)(2,1)S(1)} custom-call(s32[32]{0:T(128)S(1)} %plan.1.table, s32[4,32]{1,0:T(4,128)S(1)} %copy-done.1, bf16[4,256,512]{2,1,0:T(8,128)(2,1)S(1)} %collective-permute-done.other, bf16[4,32,256,128]{3,2,1,0:T(8,128)(2,1)S(1)} %bitcast.8, bf16[4,256,128]{2,1,0:T(8,128)(2,1)S(1)} %get-tuple-element.27.own, ...), custom_call_target="tpu_custom_call" | custom-call | flops 268435456 | bytes 1048576 | tf_op jit(solution)/shard_map/pallas_call | solution.py:173
  9.8 1.3 %shard_map.80.after = bf16[4,512,128]{2,1,0:T(8,128)(2,1)S(1)} custom-call(s32[32]{0:T(128)S(1)} %plan.1.table, s32[4,32]{1,0:T(4,128)S(1)} %copy-done.1, bf16[4,256,512]{2,1,0:T(8,128)(2,1)S(1)} %collective-permute-done.other, bf16[4,32,256,128]{3,2,1,0:T(8,128)(2,1)S(1)} %bitcast.8, bf16[4,256,128]{2,1,0:T(8,128)(2,1)S(1)} %get-tuple-element.26.after.own, ...), custom_call_target="tpu_custom_call" | custom-call | flops 268435456 | bytes 1048576 | tf_op jit(solution)/shard_map/pallas_call | solution.py:173
  11.1 1.8 %shard_map.81.after = bf16[4,512,128]{2,1,0:T(8,128)(2,1)S(1)} custom-call(s32[32]{0:T(128)S(1)} %plan.1.table, s32[4,32]{1,0:T(4,128)S(1)} %copy-done.1, bf16[4,256,512]{2,1,0:T(8,128)(2,1)S(1)} %shard_map.77.scaled, bf16[4,256,512]{2,1,0:T(8,128)(2,1)S(1)} %collective-permute-done.other, bf16[4,32,256,128]{3,2,1,0:T(8,128)(2,1)S(1)} %bitcast.8, ...), custom_call_target="tpu_custom_call" | custom-call | flops 536870912 | bytes 1048576 | tf_op jit(solution)/shard_map/pallas_call | solution.py:188
  12.9 1.7 %collective-permute-start.6 = (bf16[4,512,128]{2,1,0:T(8,128)(2,1)S(1)}, bf16[4,512,128]{2,1,0:T(8,128)(2,1)S(1)}, u32[]{:S(2)}, u32[]{:S(2)}) collective-permute-start(bf16[4,512,128]{2,1,0:T(8,128)(2,1)S(1)} %shard_map.81.after), channel_id=1, source_target_pairs={{0,192},{1,25},{2,194},{3,27},{4,196},{5,29},{6,198},{7,31},{8,200... | collective-permute-start | bytes 1572872 | tf_op jit(solution)/shard_map/ppermute | solution.py:34
  14.6 1.7 %collective-permute-start.4 = (bf16[4,512,128]{2,1,0:T(8,128)(2,1)S(1)}, bf16[4,512,128]{2,1,0:T(8,128)(2,1)S(1)}, u32[]{:S(2)}, u32[]{:S(2)}) collective-permute-start(bf16[4,512,128]{2,1,0:T(8,128)(2,1)S(1)} %shard_map.79.after), channel_id=1, source_target_pairs={{0,128},{1,17},{2,130},{3,19},{4,132},{5,21},{6,134},{7,23},{8,136... | collective-permute-start | bytes 1572872 | tf_op jit(solution)/shard_map/ppermute | solution.py:34
  16.3 1.8 %shard_map.82.after.own = f32[4,512,128]{2,1,0:T(8,128)S(1)} custom-call(s32[32]{0:T(128)S(1)} %plan.1.table, s32[4,32]{1,0:T(4,128)S(1)} %copy-done.1, bf16[4,256,512]{2,1,0:T(8,128)(2,1)S(1)} %shard_map.77.scaled, bf16[4,256,512]{2,1,0:T(8,128)(2,1)S(1)} %collective-permute-done.other, bf16[4,32,256,128]{3,2,1,0:T(8,128)(2,1)S(1)} %bitcast.8, ...), custom_call_target="tpu_custom_call" | custom-call | flops 536870912 | bytes 1048576 | tf_op jit(solution)/shard_map/pallas_call | solution.py:188
  18.1 0.1 shard_map.83
  18.3 1.8 %collective-permute-start.1 = (f32[2,128]{1,0:T(2,128)S(1)}, f32[2,128]{1,0:T(2,128)S(1)}, u32[]{:S(2)}, u32[]{:S(2)}) collective-permute-start(f32[2,128]{1,0:T(2,128)S(1)} %get-tuple-element.29), channel_id=1, source_target_pairs={{0,1},{1,0},{2,3},{3,2},{4,5},{5,4},{6,7},{7,6},{8,9},{9,8},{10,11... | collective-permute-start | bytes 3080 | tf_op jit(solution)/shard_map/ppermute | solution.py:42
  20.1 3.4 %collective-permute-start.2 = (f32[2,128]{1,0:T(2,128)S(1)}, f32[2,128]{1,0:T(2,128)S(1)}, u32[]{:S(2)}, u32[]{:S(2)}) collective-permute-start(f32[2,128]{1,0:T(2,128)S(1)} %get-tuple-element.30), channel_id=1, source_target_pairs={{1,2},{2,1},{3,4},{4,3},{5,6},{6,5},{9,10},{10,9},{11,12},{12,11},... | collective-permute-start | bytes 3080 | tf_op jit(solution)/shard_map/ppermute | solution.py:401
  23.5 1.7 %collective-permute-done.2.outer = f32[2,128]{1,0:T(2,128)S(1)} collective-permute-done((f32[2,128]{1,0:T(2,128)S(1)}, f32[2,128]{1,0:T(2,128)S(1)}, u32[]{:S(2)}, u32[]{:S(2)}) %collective-permute-start.2) | collective-permute-done | bytes 1056 | tf_op jit(solution)/shard_map/ppermute | solution.py:401
  25.3 0.1 collective-permute-start.3
  25.4 1.0 collective-permute-done.6.s3
  26.3 3.4 %collective-permute-done.5.s2 = bf16[4,512,128]{2,1,0:T(8,128)(2,1)S(1)} collective-permute-done((bf16[4,512,128]{2,1,0:T(8,128)(2,1)S(1)}, bf16[4,512,128]{2,1,0:T(8,128)(2,1)S(1)}, u32[]{:S(2)}, u32[]{:S(2)}) %collective-permute-start.5) | collective-permute-done | bytes 524320 | tf_op jit(solution)/shard_map/ppermute | solution.py:34
  29.8 0.2 shard_map.85
  30.0 2.7 %collective-permute-start.7 = (bf16[512,128]{1,0:T(8,128)(2,1)S(1)}, bf16[512,128]{1,0:T(8,128)(2,1)S(1)}, u32[]{:S(2)}, u32[]{:S(2)}) collective-permute-start(bf16[512,128]{1,0:T(8,128)(2,1)S(1)} %get-tuple-element.32), channel_id=1, source_target_pairs={{0,16},{1,129},{2,18},{3,131},{4,20},{5,133},{6,22},{7,135},{8,24}... | collective-permute-start | bytes 393224 | tf_op jit(solution)/shard_map/ppermute | solution.py:34
  32.7 0.4 collective-permute-start.8
  33.1 2.3 %collective-permute-start.9 = (bf16[512,128]{1,0:T(8,128)(2,1)S(1)}, bf16[512,128]{1,0:T(8,128)(2,1)S(1)}, u32[]{:S(2)}, u32[]{:S(2)}) collective-permute-start(bf16[512,128]{1,0:T(8,128)(2,1)S(1)} %get-tuple-element.34), channel_id=1, source_target_pairs={{0,24},{1,193},{2,26},{3,195},{4,28},{5,197},{6,30},{7,199},{8,0},... | collective-permute-start | bytes 393224 | tf_op jit(solution)/shard_map/ppermute | solution.py:34
  35.4 2.6 %collective-permute-done.8.s2 = bf16[512,128]{1,0:T(8,128)(2,1)S(1)} collective-permute-done((bf16[512,128]{1,0:T(8,128)(2,1)S(1)}, bf16[512,128]{1,0:T(8,128)(2,1)S(1)}, u32[]{:S(2)}, u32[]{:S(2)}) %collective-permute-start.8) | collective-permute-done | bytes 131104 | tf_op jit(solution)/shard_map/ppermute | solution.py:34
  38.0 0.1 shard_map.86
  38.1 7.0 %collective-permute-start.10 = (bf16[512,128]{1,0:T(8,128)(2,1)S(1)}, bf16[512,128]{1,0:T(8,128)(2,1)S(1)}, u32[]{:S(2)}, u32[]{:S(2)}) collective-permute-start(bf16[512,128]{1,0:T(8,128)(2,1)S(1)} %get-tuple-element.36.after), channel_id=1, source_target_pairs={{0,32},{8,40},{16,48},{24,56},{32,0},{40,8},{48,16},{56,24},{64,96... | collective-permute-start | bytes 393224 | tf_op jit(solution)/shard_map/ppermute | solution.py:38
  45.1 2.5 %collective-permute-done.10.crossed = bf16[512,128]{1,0:T(8,128)(2,1)S(1)} collective-permute-done((bf16[512,128]{1,0:T(8,128)(2,1)S(1)}, bf16[512,128]{1,0:T(8,128)(2,1)S(1)}, u32[]{:S(2)}, u32[]{:S(2)}) %collective-permute-start.10) | collective-permute-done | bytes 131104 | tf_op jit(solution)/shard_map/ppermute | solution.py:38
  47.6 3.9 %collective-permute-start.11 = (bf16[512,128]{1,0:T(8,128)(2,1)S(1)}, bf16[512,128]{1,0:T(8,128)(2,1)S(1)}, u32[]{:S(2)}, u32[]{:S(2)}) collective-permute-start(bf16[512,128]{1,0:T(8,128)(2,1)S(1)} %get-tuple-element.39), channel_id=1, source_target_pairs={{0,24},{1,193},{2,26},{3,195},{4,28},{5,197},{6,30},{7,199},{8,0},... | collective-permute-start | bytes 393224 | tf_op jit(solution)/shard_map/ppermute | solution.py:34
  51.5 0.7 collective-permute-start.13
  52.2 2.6 %collective-permute-done.11 = bf16[512,128]{1,0:T(8,128)(2,1)S(1)} collective-permute-done((bf16[512,128]{1,0:T(8,128)(2,1)S(1)}, bf16[512,128]{1,0:T(8,128)(2,1)S(1)}, u32[]{:S(2)}, u32[]{:S(2)}) %collective-permute-start.11) | collective-permute-done | bytes 131104 | tf_op jit(solution)/shard_map/ppermute | solution.py:34
  54.8 2.1 %collective-permute-done.12 = bf16[512,128]{1,0:T(8,128)(2,1)S(1)} collective-permute-done((bf16[512,128]{1,0:T(8,128)(2,1)S(1)}, bf16[512,128]{1,0:T(8,128)(2,1)S(1)}, u32[]{:S(2)}, u32[]{:S(2)}) %collective-permute-start.12) | collective-permute-done | bytes 131104 | tf_op jit(solution)/shard_map/ppermute | solution.py:34
  56.9 1.0 %collective-permute-done.13 = bf16[512,128]{1,0:T(8,128)(2,1)S(1)} collective-permute-done((bf16[512,128]{1,0:T(8,128)(2,1)S(1)}, bf16[512,128]{1,0:T(8,128)(2,1)S(1)}, u32[]{:S(2)}, u32[]{:S(2)}) %collective-permute-start.13) | collective-permute-done | bytes 131104 | tf_op jit(solution)/shard_map/ppermute | solution.py:34
  57.9 0.1 pad_maximum_fusion.refs_0_
  58.0 0.1 collective-permute-start.21
  58.1 0.1 collective-permute-start.19
  58.2 2.7 %collective-permute-start.16 = (bf16[3,512,128]{2,1,0:T(8,128)(2,1)S(1)}, bf16[3,512,128]{2,1,0:T(8,128)(2,1)S(1)}, u32[]{:S(2)}, u32[]{:S(2)}) collective-permute-start(bf16[3,512,128]{2,1,0:T(8,128)(2,1)S(1)} %pad_maximum_fusion.1), channel_id=1, source_target_pairs={{0,192},{1,25},{2,194},{3,27},{4,196},{5,29},{6,198},{7,31},{8,200... | collective-permute-start | bytes 1179656 | tf_op jit(solution)/shard_map/ppermute | solution.py:34
  60.9 12.3 %collective-permute-start.14 = (f32[256,128]{1,0:T(8,128)S(1)}, f32[256,128]{1,0:T(8,128)S(1)}, u32[]{:S(2)}, u32[]{:S(2)}) collective-permute-start(f32[256,128]{1,0:T(8,128)S(1)} %get-tuple-element.40), channel_id=1, source_target_pairs={{0,1},{1,0},{2,3},{3,2},{4,5},{5,4},{6,7},{7,6},{8,9},{9,8},{10,11... | collective-permute-start | bytes 393224 | tf_op jit(solution)/shard_map/ppermute | solution.py:42
  73.2 7.1 %collective-permute-start.23 = (bf16[4,256,128]{2,1,0:T(8,128)(2,1)S(1)}, bf16[4,256,128]{2,1,0:T(8,128)(2,1)S(1)}, u32[]{:S(2)}, u32[]{:S(2)}) collective-permute-start(bf16[4,256,128]{2,1,0:T(8,128)(2,1)S(1)} %shard_map.93), channel_id=1, source_target_pairs={{0,1},{1,0},{2,3},{3,2},{4,5},{5,4},{6,7},{7,6},{8,9},{9,8},{10,11... | collective-permute-start | bytes 786440 | tf_op jit(solution)/shard_map/ppermute | solution.py:42
  80.4 0.1 collective-permute-start.15
  80.5 6.0 %collective-permute-start.22 = (bf16[4,256,128]{2,1,0:T(8,128)(2,1)S(1)}, bf16[4,256,128]{2,1,0:T(8,128)(2,1)S(1)}, u32[]{:S(2)}, u32[]{:S(2)}) collective-permute-start(bf16[4,256,128]{2,1,0:T(8,128)(2,1)S(1)} %shard_map.92), channel_id=1, source_target_pairs={{0,1},{1,0},{2,3},{3,2},{4,5},{5,4},{6,7},{7,6},{8,9},{9,8},{10,11... | collective-permute-start | bytes 786440 | tf_op jit(solution)/shard_map/ppermute | solution.py:42
  86.5 5.1 %shard_map.89 = (bf16[4,512,1024]{2,1,0:T(8,128)(2,1)S(1)}, bf16[4,512,1024]{2,1,0:T(8,128)(2,1)S(1)}, bf16[4,512,1024]{2,1,0:T(8,128)(2,1)S(1)}, bf16[4,512,1024]{2,1,0:T(8,128)(2,1)S(1)}) custom-call(s32[32]{0:T(128)S(1)} %plan.1.table, s32[4,32]{1,0:T(4,128)S(1)} %copy-done.1, bf16[4,32,256,128]{3,2,1,0:T(8,128)(2,1)S(1)} %bitcast.8, ...), custom_call_target="tpu_custom_call" | custom-call | flops 2147483648 | bytes 1048576 | tf_op jit(solution)/shard_map/pallas_call | solution.py:310
  91.6 0.8 shard_map.88
  92.4 0.1 collective-permute-start.20
  92.6 0.8 collective-permute-start.17
  93.4 1.3 %shard_map.94.refs_2_.refs_3_ = f32[4,256,512]{2,1,0:T(8,128)S(1)} custom-call(bf16[4,512,1024]{2,1,0:T(8,128)(2,1)S(1)} %get-tuple-element.48.weights, bf16[4,512,128]{2,1,0:T(8,128)(2,1)S(1)} %pad_maximum_fusion.refs_0_, bf16[4,256,128]{2,1,0:T(8,128)(2,1)S(1)} %collective-permute-done.23.refs_1_, f32[8,128]{1,0:T(8,128)S(1)} %get-tuple-element.49.refs_2_), custom_call_target="tpu_custom_call" | custom-call | flops 1073741824 | bytes 1048576 | tf_op jit(solution)/shard_map/pallas_call | solution.py:354
  94.7 1.3 %shard_map.95.refs_4_.refs_5_ = f32[4,256,512]{2,1,0:T(8,128)S(1)} custom-call(bf16[4,512,1024]{2,1,0:T(8,128)(2,1)S(1)} %get-tuple-element.47.weights, bf16[4,512,128]{2,1,0:T(8,128)(2,1)S(1)} %collective-permute-done.21.refs_0_, bf16[4,256,128]{2,1,0:T(8,128)(2,1)S(1)} %collective-permute-done.22.refs_1_, f32[4,256,512]{2,1,0:T(8,128)S(1)} %shard_map.94.refs_2_.refs_3_, ...), custom_call_target="tpu_custom_call" | custom-call | flops 1073741824 | bytes 1048576 | tf_op jit(solution)/shard_map/pallas_call | solution.py:354
  96.0 1.3 %shard_map.96.before = f32[4,256,512]{2,1,0:T(8,128)S(1)} custom-call(bf16[4,512,1024]{2,1,0:T(8,128)(2,1)S(1)} %get-tuple-element.46.weights, bf16[1,512,128]{2,1,0:T(8,128)(2,1)S(1)} %bitcast.12, bf16[3,512,128]{2,1,0:T(8,128)(2,1)S(1)} %collective-permute-done.16.refs_1_, bf16[1,512,128]{2,1,0:T(8,128)(2,1)S(1)} %bitcast.10, ...), custom_call_target="tpu_custom_call" | custom-call | flops 1073741824 | bytes 1048576 | tf_op jit(solution)/shard_map/pallas_call | solution.py:354
  97.4 2.1 %leave.1 = f32[4,256,512]{2,1,0:T(8,128)} custom-call(bf16[4,512,1024]{2,1,0:T(8,128)(2,1)S(1)} %get-tuple-element.42.weights, bf16[4,256,128]{2,1,0:T(8,128)(2,1)S(1)} %collective-permute-done.17.one, bf16[4,256,128]{2,1,0:T(8,128)(2,1)S(1)} %collective-permute-done.20.two, f32[4,256,512]{2,1,0:T(8,128)S(1)} %shard_map.96.before), custom_call_target="tpu_custom_call" | custom-call | flops 536870912 | bytes 1048576 | tf_op jit(solution)/shard_map/leave/pallas_call | solution.py:370
  (39 shorter events, 0.3 us)
Async XLA Ops:
  0.6 0.7 copy-start.4
  0.6 1.6 %copy-start.2 = (f32[4,2,128,512]{3,2,1,0:T(8,128)S(1)}, f32[4,2,128,512]{3,2,1,0:T(8,128)}, u32[]{:S(2)}) copy-start(f32[4,2,128,512]{3,2,1,0:T(8,128)} %updates.1) | copy-start | bytes 6291460
  0.6 1.6 %copy-start.3 = (s32[4]{0:T(128)S(1)}, s32[4]{0:T(128)}, u32[]{:S(2)}) copy-start(s32[4]{0:T(128)} %ids.1) | copy-start | bytes 52
  0.7 5.5 %slice-start = ((s8[8388608]{0:T(1024)(128)(4,1)}), s8[4194304]{0:T(1024)(128)(4,1)S(1)}, s32[]{:S(2)}) async-start(s8[8388608]{0:T(1024)(128)(4,1)} %bitcast.7), calls=%async_computation | async-start | bytes 8388608
  2.2 4.0 %slice-start.1 = ((s8[8388608]{0:T(1024)(128)(4,1)}), s8[4194304]{0:T(1024)(128)(4,1)S(1)}, s32[]{:S(2)}) async-start(s8[8388608]{0:T(1024)(128)(4,1)} %bitcast.7), calls=%async_computation.1 | async-start | bytes 8388608
  2.2 4.0 %copy-start.1 = (s32[4,32]{1,0:T(4,128)S(1)}, s32[4,32]{1,0:T(4,128)}, u32[]{:S(2)}) copy-start(s32[4,32]{1,0:T(4,128)} %starts.11) | copy-start | bytes 1540
  2.9 5.6 %collective-permute-start = (bf16[4,256,512]{2,1,0:T(8,128)(2,1)S(1)}, bf16[4,256,512]{2,1,0:T(8,128)(2,1)S(1)}, u32[]{:S(2)}, u32[]{:S(2)}) collective-permute-start(bf16[4,256,512]{2,1,0:T(8,128)(2,1)S(1)} %shard_map.77.scaled), channel_id=1, source_target_pairs={{0,1},{1,0},{2,3},{3,2},{4,5},{5,4},{6,7},{7,6},{8,9},{9,8},{10,11... | collective-permute-start | bytes 3145736 | tf_op jit(solution)/shard_map/ppermute | solution.py:42
  12.9 5.2 %copy-start = (f32[128,2,128]{2,1,0:T(2,128)S(1)}, f32[128,2,128]{2,1,0:T(2,128)}, u32[]{:S(2)}) copy-start(f32[128,2,128]{2,1,0:T(2,128)} %volume.1) | copy-start | bytes 393220
  12.9 13.4 %collective-permute-start.6 = (bf16[4,512,128]{2,1,0:T(8,128)(2,1)S(1)}, bf16[4,512,128]{2,1,0:T(8,128)(2,1)S(1)}, u32[]{:S(2)}, u32[]{:S(2)}) collective-permute-start(bf16[4,512,128]{2,1,0:T(8,128)(2,1)S(1)} %shard_map.81.after), channel_id=1, source_target_pairs={{0,192},{1,25},{2,194},{3,27},{4,196},{5,29},{6,198},{7,31},{8,200... | collective-permute-start | bytes 1572872 | tf_op jit(solution)/shard_map/ppermute | solution.py:34
  14.6 15.2 %collective-permute-start.5 = (bf16[4,512,128]{2,1,0:T(8,128)(2,1)S(1)}, bf16[4,512,128]{2,1,0:T(8,128)(2,1)S(1)}, u32[]{:S(2)}, u32[]{:S(2)}) collective-permute-start(bf16[4,512,128]{2,1,0:T(8,128)(2,1)S(1)} %shard_map.80.after), channel_id=1, source_target_pairs={{0,64},{1,9},{2,66},{3,11},{4,68},{5,13},{6,70},{7,15},{8,72},{9,1... | collective-permute-start | bytes 1572872 | tf_op jit(solution)/shard_map/ppermute | solution.py:34
  14.6 15.2 %collective-permute-start.4 = (bf16[4,512,128]{2,1,0:T(8,128)(2,1)S(1)}, bf16[4,512,128]{2,1,0:T(8,128)(2,1)S(1)}, u32[]{:S(2)}, u32[]{:S(2)}) collective-permute-start(bf16[4,512,128]{2,1,0:T(8,128)(2,1)S(1)} %shard_map.79.after), channel_id=1, source_target_pairs={{0,128},{1,17},{2,130},{3,19},{4,132},{5,21},{6,134},{7,23},{8,136... | collective-permute-start | bytes 1572872 | tf_op jit(solution)/shard_map/ppermute | solution.py:34
  18.3 5.2 %collective-permute-start.1 = (f32[2,128]{1,0:T(2,128)S(1)}, f32[2,128]{1,0:T(2,128)S(1)}, u32[]{:S(2)}, u32[]{:S(2)}) collective-permute-start(f32[2,128]{1,0:T(2,128)S(1)} %get-tuple-element.29), channel_id=1, source_target_pairs={{0,1},{1,0},{2,3},{3,2},{4,5},{5,4},{6,7},{7,6},{8,9},{9,8},{10,11... | collective-permute-start | bytes 3080 | tf_op jit(solution)/shard_map/ppermute | solution.py:42
  20.1 5.2 %collective-permute-start.2 = (f32[2,128]{1,0:T(2,128)S(1)}, f32[2,128]{1,0:T(2,128)S(1)}, u32[]{:S(2)}, u32[]{:S(2)}) collective-permute-start(f32[2,128]{1,0:T(2,128)S(1)} %get-tuple-element.30), channel_id=1, source_target_pairs={{1,2},{2,1},{3,4},{4,3},{5,6},{6,5},{9,10},{10,9},{11,12},{12,11},... | collective-permute-start | bytes 3080 | tf_op jit(solution)/shard_map/ppermute | solution.py:401
  25.3 10.1 %collective-permute-start.3 = (f32[256,128]{1,0:T(8,128)S(1)}, f32[256,128]{1,0:T(8,128)S(1)}, u32[]{:S(2)}, u32[]{:S(2)}) collective-permute-start(f32[256,128]{1,0:T(8,128)S(1)} %shard_map.84.smooth), channel_id=1, source_target_pairs={{0,1},{1,0},{2,3},{3,2},{4,5},{5,4},{6,7},{7,6},{8,9},{9,8},{10,11... | collective-permute-start | bytes 393224 | tf_op jit(solution)/shard_map/ppermute | solution.py:42
  30.0 5.4 %collective-permute-start.7 = (bf16[512,128]{1,0:T(8,128)(2,1)S(1)}, bf16[512,128]{1,0:T(8,128)(2,1)S(1)}, u32[]{:S(2)}, u32[]{:S(2)}) collective-permute-start(bf16[512,128]{1,0:T(8,128)(2,1)S(1)} %get-tuple-element.32), channel_id=1, source_target_pairs={{0,16},{1,129},{2,18},{3,131},{4,20},{5,133},{6,22},{7,135},{8,24}... | collective-permute-start | bytes 393224 | tf_op jit(solution)/shard_map/ppermute | solution.py:34
  32.7 5.3 %collective-permute-start.8 = (bf16[512,128]{1,0:T(8,128)(2,1)S(1)}, bf16[512,128]{1,0:T(8,128)(2,1)S(1)}, u32[]{:S(2)}, u32[]{:S(2)}) collective-permute-start(bf16[512,128]{1,0:T(8,128)(2,1)S(1)} %get-tuple-element.33), channel_id=1, source_target_pairs={{0,8},{1,65},{2,10},{3,67},{4,12},{5,69},{6,14},{7,71},{8,16},{9,7... | collective-permute-start | bytes 393224 | tf_op jit(solution)/shard_map/ppermute | solution.py:34
  33.1 4.9 %collective-permute-start.9 = (bf16[512,128]{1,0:T(8,128)(2,1)S(1)}, bf16[512,128]{1,0:T(8,128)(2,1)S(1)}, u32[]{:S(2)}, u32[]{:S(2)}) collective-permute-start(bf16[512,128]{1,0:T(8,128)(2,1)S(1)} %get-tuple-element.34), channel_id=1, source_target_pairs={{0,24},{1,193},{2,26},{3,195},{4,28},{5,197},{6,30},{7,199},{8,0},... | collective-permute-start | bytes 393224 | tf_op jit(solution)/shard_map/ppermute | solution.py:34
  38.1 9.4 %collective-permute-start.10 = (bf16[512,128]{1,0:T(8,128)(2,1)S(1)}, bf16[512,128]{1,0:T(8,128)(2,1)S(1)}, u32[]{:S(2)}, u32[]{:S(2)}) collective-permute-start(bf16[512,128]{1,0:T(8,128)(2,1)S(1)} %get-tuple-element.36.after), channel_id=1, source_target_pairs={{0,32},{8,40},{16,48},{24,56},{32,0},{40,8},{48,16},{56,24},{64,96... | collective-permute-start | bytes 393224 | tf_op jit(solution)/shard_map/ppermute | solution.py:38
  47.6 7.2 %collective-permute-start.11 = (bf16[512,128]{1,0:T(8,128)(2,1)S(1)}, bf16[512,128]{1,0:T(8,128)(2,1)S(1)}, u32[]{:S(2)}, u32[]{:S(2)}) collective-permute-start(bf16[512,128]{1,0:T(8,128)(2,1)S(1)} %get-tuple-element.39), channel_id=1, source_target_pairs={{0,24},{1,193},{2,26},{3,195},{4,28},{5,197},{6,30},{7,199},{8,0},... | collective-permute-start | bytes 393224 | tf_op jit(solution)/shard_map/ppermute | solution.py:34
  51.5 5.4 %collective-permute-start.12 = (bf16[512,128]{1,0:T(8,128)(2,1)S(1)}, bf16[512,128]{1,0:T(8,128)(2,1)S(1)}, u32[]{:S(2)}, u32[]{:S(2)}) collective-permute-start(bf16[512,128]{1,0:T(8,128)(2,1)S(1)} %get-tuple-element.39), channel_id=1, source_target_pairs={{0,16},{1,129},{2,18},{3,131},{4,20},{5,133},{6,22},{7,135},{8,24}... | collective-permute-start | bytes 393224 | tf_op jit(solution)/shard_map/ppermute | solution.py:34
  51.5 6.4 %collective-permute-start.13 = (bf16[512,128]{1,0:T(8,128)(2,1)S(1)}, bf16[512,128]{1,0:T(8,128)(2,1)S(1)}, u32[]{:S(2)}, u32[]{:S(2)}) collective-permute-start(bf16[512,128]{1,0:T(8,128)(2,1)S(1)} %get-tuple-element.39), channel_id=1, source_target_pairs={{0,8},{1,65},{2,10},{3,67},{4,12},{5,69},{6,14},{7,71},{8,16},{9,7... | collective-permute-start | bytes 393224 | tf_op jit(solution)/shard_map/ppermute | solution.py:34
  58.0 15.2 %collective-permute-start.21 = (bf16[4,512,128]{2,1,0:T(8,128)(2,1)S(1)}, bf16[4,512,128]{2,1,0:T(8,128)(2,1)S(1)}, u32[]{:S(2)}, u32[]{:S(2)}) collective-permute-start(bf16[4,512,128]{2,1,0:T(8,128)(2,1)S(1)} %pad_maximum_fusion.refs_0_), channel_id=1, source_target_pairs={{0,128},{1,17},{2,130},{3,19},{4,132},{5,21},{6,134},{7,23},{8,136... | collective-permute-start | bytes 1572872 | tf_op jit(solution)/shard_map/ppermute | solution.py:34
  58.1 34.3 %collective-permute-start.19 = (bf16[3,512,128]{2,1,0:T(8,128)(2,1)S(1)}, bf16[3,512,128]{2,1,0:T(8,128)(2,1)S(1)}, u32[]{:S(2)}, u32[]{:S(2)}) collective-permute-start(bf16[3,512,128]{2,1,0:T(8,128)(2,1)S(1)} %pad_maximum_fusion.1), channel_id=1, source_target_pairs={{0,64},{1,9},{2,66},{3,11},{4,68},{5,13},{6,70},{7,15},{8,72},{9,1... | collective-permute-start | bytes 1179656 | tf_op jit(solution)/shard_map/ppermute | solution.py:34
  58.2 34.3 %collective-permute-start.16 = (bf16[3,512,128]{2,1,0:T(8,128)(2,1)S(1)}, bf16[3,512,128]{2,1,0:T(8,128)(2,1)S(1)}, u32[]{:S(2)}, u32[]{:S(2)}) collective-permute-start(bf16[3,512,128]{2,1,0:T(8,128)(2,1)S(1)} %pad_maximum_fusion.1), channel_id=1, source_target_pairs={{0,192},{1,25},{2,194},{3,27},{4,196},{5,29},{6,198},{7,31},{8,200... | collective-permute-start | bytes 1179656 | tf_op jit(solution)/shard_map/ppermute | solution.py:34
  60.9 19.5 %collective-permute-start.18 = (bf16[512,128]{1,0:T(8,128)(2,1)S(1)}, bf16[512,128]{1,0:T(8,128)(2,1)S(1)}, u32[]{:S(2)}, u32[]{:S(2)}) collective-permute-start(bf16[512,128]{1,0:T(8,128)(2,1)S(1)} %get-tuple-element.39), channel_id=1, source_target_pairs={{0,64},{1,9},{2,66},{3,11},{4,68},{5,13},{6,70},{7,15},{8,72},{9,1... | collective-permute-start | bytes 393224 | tf_op jit(solution)/shard_map/ppermute | solution.py:34
  60.9 19.6 %collective-permute-start.14 = (f32[256,128]{1,0:T(8,128)S(1)}, f32[256,128]{1,0:T(8,128)S(1)}, u32[]{:S(2)}, u32[]{:S(2)}) collective-permute-start(f32[256,128]{1,0:T(8,128)S(1)} %get-tuple-element.40), channel_id=1, source_target_pairs={{0,1},{1,0},{2,3},{3,2},{4,5},{5,4},{6,7},{7,6},{8,9},{9,8},{10,11... | collective-permute-start | bytes 393224 | tf_op jit(solution)/shard_map/ppermute | solution.py:42
  73.2 20.2 %collective-permute-start.23 = (bf16[4,256,128]{2,1,0:T(8,128)(2,1)S(1)}, bf16[4,256,128]{2,1,0:T(8,128)(2,1)S(1)}, u32[]{:S(2)}, u32[]{:S(2)}) collective-permute-start(bf16[4,256,128]{2,1,0:T(8,128)(2,1)S(1)} %shard_map.93), channel_id=1, source_target_pairs={{0,1},{1,0},{2,3},{3,2},{4,5},{5,4},{6,7},{7,6},{8,9},{9,8},{10,11... | collective-permute-start | bytes 786440 | tf_op jit(solution)/shard_map/ppermute | solution.py:42
  80.4 12.2 %collective-permute-start.15 = (bf16[512,128]{1,0:T(8,128)(2,1)S(1)}, bf16[512,128]{1,0:T(8,128)(2,1)S(1)}, u32[]{:S(2)}, u32[]{:S(2)}) collective-permute-start(bf16[512,128]{1,0:T(8,128)(2,1)S(1)} %get-tuple-element.39), channel_id=1, source_target_pairs={{0,192},{1,25},{2,194},{3,27},{4,196},{5,29},{6,198},{7,31},{8,200... | collective-permute-start | bytes 393224 | tf_op jit(solution)/shard_map/ppermute | solution.py:34
  80.5 14.2 %collective-permute-start.22 = (bf16[4,256,128]{2,1,0:T(8,128)(2,1)S(1)}, bf16[4,256,128]{2,1,0:T(8,128)(2,1)S(1)}, u32[]{:S(2)}, u32[]{:S(2)}) collective-permute-start(bf16[4,256,128]{2,1,0:T(8,128)(2,1)S(1)} %shard_map.92), channel_id=1, source_target_pairs={{0,1},{1,0},{2,3},{3,2},{4,5},{5,4},{6,7},{7,6},{8,9},{9,8},{10,11... | collective-permute-start | bytes 786440 | tf_op jit(solution)/shard_map/ppermute | solution.py:42
  92.4 4.9 %collective-permute-start.20 = (bf16[4,256,128]{2,1,0:T(8,128)(2,1)S(1)}, bf16[4,256,128]{2,1,0:T(8,128)(2,1)S(1)}, u32[]{:S(2)}, u32[]{:S(2)}) collective-permute-start(bf16[4,256,128]{2,1,0:T(8,128)(2,1)S(1)} %shard_map.91), channel_id=1, source_target_pairs={{0,1},{1,0},{2,3},{3,2},{4,5},{5,4},{6,7},{7,6},{8,9},{9,8},{10,11... | collective-permute-start | bytes 786440 | tf_op jit(solution)/shard_map/ppermute | solution.py:42
  92.6 4.8 %collective-permute-start.17 = (bf16[4,256,128]{2,1,0:T(8,128)(2,1)S(1)}, bf16[4,256,128]{2,1,0:T(8,128)(2,1)S(1)}, u32[]{:S(2)}, u32[]{:S(2)}) collective-permute-start(bf16[4,256,128]{2,1,0:T(8,128)(2,1)S(1)} %shard_map.90), channel_id=1, source_target_pairs={{0,1},{1,0},{2,3},{3,2},{4,5},{5,4},{6,7},{7,6},{8,9},{9,8},{10,11... | collective-permute-start | bytes 786440 | tf_op jit(solution)/shard_map/ppermute | solution.py:42
